TPU v7x, 32 devices: a whole 2x2x4 slice. The times are simulated.
32 devices in a mesh: seq: 4 (over z), fsdp: 8 (over y, x, core).
Axes of the slice: x: 2, y: 2, z: 4, core: 2. Of those that a mesh axis runs over, the one named last changes fastest.
Arguments:
- tokens: bfloat16 [8, 1024, 1152], P('fsdp', 'seq'), may hold values from -6 to 6
- pre_attn_gain: float32 [1152], replicated, may hold values from 0.1 to 1.9
- qkv_weight: bfloat16 [1152, 4096], P('fsdp'), may hold values from -0.1875 to 0.1875
- out_weight: bfloat16 [2048, 1152], P('fsdp'), may hold values from -0.125 to 0.125
- post_attn_gain: float32 [1152], replicated, may hold values from 0.1 to 1.9
- pre_ffn_gain: float32 [1152], replicated, may hold values from 0.1 to 1.9
- gate_up_weight: bfloat16 [1152, 13824], P('fsdp'), may hold values from -0.1875 to 0.1875
- down_weight: bfloat16 [6912, 1152], P('fsdp'), may hold values from -0.078125 to 0.078125
- post_ffn_gain: float32 [1152], replicated, may hold values from 0.1 to 1.9
- out_grad: bfloat16 [8, 1024, 1152], P('fsdp', 'seq'), may hold values from -6 to 6
Outputs:
- layer_out: bfloat16 [8, 1024, 1152], P('fsdp', 'seq')
- tokens_grad: float32 [8, 1024, 1152], P('fsdp', 'seq')
- pre_attn_gain_grad: float32 [1152], replicated
- qkv_weight_grad: float32 [1152, 4096], P('fsdp')
- out_weight_grad: float32 [2048, 1152], P('fsdp')
- post_attn_gain_grad: float32 [1152], replicated
- pre_ffn_gain_grad: float32 [1152], replicated
- gate_up_weight_grad: float32 [1152, 13824], P('fsdp')
- down_weight_grad: float32 [6912, 1152], P('fsdp')
- post_ffn_gain_grad: float32 [1152], replicated
All inputs are finite; a program needn't handle non-finite values.
Results may differ from a plain program's by a relative error of at most 0.02.
Values may be sent and summed in bfloat16 or wider, within the bound.
A program may use at most 320 MiB of HBM per device.

v0:
```python
import math

import jax
import jax.numpy as jnp
from jax import lax
from jax.sharding import PartitionSpec as P

H = 8
KV = 4
HD = 256
FF = 6912


EPSILON = 1e-06
SOFT_CAP = 50.0
QUERY_FACTOR = 0.0625
GELU_COEFF = math.sqrt(2.0 / math.pi)
CUBIC = 0.044715
MASKED = -1e30


def inverse_rms(values):
    return lax.rsqrt(jnp.mean(values * values, axis=-1, keepdims=True) + EPSILON)


def norm_back(upstream, values, inv_scale, gains):
    weighted = upstream * gains
    inner_mean = jnp.mean(weighted * values, axis=-1, keepdims=True)
    gradient = inv_scale * weighted - values * (inv_scale * inv_scale * inv_scale) * inner_mean
    gain_grad = jnp.sum(upstream * values * inv_scale, axis=0)
    return (gradient, gain_grad)


def gelu_pair(values):
    inner_part = GELU_COEFF * (values + CUBIC * values * values * values)
    tanh_part = jnp.tanh(inner_part)
    activated = 0.5 * values * (1.0 + tanh_part)
    derivative = 0.5 * (1.0 + tanh_part) + 0.5 * values * (
        1.0 - tanh_part * tanh_part
    ) * GELU_COEFF * (1.0 + 3.0 * CUBIC * values * values)
    return (activated, derivative)


def batched_contraction(pattern, left_side, right_side):
    return jnp.einsum(pattern, left_side, right_side, preferred_element_type=jnp.float32)


def capped_scores(block_of_queries, key_row_slices, offset):
    amount = block_of_queries.shape[0]
    key_count = key_row_slices.shape[0]
    unscaled_logits = (
        batched_contraction("olv,ilv->loi", block_of_queries, key_row_slices) * QUERY_FACTOR
    )
    tanh_part = jnp.tanh(unscaled_logits / SOFT_CAP)
    allowed = (
        jnp.arange(key_count, dtype=jnp.int32)[None, :]
        <= (offset + jnp.arange(amount, dtype=jnp.int32))[:, None]
    )
    capped = jnp.where(allowed[None], SOFT_CAP * tanh_part, MASKED)
    return (tanh_part, capped)


def attend(queries, key_row_slices, value_row_slices):
    length = queries.shape[0]
    block_size = min(512, length)
    blocks = length // block_size

    def one_block(block_id):
        offset = block_id * block_size
        block_of_queries = lax.dynamic_slice_in_dim(queries, offset, block_size, 0)
        tanh_part, capped = capped_scores(block_of_queries, key_row_slices, offset)
        biggest = jnp.max(capped, axis=-1, keepdims=True)
        logsum = biggest + jnp.log(jnp.sum(jnp.exp(capped - biggest), axis=-1, keepdims=True))
        attention_probabilities = jnp.exp(capped - logsum).astype(jnp.bfloat16)
        layer_result = batched_contraction(
            "vxn,nvs->xvs", attention_probabilities, value_row_slices
        ).astype(jnp.bfloat16)
        return (layer_result, logsum[..., 0])

    outputs, logsums = lax.map(one_block, jnp.arange(blocks, dtype=jnp.int32))
    return (outputs.reshape(queries.shape), logsums)


def attend_back(queries, key_row_slices, value_row_slices, outputs, out_delta, logsums):
    length = queries.shape[0]
    block_size = min(512, length)
    blocks = length // block_size
    row_dots = batched_contraction("qbd,qbd->bq", out_delta, outputs)

    def one_block(carried, inputs):
        key_accumulator, value_accumulator = carried
        block_id, block_logsum = inputs
        offset = block_id * block_size
        block_of_queries = lax.dynamic_slice_in_dim(queries, offset, block_size, 0)
        block_correction = lax.dynamic_slice_in_dim(out_delta, offset, block_size, 0)
        tanh_part, capped = capped_scores(block_of_queries, key_row_slices, offset)
        attention_probabilities = jnp.exp(capped - block_logsum[..., None])
        probability_gradients = batched_contraction(
            "olv,ilv->loi", block_correction, value_row_slices
        )
        dots_block = lax.dynamic_slice_in_dim(row_dots, offset, block_size, 1)
        logit_gradients = (
            attention_probabilities
            * (probability_gradients - dots_block[..., None])
            * (1.0 - tanh_part * tanh_part)
            * QUERY_FACTOR
        ).astype(jnp.bfloat16)
        rounded_values = attention_probabilities.astype(jnp.bfloat16)
        value_accumulator = value_accumulator + batched_contraction(
            "pfm,fpg->mpg", rounded_values, block_correction
        )
        key_accumulator = key_accumulator + batched_contraction(
            "pfm,fpg->mpg", logit_gradients, block_of_queries
        )
        query_gradient = batched_contraction(
            "vxn,nvs->xvs", logit_gradients, key_row_slices
        ).astype(jnp.bfloat16)
        return ((key_accumulator, value_accumulator), query_gradient)

    zero_acc = jnp.zeros(key_row_slices.shape, jnp.float32)
    (key_accumulator, value_accumulator), query_grads = lax.scan(
        one_block, (zero_acc, zero_acc), (jnp.arange(blocks, dtype=jnp.int32), logsums)
    )
    return (
        query_grads.reshape(queries.shape),
        key_accumulator.astype(jnp.bfloat16),
        value_accumulator.astype(jnp.bfloat16),
    )


def project(activations, weight_shard):
    return jnp.dot(
        activations,
        lax.all_gather(weight_shard, "fsdp", axis=0, tiled=True),
        preferred_element_type=jnp.float32,
    )


def project_back(gradient, weight_shard):
    return lax.dot_general(
        gradient,
        lax.all_gather(weight_shard, "fsdp", axis=0, tiled=True),
        (((1,), (1,)), ((), ())),
        preferred_element_type=jnp.float32,
    )


def term_maker(activations, gradient):
    return lax.dot_general(
        activations, gradient, (((0,), (0,)), ((), ())), preferred_element_type=jnp.float32
    )


def weight_term(activations, gradient):
    sliced = lax.psum_scatter(
        term_maker(activations, gradient).astype(jnp.bfloat16),
        "fsdp",
        scatter_dimension=0,
        tiled=True,
    )
    return lax.psum(sliced, "seq").astype(jnp.float32)


def on_device(
    tokens,
    pre_attn_gain,
    qkv_weight,
    out_weight,
    post_attn_gain,
    pre_ffn_gain,
    gate_up_weight,
    down_weight,
    post_ffn_gain,
    out_grad,
):
    groups, local_len, width = tokens.shape
    row_count = groups * local_len
    head_repeat = H // KV
    residual_in = tokens.reshape(row_count, width).astype(jnp.float32)
    scale_one = inverse_rms(residual_in)
    normed_in = (residual_in * scale_one * pre_attn_gain).astype(jnp.bfloat16)
    projected = project(normed_in, qkv_weight).astype(jnp.bfloat16)
    queries = projected[:, : H * HD].reshape(groups, local_len, H, HD)
    key_row_slices = jnp.repeat(
        projected[:, H * HD : (H + KV) * HD].reshape(groups, local_len, KV, HD), head_repeat, axis=2
    )
    value_row_slices = jnp.repeat(
        projected[:, (H + KV) * HD :].reshape(groups, local_len, KV, HD), head_repeat, axis=2
    )
    head_queries, head_keys, head_values = (
        lax.all_to_all(queries, "seq", split_axis=2, concat_axis=1, tiled=True),
        lax.all_to_all(key_row_slices, "seq", split_axis=2, concat_axis=1, tiled=True),
        lax.all_to_all(value_row_slices, "seq", split_axis=2, concat_axis=1, tiled=True),
    )
    head_out, logsums = jax.vmap(attend)(head_queries, head_keys, head_values)
    attn_out = lax.all_to_all(head_out, "seq", split_axis=1, concat_axis=2, tiled=True).reshape(
        row_count, H * HD
    )
    branch_one = project(attn_out, out_weight)
    scale_two = inverse_rms(branch_one)
    hidden = residual_in + branch_one * scale_two * post_attn_gain
    scale_three = inverse_rms(hidden)
    normed_mid = (hidden * scale_three * pre_ffn_gain).astype(jnp.bfloat16)
    gate_up = project(normed_mid, gate_up_weight)
    gate_part = gate_up[:, :FF]
    up_part = gate_up[:, FF:]
    activated, derivative = gelu_pair(gate_part)
    mixed = (activated * up_part).astype(jnp.bfloat16)
    branch_two = project(mixed, down_weight)
    scale_four = inverse_rms(branch_two)
    layer_out = (
        (hidden + branch_two * scale_four * post_ffn_gain)
        .astype(jnp.bfloat16)
        .reshape(groups, local_len, width)
    )
    upstream = out_grad.reshape(row_count, width).astype(jnp.float32)
    branch_two_grad, post_ffn_term = norm_back(upstream, branch_two, scale_four, post_ffn_gain)
    branch_two_grad = branch_two_grad.astype(jnp.bfloat16)
    down_wgrad = weight_term(mixed, branch_two_grad)
    mixed_grad = project_back(branch_two_grad, down_weight)
    gate_up_grad = jnp.concatenate(
        [mixed_grad * up_part * derivative, mixed_grad * activated], axis=1
    ).astype(jnp.bfloat16)
    gate_up_wgrad = weight_term(normed_mid, gate_up_grad)
    normed_mid_grad = project_back(gate_up_grad, gate_up_weight)
    hidden_part, pre_ffn_term = norm_back(normed_mid_grad, hidden, scale_three, pre_ffn_gain)
    hidden_grad = upstream + hidden_part
    branch_one_grad, post_attn_term = norm_back(hidden_grad, branch_one, scale_two, post_attn_gain)
    branch_one_grad = branch_one_grad.astype(jnp.bfloat16)
    out_wgrad = weight_term(attn_out, branch_one_grad)
    attn_grad = (
        project_back(branch_one_grad, out_weight)
        .astype(jnp.bfloat16)
        .reshape(groups, local_len, H, HD)
    )
    head_delta = lax.all_to_all(attn_grad, "seq", split_axis=2, concat_axis=1, tiled=True)
    query_gradient, key_grad, value_grad = jax.vmap(attend_back)(
        head_queries, head_keys, head_values, head_out, head_delta, logsums
    )
    query_tok, key_tok, value_tok = (
        lax.all_to_all(query_gradient, "seq", split_axis=1, concat_axis=2, tiled=True),
        lax.all_to_all(key_grad, "seq", split_axis=1, concat_axis=2, tiled=True),
        lax.all_to_all(value_grad, "seq", split_axis=1, concat_axis=2, tiled=True),
    )
    key_sum = (
        key_tok.astype(jnp.float32)
        .reshape(groups, local_len, KV, head_repeat, HD)
        .sum(axis=3)
        .astype(jnp.bfloat16)
    )
    value_sum = (
        value_tok.astype(jnp.float32)
        .reshape(groups, local_len, KV, head_repeat, HD)
        .sum(axis=3)
        .astype(jnp.bfloat16)
    )
    qkv_grad = jnp.concatenate(
        [
            query_tok.reshape(row_count, H * HD),
            key_sum.reshape(row_count, KV * HD),
            value_sum.reshape(row_count, KV * HD),
        ],
        axis=1,
    )
    qkv_wgrad = weight_term(normed_in, qkv_grad)
    normed_in_grad = project_back(qkv_grad, qkv_weight)
    input_part, pre_attn_term = norm_back(normed_in_grad, residual_in, scale_one, pre_attn_gain)
    tokens_grad = (hidden_grad + input_part).reshape(groups, local_len, width)
    gain_sums = lax.psum(
        (pre_attn_term, post_attn_term, pre_ffn_term, post_ffn_term), ("seq", "fsdp")
    )
    return (
        layer_out,
        tokens_grad,
        gain_sums[0],
        qkv_wgrad,
        out_wgrad,
        gain_sums[1],
        gain_sums[2],
        gate_up_wgrad,
        down_wgrad,
        gain_sums[3],
    )


def solution(mesh):
    in_specs = (
        P("fsdp", "seq", None),
        P(),
        P("fsdp", None),
        P("fsdp", None),
        P(),
        P(),
        P("fsdp", None),
        P("fsdp", None),
        P(),
        P("fsdp", "seq", None),
    )
    out_specs = (
        P("fsdp", "seq", None),
        P("fsdp", "seq", None),
        P(),
        P("fsdp", None),
        P("fsdp", None),
        P(),
        P(),
        P("fsdp", None),
        P("fsdp", None),
        P(),
    )
    return jax.shard_map(
        on_device, mesh=mesh, in_specs=in_specs, out_specs=out_specs, check_vma=False
    )
```

profile of v0, /device:TPU:0, one launch (start us, length us, event | category | flops | bytes accessed | tf_op | source)
XLA Modules:
  0.0 1268.4 jit_solution(4734523101513509988)
XLA Ops:
  10.8 60.5 %all-gather.5.cloned.1.call-done = bf16[1152,4096]{1,0:T(8,128)(2,1)} async-done(((bf16[144,4096]{1,0:T(8,128)(2,1)}), bf16[1152,4096]{1,0:T(8,128)(2,1)}) %all-gather.5.cloned.1.call-update) | async-done | bytes 9437200 | tf_op jit(solution)/shard_map/all_gather | solution.py:134
  71.3 6.9 convolution_convert_fusion.5
  80.8 4.6 all-to-all-start
  87.5 24.0 %all-to-all-done = bf16[1,256,8,256]{3,1,0,2:T(8,128)(2,1)S(1)} async-done(((bf16[1,256,8,256]{3,1,0,2:T(8,128)(2,1)}), bf16[1,256,8,256]{3,1,0,2:T(8,128)(2,1)S(1)}, u32[]{:S(2)}, u32[]{:S(2)}) %all-to-all-start) | async-done | bytes 1048608 | tf_op jit(solution)/shard_map/all_to_all | solution.py:191
  117.2 24.2 %all-to-all-done.1 = bf16[1,256,8,256]{3,1,0,2:T(8,128)(2,1)S(1)} async-done(((bf16[1,256,8,256]{3,1,0,2:T(8,128)(2,1)}), bf16[1,256,8,256]{3,1,0,2:T(8,128)(2,1)S(1)}, u32[]{:S(2)}, u32[]{:S(2)}) %all-to-all-start.1) | async-done | bytes 1048608 | tf_op jit(solution)/shard_map/all_to_all | solution.py:192
  148.1 23.9 %all-to-all-done.2 = bf16[1,256,8,256]{3,1,0,2:T(8,128)(2,1)} async-done(((bf16[1,256,8,256]{3,1,0,2:T(8,128)(2,1)}), bf16[1,256,8,256]{3,1,0,2:T(8,128)(2,1)}, u32[]{:S(2)}, u32[]{:S(2)}) %all-to-all-start.2) | async-done | bytes 1048608 | tf_op jit(solution)/shard_map/all_to_all | solution.py:193
  175.4 14.8 %while.35 = (s32[]{:T(128)}, bf16[2,1,512,2,256]{4,2,0,3,1:T(8,128)(2,1)}, f32[2,1,2,512]{3,2,1,0:T(2,128)S(1)}, s32[2]{0:T(128)S(1)}, bf16[1,1024,2,256]{3,1,2,...) while((s32[]{:T(128)}, ...), condition=%wide.region_4.5_spmd, body=%wide.region_1.4_spmd.sunk | while | flops 1089207808 | bytes 30446368 | solution.py:80
  192.9 27.9 %all_to_all.120 = bf16[1,1024,2,256]{3,2,0,1:T(2,128)(2,1)S(1)} all-to-all(bf16[1,1024,2,256]{3,2,0,1:T(2,128)(2,1)S(1)} %copy.137), channel_id=1, replica_groups=mesh['seq'=4,'fsdp'=8] {'seq'}, dimensions={1} | all-to-all | bytes 2097152 | tf_op jit(solution)/shard_map/all_to_all | solution.py:196
  229.8 37.6 %all-gather.9.cloned.1.call-done = bf16[1152,13824]{1,0:T(8,128)(2,1)} async-done(((bf16[144,13824]{1,0:T(8,128)(2,1)}), bf16[1152,13824]{1,0:T(8,128)(2,1)}) %all-gather.9.cloned.1.call-update) | async-done | bytes 31850512 | tf_op jit(solution)/shard_map/all_gather | solution.py:134
  267.4 18.9 %fusion.80 = f32[256,13824]{1,0:T(8,128)} fusion(bf16[1152,13824]{1,0:T(8,128)(2,1)} %all-gather.9.cloned.1.call-done, f32[256,1152]{1,0:T(8,128)S(1)} %get-tuple-element.380, f32[1152]{0:T(1024)S(1)} %copy-done.36, f32[256]{0:T(256)S(1)} %get-tuple-element.394), kind=kOutput, calls=%fused_computation.142 | convolution fusion | flops 8154611712 | bytes 47191552 | tf_op jit(solution)/shard_map/dot_general | solution.py:132
  286.3 7.5 multiply_convert_fusion.2
  293.8 61.5 %all-gather.11.cloned.1.call-done = bf16[6912,1152]{1,0:T(8,128)(2,1)} async-done(((bf16[864,1152]{1,0:T(8,128)(2,1)}), bf16[6912,1152]{1,0:T(8,128)(2,1)}) %all-gather.11.cloned.1.call-update) | async-done | bytes 15925264 | tf_op jit(solution)/shard_map/all_gather | solution.py:134
  355.3 10.4 multiply_reduce_fusion.4
  368.1 15.9 %fusion.52 = (bf16[256,6912]{1,0:T(8,128)(2,1)}, bf16[256,6912]{1,0:T(8,128)(2,1)}) fusion(f32[256,13824]{1,0:T(8,128)} %fusion.80, bf16[256,1152]{1,0:T(8,128)(2,1)S(1)} %get-tuple-element.387, bf16[6912,1152]{1,0:T(8,128)(2,1)} %all-gather.11.cloned.1.call-done), kind=kOutput, calls=%fused_computation.75 | convolution fusion | flops 4117561344 | bytes 37748736 | tf_op jit(solution)/shard_map/dot_general | solution.py:140
  384.0 19.4 %multiply_reduce_fusion = (f32[1152]{0:T(1024)}, f32[256]{0:T(256)S(1)}, f32[256,1152]{1,0:T(8,128)}) fusion(f32[256,1152]{1,0:T(8,128)S(1)} %get-tuple-element.380, f32[256]{0:T(256)S(1)} %get-tuple-element.394, f32[1152]{0:T(1024)S(1)} %copy-done.36, bf16[1152,13824]{1,0:T(8,128)(2,1)} %all-gather.9.cloned.1.call-done, ...), kind=kOutput, calls=%fused_computation.112 | convolution fusion | flops 8169651200 | bytes 41298944 | tf_op jit(solution)/shard_map/dot_general | solution.py:140
  413.1 4.6 all-to-all-start.4
  417.7 5.1 convolution_convert_fusion.4
  422.8 21.1 %all-to-all-done.4 = bf16[1,256,8,256]{3,1,0,2:T(8,128)(2,1)} async-done(((bf16[1,256,8,256]{3,1,0,2:T(8,128)(2,1)}), bf16[1,256,8,256]{3,1,0,2:T(8,128)(2,1)}, u32[]{:S(2)}, u32[]{:S(2)}) %all-to-all-start.4) | async-done | bytes 1048608 | tf_op jit(solution)/shard_map/all_to_all | solution.py:236
  448.5 38.1 %while.36 = (s32[]{:T(128)}, f32[1,1024,2,256]{1,3,2,0:T(8,128)S(1)}, f32[1,1024,2,256]{1,3,2,0:T(8,128)}, bf16[2,1,512,2,256]{4,2,0,3,1:T(8,128)(2,1)}, s32[2]{...) while((s32[]{:T(128)}, ...), condition=%wide.region_12.13_spmd.clone, body=%wide.region_11.12_spmd.clone.sunk | while | flops 2704015872 | bytes 105941600 | solution.py:121
  479.9 5.1 bitcast_add_fusion.5
  496.4 23.1 %all-to-all-done.7 = bf16[1,1024,2,256]{3,2,0,1:T(2,128)(2,1)S(1)} async-done(((bf16[1,1024,2,256]{3,2,0,1:T(2,128)(2,1)}), bf16[1,1024,2,256]{3,2,0,1:T(2,128)(2,1)S(1)}, u32[]{:S(2)}, u32[]{:S(2)}) %all-to-all-start.7) | async-done | bytes 1048608 | tf_op jit(solution)/shard_map/all_to_all | solution.py:243
  526.4 21.9 %all-to-all-done.6 = bf16[1,1024,2,256]{3,2,0,1:T(2,128)(2,1)S(1)} async-done(((bf16[1,1024,2,256]{3,2,0,1:T(2,128)(2,1)}), bf16[1,1024,2,256]{3,2,0,1:T(2,128)(2,1)S(1)}, u32[]{:S(2)}, u32[]{:S(2)}) %all-to-all-start.6) | async-done | bytes 1048608 | tf_op jit(solution)/shard_map/all_to_all | solution.py:242
  563.3 13.8 %all-to-all-done.5 = bf16[1,1024,2,256]{3,2,0,1:T(2,128)(2,1)S(1)} async-done(((bf16[1,1024,2,256]{3,2,0,1:T(2,128)(2,1)}), bf16[1,1024,2,256]{3,2,0,1:T(2,128)(2,1)S(1)}, u32[]{:S(2)}, u32[]{:S(2)}) %all-to-all-start.5) | async-done | bytes 1048608 | tf_op jit(solution)/shard_map/all_to_all | solution.py:241
  579.7 7.9 convolution_convert_fusion.3
  589.6 12.2 convolution_convert_fusion.2
  603.2 17.6 %convolution_convert_fusion.1 = bf16[1152,13824]{1,0:T(8,128)(2,1)} fusion(bf16[256,6912]{1,0:T(8,128)(2,1)} %get-tuple-element.384, bf16[256,6912]{1,0:T(8,128)(2,1)} %get-tuple-element.383, f32[256,1152]{1,0:T(8,128)S(1)} %copy-done.6, f32[1152]{0:T(1024)S(1)} %copy-done.36, f32[256]{0:T(256)S(1)} %copy-done.40), kind=kOutput, calls=%fused_computation.63 | convolution fusion | flops 8184692736 | bytes 40113664 | tf_op jit(solution)/shard_map/dot_general | solution.py:149
  620.8 41.8 %reduce-scatter.5.cloned.1.call-done = bf16[144,4096]{1,0:T(8,128)(2,1)} async-done(((bf16[1152,4096]{1,0:T(8,128)(2,1)}), bf16[144,4096]{1,0:T(8,128)(2,1)}) %reduce-scatter.5.cloned.1.call-update) | async-done | bytes 1179664 | tf_op jit(solution)/shard_map/reduce_scatter | solution.py:155
  662.6 114.8 %reduce-scatter.11.cloned.1.call-done = bf16[864,1152]{1,0:T(8,128)(2,1)} async-done(((bf16[6912,1152]{1,0:T(8,128)(2,1)}), bf16[864,1152]{1,0:T(8,128)(2,1)}) %reduce-scatter.11.cloned.1.call-update) | async-done | bytes 1990672 | tf_op jit(solution)/shard_map/reduce_scatter | solution.py:155
  777.4 198.7 %reduce-scatter.9.cloned.1.call-done = bf16[144,13824]{1,0:T(8,128)(2,1)} async-done(((bf16[1152,13824]{1,0:T(8,128)(2,1)}), bf16[144,13824]{1,0:T(8,128)(2,1)}) %reduce-scatter.9.cloned.1.call-update) | async-done | bytes 3981328 | tf_op jit(solution)/shard_map/reduce_scatter | solution.py:155
  977.7 7.9 fusion.71
  985.6 45.9 %all-reduce.2 = (f32[1152]{0:T(1024)}, f32[1152]{0:T(1024)}, f32[1152]{0:T(1024)}, f32[1152]{0:T(1024)}) all-reduce(f32[1152]{0:T(1024)S(1)} %get-tuple-element.330, f32[1152]{0:T(1024)S(1)} %copy-done.44, f32[1152]{0:T(1024)S(1)} %copy-done.48, f32[1152]{0:T(1024)S(1)} %copy-done.43), channel_id=1, replica_groups=mesh['seq'=4,'fsdp'=8] {'seq','fsdp'}, use_global_device_ids=true, to_apply=%region_17.18 | all-reduce | flops 4608 | bytes 36864 | tf_op jit(solution)/shard_map/psum | solution.py:269
  1034.1 215.8 %all-reduce.6.cloned.1.call-done = (bf16[144,4096]{1,0:T(8,128)(2,1)}, bf16[256,1152]{1,0:T(8,128)(2,1)}, bf16[144,13824]{1,0:T(8,128)(2,1)}, bf16[864,1152]{1,0:T(8,128)(2,1)}) async-done(((bf16[144,4096]{1,0:T(8,128)(2,1)}, bf16[256,1152]{1,0:T(8,128)(2,1)}, bf16[144,13824]{1,0:T(8,128)(2,1)}, bf16[864,1152]{1,0:T(8,128)(2,1)}), (bf16[144,4096]{1,0:T(8,128)(2,1)}, bf16[256,1152]{1,0:T(8,128)(2,1)}, ...) | async-done | bytes 7741456 | tf_op jit(solution)/shard_map/psum | solution.py:161
  (249 shorter events, 150.0 us)
Async XLA Ops:
  7.2 64.1 %all-gather.5.cloned.1.call-start = ((), (), s32[]{:S(2)}) async-start(), calls=%async_computation.12 | async-start | bytes 10616832 | tf_op jit(solution)/shard_map/all_gather | solution.py:134
  7.9 63.4 %copy-start.37 = (f32[1152]{0:T(1024)S(1)}, f32[1152]{0:T(1024)}, u32[]{:S(2)}) copy-start(f32[1152]{0:T(1024)} %param.15) | copy-start | bytes 13828
  7.9 216.5 %all-gather.7.cloned.1.call-start = ((), (), s32[]{:S(2)}) async-start(), calls=%async_computation.13 | async-start | bytes 5308416 | tf_op jit(solution)/shard_map/all_gather | solution.py:134
  8.7 258.7 %all-gather.9.cloned.1.call-start = ((), (), s32[]{:S(2)}) async-start(), calls=%async_computation.14 | async-start | bytes 35831808 | tf_op jit(solution)/shard_map/all_gather | solution.py:134
  9.4 345.9 %all-gather.11.cloned.1.call-start = ((), (), s32[]{:S(2)}) async-start(), calls=%async_computation.15 | async-start | bytes 17915904 | tf_op jit(solution)/shard_map/all_gather | solution.py:134
  10.8 67.5 %copy-start.45 = (f32[256]{0:T(256)}, f32[256]{0:T(256)S(1)}, u32[]{:S(2)}) copy-start(f32[256]{0:T(256)S(1)} %get-tuple-element.390) | copy-start | bytes 3076
  80.8 30.7 %all-to-all-start = ((bf16[1,256,8,256]{3,1,0,2:T(8,128)(2,1)}), bf16[1,256,8,256]{3,1,0,2:T(8,128)(2,1)S(1)}, u32[]{:S(2)}, u32[]{:S(2)}) async-start(bf16[1,256,8,256]{3,1,0,2:T(8,128)(2,1)} %copy.130), calls=%async_computation | async-start | bytes 2097152 | tf_op jit(solution)/shard_map/all_to_all | solution.py:191
  112.6 28.8 %all-to-all-start.1 = ((bf16[1,256,8,256]{3,1,0,2:T(8,128)(2,1)}), bf16[1,256,8,256]{3,1,0,2:T(8,128)(2,1)S(1)}, u32[]{:S(2)}, u32[]{:S(2)}) async-start(bf16[1,256,8,256]{3,1,0,2:T(8,128)(2,1)} %bitcast.257), calls=%async_computation.1 | async-start | bytes 2097152 | tf_op jit(solution)/shard_map/all_to_all | solution.py:192
  142.5 29.6 %all-to-all-start.2 = ((bf16[1,256,8,256]{3,1,0,2:T(8,128)(2,1)}), bf16[1,256,8,256]{3,1,0,2:T(8,128)(2,1)}, u32[]{:S(2)}, u32[]{:S(2)}) async-start(bf16[1,256,8,256]{3,1,0,2:T(8,128)(2,1)} %bitcast.255), calls=%async_computation.2 | async-start | bytes 2097152 | tf_op jit(solution)/shard_map/all_to_all | solution.py:193
  190.2 34.3 %copy-start.3 = (bf16[1,1024,2,256]{3,1,2,0:T(8,128)(2,1)}, bf16[1,1024,2,256]{3,1,2,0:T(8,128)(2,1)S(1)}, u32[]{:S(2)}) copy-start(bf16[1,1024,2,256]{3,1,2,0:T(8,128)(2,1)S(1)} %get-tuple-element.625) | copy-start | bytes 3145732
  224.4 43.0 %copy-start.36 = (f32[1152]{0:T(1024)S(1)}, f32[1152]{0:T(1024)}, u32[]{:S(2)}) copy-start(f32[1152]{0:T(1024)} %param.19) | copy-start | bytes 13828
  229.8 173.6 %copy-start.5 = (f32[256,1152]{1,0:T(8,128)}, f32[256,1152]{1,0:T(8,128)S(1)}, u32[]{:S(2)}) copy-start(f32[256,1152]{1,0:T(8,128)S(1)} %get-tuple-element.380) | copy-start | bytes 3538948
  229.8 173.6 %copy-start.39 = (f32[256]{0:T(256)}, f32[256]{0:T(256)S(1)}, u32[]{:S(2)}) copy-start(f32[256]{0:T(256)S(1)} %get-tuple-element.394) | copy-start | bytes 3076
  293.8 71.9 %copy-start.19 = (bf16[1,256,1152]{2,1,0:T(8,128)(2,1)S(1)}, bf16[1,256,1152]{2,1,0:T(8,128)(2,1)}, u32[]{:S(2)}) copy-start(bf16[1,256,1152]{2,1,0:T(8,128)(2,1)} %param.23) | copy-start | bytes 1769476
  293.8 71.9 %copy-start.42 = (f32[1152]{0:T(1024)S(1)}, f32[1152]{0:T(1024)}, u32[]{:S(2)}) copy-start(f32[1152]{0:T(1024)} %param.22) | copy-start | bytes 13828
  368.1 15.9 %copy-start.29 = (bf16[256,1152]{1,0:T(8,128)(2,1)}, bf16[256,1152]{1,0:T(8,128)(2,1)S(1)}, u32[]{:S(2)}) copy-start(bf16[256,1152]{1,0:T(8,128)(2,1)S(1)} %get-tuple-element.387) | copy-start | bytes 1769476
  384.0 19.4 %copy-start.14 = (f32[256,1152]{1,0:T(8,128)S(1)}, f32[256,1152]{1,0:T(8,128)}, u32[]{:S(2)}) copy-start(f32[256,1152]{1,0:T(8,128)} %copy-done.13) | copy-start | bytes 3538948
  413.1 30.8 %all-to-all-start.4 = ((bf16[1,256,8,256]{3,1,0,2:T(8,128)(2,1)}), bf16[1,256,8,256]{3,1,0,2:T(8,128)(2,1)}, u32[]{:S(2)}, u32[]{:S(2)}) async-start(bf16[1,256,8,256]{3,1,0,2:T(8,128)(2,1)} %copy.140), calls=%async_computation.4 | async-start | bytes 2097152 | tf_op jit(solution)/shard_map/all_to_all | solution.py:236
  417.7 203.1 %reduce-scatter.7.cloned.1.call-start = ((), (), s32[]{:S(2)}) async-start(), calls=%async_computation.17 | async-start | bytes 5308416 | tf_op jit(solution)/shard_map/reduce_scatter | solution.py:155
  490.6 28.9 %all-to-all-start.7 = ((bf16[1,1024,2,256]{3,2,0,1:T(2,128)(2,1)}), bf16[1,1024,2,256]{3,2,0,1:T(2,128)(2,1)S(1)}, u32[]{:S(2)}, u32[]{:S(2)}) async-start(bf16[1,1024,2,256]{3,2,0,1:T(2,128)(2,1)} %copy.152), calls=%async_computation.7 | async-start | bytes 2097152 | tf_op jit(solution)/shard_map/all_to_all | solution.py:243
  519.5 28.8 %all-to-all-start.6 = ((bf16[1,1024,2,256]{3,2,0,1:T(2,128)(2,1)}), bf16[1,1024,2,256]{3,2,0,1:T(2,128)(2,1)S(1)}, u32[]{:S(2)}, u32[]{:S(2)}) async-start(bf16[1,1024,2,256]{3,2,0,1:T(2,128)(2,1)} %copy.148), calls=%async_computation.6 | async-start | bytes 2097152 | tf_op jit(solution)/shard_map/all_to_all | solution.py:242
  548.3 28.8 %all-to-all-start.5 = ((bf16[1,1024,2,256]{3,2,0,1:T(2,128)(2,1)}), bf16[1,1024,2,256]{3,2,0,1:T(2,128)(2,1)S(1)}, u32[]{:S(2)}, u32[]{:S(2)}) async-start(bf16[1,1024,2,256]{3,2,0,1:T(2,128)(2,1)} %copy.145), calls=%async_computation.5 | async-start | bytes 2097152 | tf_op jit(solution)/shard_map/all_to_all | solution.py:241
  551.8 110.8 %reduce-scatter.5.cloned.1.call-start = ((), (), s32[]{:S(2)}) async-start(), calls=%async_computation.16 | async-start | bytes 10616832 | tf_op jit(solution)/shard_map/reduce_scatter | solution.py:155
  557.6 22.0 %copy-start.11 = (bf16[1,256,1152]{2,1,0:T(8,128)(2,1)S(1)}, bf16[1,256,1152]{2,1,0:T(8,128)(2,1)}, u32[]{:S(2)}) copy-start(bf16[1,256,1152]{2,1,0:T(8,128)(2,1)} %param.14) | copy-start | bytes 1769476
  557.6 22.0 %copy-start.38 = (f32[1152]{0:T(1024)S(1)}, f32[1152]{0:T(1024)}, u32[]{:S(2)}) copy-start(f32[1152]{0:T(1024)} %param.15) | copy-start | bytes 13828
  557.7 22.0 %copy-start.46 = (f32[256]{0:T(256)S(1)}, f32[256]{0:T(256)}, u32[]{:S(2)}) copy-start(f32[256]{0:T(256)} %copy-done.45) | copy-start | bytes 3076
  587.7 189.8 %reduce-scatter.11.cloned.1.call-start = ((), (), s32[]{:S(2)}) async-start(), calls=%async_computation.19 | async-start | bytes 17915904 | tf_op jit(solution)/shard_map/reduce_scatter | solution.py:155
  601.9 374.2 %reduce-scatter.9.cloned.1.call-start = ((), (), s32[]{:S(2)}) async-start(), calls=%async_computation.18 | async-start | bytes 35831808 | tf_op jit(solution)/shard_map/reduce_scatter | solution.py:155
  620.8 629.1 %all-reduce.6.cloned.1.call-start = ((), (), s32[]{:S(2)}) async-start(), calls=%async_computation.20 | async-start | bytes 15482880 | tf_op jit(solution)/shard_map/psum | solution.py:161
  977.6 8.0 copy-start.48
  977.6 53.8 %copy-start.16 = (f32[256,1152]{1,0:T(8,128)S(1)}, f32[256,1152]{1,0:T(8,128)}, u32[]{:S(2)}) copy-start(f32[256,1152]{1,0:T(8,128)} %copy-done.15) | copy-start | bytes 3538948
  977.7 53.8 %copy-start.49 = (f32[256]{0:T(256)S(1)}, f32[256]{0:T(256)}, u32[]{:S(2)}) copy-start(f32[256]{0:T(256)} %get-tuple-element.389) | copy-start | bytes 3076
  (48 other events, 145.6 us)
Sparse Core Ops, SparseCore 0:
  9.9 61.4 all-gather.4
  73.2 38.7 all-gather.6
  113.9 153.4 all-gather.8
  269.2 86.0 all-gather.10
  423.0 54.2 reduce-scatter.6
  587.8 74.8 reduce-scatter.4
  666.3 111.0 reduce-scatter.10
  781.0 195.0 reduce-scatter.8
  978.8 271.1 all-reduce.5
where the time goes:
time: 1280 us; the launch traced here: 1270 us
  waiting for transfers between devices  885 us (69%)
  matrix products  164 us (13%)
  blocking collectives  73.8 us (6%)
  local copies, waits for them, and re-layouts  57.5 us (4%)
  other arithmetic  42 us (3%)
  starting transfers between devices  28.3 us (2%)
  between operations  14.7 us (1%)
    reduce_scatter x4, waiting for transfers between devices, weight_term(): lax.psum_scatter(term_maker(activations, gradient).astype(jnp.bfloat16),...  355 us
    psum x1, waiting for transfers between devices, weight_term(): return lax.psum(sliced, 'seq').astype(jnp.float32)  216 us
    all_gather x4, waiting for transfers between devices, project(): lax.all_gather(weight_shard, 'fsdp', axis=0, tiled=True)  160 us
    dot_general x4, matrix products, project_back(): lax.dot_general(gradient, lax.all_gather(weight_shard, 'fsdp', axis=0, ti...  47.3 us
    psum x1, blocking collectives, on_device(): lax.psum((pre_attn_term, post_attn_term, pre_ffn_term, post_ffn_term), ('...  45.9 us
    dot_general x4, matrix products, term_maker(): lax.dot_general(activations, gradient, (((0,), (0,)), ((), ())), preferre...  42.8 us
    dot_general x4, matrix products, project(): jnp.dot(activations, lax.all_gather(weight_shard, 'fsdp', axis=0, tiled=T...  40.6 us
    dot_general x14, matrix products, batched_contraction(): jnp.einsum(pattern, left_side, right_side, preferred_element_type=jnp.flo...  32.9 us
  transfers between devices with their start and end apart: 16, of which 14 were waited for; matrix products, arithmetic and copies ran while one was open for 14% of the time, Pallas kernels for 0%

commit v1 on v0

--- a/solution.py
+++ b/solution.py
@@ -1,15 +1,16 @@
+import functools
 import math
 
 import jax
 import jax.numpy as jnp
 from jax import lax
+from jax.experimental import pallas as pl
+from jax.experimental.pallas import tpu as pltpu
 from jax.sharding import PartitionSpec as P
 
 H = 8
 KV = 4
 HD = 256
-FF = 6912
-
 
 EPSILON = 1e-06
 SOFT_CAP = 50.0
@@ -17,6 +18,10 @@
 GELU_COEFF = math.sqrt(2.0 / math.pi)
 CUBIC = 0.044715
 MASKED = -1e30
+MESH = pl.DeviceIdType.MESH
+F32 = jnp.float32
+BF16 = jnp.bfloat16
+LANES = 128
 
 
 def inverse_rms(values):
@@ -27,7 +32,7 @@
     weighted = upstream * gains
     inner_mean = jnp.mean(weighted * values, axis=-1, keepdims=True)
     gradient = inv_scale * weighted - values * (inv_scale * inv_scale * inv_scale) * inner_mean
-    gain_grad = jnp.sum(upstream * values * inv_scale, axis=0)
+    gain_grad = jnp.sum(upstream * values * inv_scale, axis=0, keepdims=True)
     return (gradient, gain_grad)
 
 
@@ -41,11 +46,407 @@
     return (activated, derivative)
 
 
+def plane_kernel(reduce, gather, n_in, n_own, body, *refs):
+    refs = list(refs)
+    part = refs.pop(0) if reduce else None
+    ins = [refs.pop(0) for _ in range(n_in)]
+    full = refs.pop(0) if gather else None
+    outs = [refs.pop(0) for _ in range(n_own)]
+    if reduce:
+        acc, other, ra, rb, rx, ry = (refs.pop(0) for _ in range(6))
+    block = refs.pop(0) if gather else None
+    lsem, ssem, rsem = refs
+    rows = ins[0].shape[0]
+    half = rows // 2
+    halves = (pl.ds(0, half), pl.ds(half, half))
+
+    me = lax.axis_index("fsdp")
+    core, xpos, ypos = me % 2, (me // 2) % 2, me // 4
+    step = 1 - 2 * core
+    mate = me + step
+    xn = me + 2 - 4 * xpos
+    yn = me + 4 - 8 * ypos
+    diag = xn + 4 - 8 * ypos
+
+    counter = [0]
+    waits = []
+
+    def send(src, dst, to):
+        k = counter[0]
+        counter[0] += 1
+        copy = pltpu.make_async_remote_copy(
+            src_ref=src, dst_ref=dst, send_sem=ssem.at[k], recv_sem=rsem.at[k],
+            device_id={"fsdp": to}, device_id_type=MESH,
+        )
+        copy.start()
+        waits.append(copy)
+        return copy
+
+    locals_ = []
+
+    def local(src, dst):
+        copy = pltpu.make_async_copy(src, dst, lsem.at[len(locals_)])
+        copy.start()
+        locals_.append(copy)
+        return copy
+
+    if reduce:
+        order = (diag, xn, yn, me)
+        own = [local(part.at[:, b], acc.at[k]) for k, b in enumerate(order)]
+
+    barrier = pltpu.get_barrier_semaphore()
+    for to in (mate, xn, yn):
+        pl.semaphore_signal(barrier, inc=1, device_id={"fsdp": to}, device_id_type=MESH)
+    pl.semaphore_wait(barrier, 3)
+
+    if reduce:
+        mates = [send(part.at[:, b + step], other.at[k], mate) for k, b in enumerate(order)]
+
+        def add(dst, src, lo, count):
+            def one(i, _):
+                dst[lo + i] = (dst[lo + i].astype(F32) + src[i].astype(F32)).astype(BF16)
+                return 0
+
+            lax.fori_loop(0, count, one, 0)
+
+        def join(k):
+            own[k].wait()
+            mates[k].wait_recv()
+            add(acc.at[k], other.at[k], 0, rows)
+
+        join(0)
+        ca = send(acc.at[0, halves[0]], ra, yn)
+        cb = send(acc.at[0, halves[1]], rb, xn)
+        join(1)
+        cx1 = send(acc.at[1, halves[1]], rx.at[halves[1]], xn)
+        join(2)
+        cy0 = send(acc.at[2, halves[0]], ry.at[halves[0]], yn)
+        ca.wait_recv()
+        add(acc.at[1], ra, 0, half)
+        cx0 = send(acc.at[1, halves[0]], rx.at[halves[0]], xn)
+        cb.wait_recv()
+        add(acc.at[2], rb, half, half)
+        cy1 = send(acc.at[2, halves[1]], ry.at[halves[1]], yn)
+        own[3].wait()
+        mates[3].wait_recv()
+        for copy in (cx1, cy0, cx0, cy1):
+            copy.wait_recv()
+
+    def one(i, sums):
+        if reduce:
+            total = (
+                acc[3, i].astype(F32) + other[3, i].astype(F32)
+            ) + (rx[i].astype(F32) + ry[i].astype(F32))
+        else:
+            total = None
+        sent, extra = body(i, total, ins, outs)
+        if gather:
+            block[i] = sent
+        if extra is None:
+            return sums
+        return tuple(s + e for s, e in zip(sums, extra))
+
+    width = ins[0].shape[-1]
+    n_sums = body.n_sums
+    sums = lax.fori_loop(0, rows, one, tuple(jnp.zeros((1, width), F32) for _ in range(n_sums)))
+    for s, ref in zip(sums, outs[n_own - n_sums :]):
+        ref[...] = s
+
+    if gather:
+        keep = local(block, full.at[:, me])
+        h0, h1 = halves
+
+        def forward(copy, where, blk, to):
+            copy.wait_recv()
+            return send(full.at[where, blk], full.at[where, blk], to)
+
+        y0 = send(block.at[h0], full.at[h0, me], yn)
+        x1 = send(block.at[h1], full.at[h1, me], xn)
+        y1 = send(block.at[h1], full.at[h1, me], yn)
+        x0 = send(block.at[h0], full.at[h0, me], xn)
+        m = send(block, full.at[:, me], mate)
+        gx = forward(y0, h0, yn, xn)
+        fy0 = send(full.at[h0, yn], full.at[h0, yn], mate)
+        gy = forward(x1, h1, xn, yn)
+        fx1 = send(full.at[h1, xn], full.at[h1, xn], mate)
+        forward(y1, h1, yn, mate)
+        forward(x0, h0, xn, mate)
+        forward(gx, h0, diag, mate)
+        forward(gy, h1, diag, mate)
+        for copy in (m, fy0, fx1):
+            copy.wait_recv()
+        for copy in waits[-4:]:
+            copy.wait_recv()
+        keep.wait()
+    for copy in waits:
+        copy.wait_send()
+
+
+def plane_call(name, cid, body, part, ins, own_types, gather, planes, width):
+    reduce = part is not None
+    rows, r = ins[0].shape[0], ins[0].shape[1]
+    shape = (rows, r, width)
+    out_shape, out_specs = [], []
+    if gather:
+        out_shape.append(jax.ShapeDtypeStruct((rows, planes, r, width), BF16))
+        out_specs.append(pl.BlockSpec(memory_space=pl.ANY))
+    for t in own_types:
+        out_shape.append(jax.ShapeDtypeStruct(shape, t))
+        out_specs.append(pl.BlockSpec(memory_space=pltpu.VMEM))
+    for _ in range(body.n_sums):
+        out_shape.append(jax.ShapeDtypeStruct((1, width), F32))
+        out_specs.append(pl.BlockSpec(memory_space=pltpu.VMEM))
+    scratch = []
+    if reduce:
+        hs = (rows // 2, r, width)
+        scratch += [pltpu.VMEM((4,) + shape, BF16)] * 2 + [pltpu.VMEM(hs, BF16)] * 2
+        scratch += [pltpu.VMEM(shape, BF16)] * 2
+    if gather:
+        scratch.append(pltpu.VMEM(shape, BF16))
+    n_send = (10 if reduce else 0) + (13 if gather else 0)
+    scratch += [
+        pltpu.SemaphoreType.DMA((5,)),
+        pltpu.SemaphoreType.DMA((n_send,)),
+        pltpu.SemaphoreType.DMA((n_send,)),
+    ]
+    operands = ([part] if reduce else []) + list(ins)
+    in_specs = ([pl.BlockSpec(memory_space=pl.ANY)] if reduce else []) + [
+        pl.BlockSpec(memory_space=pltpu.VMEM)
+    ] * len(ins)
+    return pl.pallas_call(
+        functools.partial(
+            plane_kernel, reduce, gather, len(ins), len(own_types) + body.n_sums, body
+        ),
+        name=name,
+        out_shape=out_shape,
+        in_specs=in_specs,
+        out_specs=out_specs,
+        scratch_shapes=scratch,
+        compiler_params=pltpu.CompilerParams(collective_id=cid, has_side_effects=True),
+    )(*operands)
+
+
+def with_sums(n):
+    def mark(f):
+        f.n_sums = n
+        return f
+
+    return mark
+
+
+@with_sums(0)
+def body_first(i, _, ins, outs):
+    tokens, gain = ins
+    values = tokens[i].astype(F32)
+    return (values * inverse_rms(values) * gain[...]).astype(BF16), None
+
+
+@with_sums(0)
+def body_mid(i, branch, ins, outs):
+    tokens, gain_attn, gain_ffn = ins
+    branch_out, hidden_out = outs
+    hidden = tokens[i].astype(F32) + branch * inverse_rms(branch) * gain_attn[...]
+    branch_out[i] = branch
+    hidden_out[i] = hidden
+    return (hidden * inverse_rms(hidden) * gain_ffn[...]).astype(BF16), None
+
+
+@with_sums(1)
+def body_turn(i, branch, ins, outs):
+    hidden, upstream, gain = ins
+    scale = inverse_rms(branch)
+    outs[0][i] = (hidden[i] + branch * scale * gain[...]).astype(BF16)
+    grad, term = norm_back(upstream[i].astype(F32), branch, scale, gain[...])
+    return grad.astype(BF16), (term,)
+
+
+@with_sums(2)
+def body_back(i, delta, ins, outs):
+    hidden, branch, upstream, gain_attn, gain_ffn = ins
+    hid, y1 = hidden[i], branch[i]
+    part, term_ffn = norm_back(delta, hid, inverse_rms(hid), gain_ffn[...])
+    hid_grad = upstream[i].astype(F32) + part
+    outs[0][i] = hid_grad
+    grad, term_attn = norm_back(hid_grad, y1, inverse_rms(y1), gain_attn[...])
+    return grad.astype(BF16), (term_ffn, term_attn)
+
+
+@with_sums(1)
+def body_last(i, delta, ins, outs):
+    tokens, hidden_grad, gain = ins
+    values = tokens[i].astype(F32)
+    part, term = norm_back(delta, values, inverse_rms(values), gain[...])
+    outs[0][i] = (hidden_grad[i] + part).astype(BF16)
+    return None, (term,)
+
+
+def scores(q, k):
+    s = jnp.einsum("bqd,bkd->bqk", q, k, preferred_element_type=F32) * QUERY_FACTOR
+    t = jnp.tanh(s / SOFT_CAP)
+    length = q.shape[1]
+    allowed = jnp.arange(length)[None, :] <= jnp.arange(length)[:, None]
+    return t, jnp.where(allowed[None], SOFT_CAP * t, MASKED)
+
+
+def attend(q, k, v):
+    _, c = scores(q, k)
+    top = jnp.max(c, axis=-1, keepdims=True)
+    lse = top + jnp.log(jnp.sum(jnp.exp(c - top), axis=-1, keepdims=True))
+    p = jnp.exp(c - lse).astype(BF16)
+    return jnp.einsum("bqk,bkd->bqd", p, v, preferred_element_type=F32).astype(BF16), lse
+
+
+def attend_back(q, k, v, o, do, lse):
+    t, c = scores(q, k)
+    p = jnp.exp(c - lse)
+    dd = jnp.sum(do.astype(F32) * o.astype(F32), axis=-1, keepdims=True)
+    dp = jnp.einsum("bqd,bkd->bqk", do, v, preferred_element_type=F32)
+    ds = (p * (dp - dd) * (1.0 - t * t) * QUERY_FACTOR).astype(BF16)
+    dv = jnp.einsum("bqk,bqd->bkd", p.astype(BF16), do, preferred_element_type=F32)
+    dk = jnp.einsum("bqk,bqd->bkd", ds, q, preferred_element_type=F32)
+    dq = jnp.einsum("bqk,bkd->bqd", ds, k, preferred_element_type=F32)
+    return dq.astype(BF16), dk.astype(BF16), dv.astype(BF16)
+
+
+def dot_f32(a, b):
+    return jnp.dot(a, b, preferred_element_type=F32)
+
+
+def dot_nt(a, b):
+    return lax.dot_general(a, b, (((1,), (1,)), ((), ())), preferred_element_type=F32)
+
+
+def dot_tn(a, b):
+    return lax.dot_general(a, b, (((0,), (0,)), ((), ())), preferred_element_type=F32)
+
+
+def swap(x, axis):
+    return lax.all_to_all(x, axis, split_axis=0, concat_axis=0, tiled=True)
+
+
+def on_device_plane(
+    ns, nf,
+    tokens, pre_attn_gain, qkv_weight, out_weight, post_attn_gain, pre_ffn_gain,
+    gate_up_weight, down_weight, post_ffn_gain, out_grad,
+):
+    _, chunk, width = tokens.shape
+    length = chunk * ns
+    spp = nf // ns
+    r = chunk // nf
+    rows = spp * ns
+    group = H // KV
+    ff = down_weight.shape[0]
+    ffp = -(-ff // LANES) * LANES
+    depth = qkv_weight.shape[0]
+
+    both = jnp.stack([tokens[0], out_grad[0]])
+    both = both.reshape(2, nf, r, width).transpose(1, 0, 2, 3)
+    both = swap(both, "fsdp")
+    both = swap(both.reshape(ns, spp * 2 * r, width), "seq")
+    both = both.reshape(ns, spp, 2, r, width)
+    x_own = both[:, :, 0].transpose(1, 0, 2, 3).reshape(rows, r, width)
+    g_own = both[:, :, 1].transpose(1, 0, 2, 3).reshape(rows, r, width)
+
+    q_cols = qkv_weight[:, : H * HD].reshape(depth, H, HD)
+    k_cols = jnp.repeat(qkv_weight[:, H * HD : (H + KV) * HD].reshape(depth, KV, HD), group, axis=1)
+    v_cols = jnp.repeat(qkv_weight[:, (H + KV) * HD :].reshape(depth, KV, HD), group, axis=1)
+    w_qkv = jnp.concatenate([q_cols, k_cols, v_cols], axis=2).transpose(1, 0, 2)
+    w_qkv = swap(w_qkv, "fsdp").reshape(nf * depth, 3 * HD)
+    w_gu = jnp.pad(gate_up_weight.reshape(depth, 2, nf, ff), ((0, 0), (0, 0), (0, 0), (0, ffp - ff)))
+    w_gu = swap(w_gu.transpose(2, 0, 1, 3).reshape(nf, depth, 2 * ffp), "fsdp")
+    w_gu = w_gu.reshape(nf * depth, 2 * ffp)
+    w_down = jnp.pad(down_weight, ((0, ffp - ff), (0, 0)))
+
+    gains = [g.reshape(1, width) for g in (pre_attn_gain, post_attn_gain, pre_ffn_gain, post_ffn_gain)]
+    flat = (rows * nf * r, width)
+    terms = (rows, nf, r, width)
+
+    a_full, = plane_call("gather_a", 1, body_first, None, [x_own, gains[0]], [], True, nf, width)
+    a_full = a_full.reshape(flat)
+    qkv = dot_f32(a_full, w_qkv).astype(BF16)
+    q, k, v = (qkv[:, i * HD : (i + 1) * HD].reshape(spp, length, HD) for i in range(3))
+    o, lse = attend(q, k, v)
+    o_flat = o.reshape(-1, HD)
+    y1_terms = dot_f32(o_flat, out_weight).astype(BF16).reshape(terms)
+    n_full, y1, hidden = plane_call(
+        "mid", 2, body_mid, y1_terms, [x_own, gains[1], gains[2]], [F32, F32], True, nf, width
+    )
+    n_full = n_full.reshape(flat)
+    gu = dot_f32(n_full, w_gu)
+    gate, up = gu[:, :ffp], gu[:, ffp:]
+    activated, derivative = gelu_pair(gate)
+    mixed = (activated * up).astype(BF16)
+    y2_terms = dot_f32(mixed, w_down).astype(BF16).reshape(terms)
+    dy2_full, out_own, post_ffn_term = plane_call(
+        "turn", 3, body_turn, y2_terms, [hidden, g_own, gains[3]], [BF16], True, nf, width
+    )
+    dy2_full = dy2_full.reshape(flat)
+    down_wg = dot_tn(mixed, dy2_full)[:ff].astype(BF16)
+    down_wg = lax.psum(down_wg, "seq")
+    dm = dot_nt(dy2_full, w_down)
+    dgu = jnp.concatenate([dm * up * derivative, dm * activated], axis=1).astype(BF16)
+    dn_terms = dot_nt(dgu, w_gu).astype(BF16).reshape(terms)
+    gu_wg = dot_tn(n_full, dgu).astype(BF16).reshape(nf, depth, 2 * ffp)
+    gu_wg = swap(gu_wg, "fsdp").reshape(nf, depth, 2, ffp)[..., :ff]
+    gu_wg = lax.psum(gu_wg.transpose(1, 2, 0, 3).reshape(depth, 2 * nf * ff), "seq")
+    dy1_full, hidden_grad, pre_ffn_term, post_attn_term = plane_call(
+        "back", 4, body_back, dn_terms, [hidden, y1, g_own, gains[1], gains[2]], [F32], True, nf, width
+    )
+    dy1_full = dy1_full.reshape(flat)
+    do = dot_nt(dy1_full, out_weight).astype(BF16).reshape(o.shape)
+    out_wg = dot_tn(o_flat, dy1_full).astype(BF16)
+    dq, dk, dv = attend_back(q, k, v, o, do, lse)
+    dqkv = jnp.concatenate([dq, dk, dv], axis=2).reshape(-1, 3 * HD)
+    da_terms = dot_nt(dqkv, w_qkv).astype(BF16).reshape(terms)
+    qkv_wg = dot_tn(a_full, dqkv).astype(BF16).reshape(nf, depth, 3 * HD)
+    qkv_wg = swap(qkv_wg, "fsdp").transpose(1, 0, 2)
+    kv_wg = qkv_wg[:, :, HD:].astype(F32).reshape(depth, KV, group, 2 * HD).sum(axis=2).astype(BF16)
+    qkv_wg = jnp.concatenate(
+        [
+            qkv_wg[:, :, :HD].reshape(depth, H * HD),
+            kv_wg[:, :, :HD].reshape(depth, KV * HD),
+            kv_wg[:, :, HD:].reshape(depth, KV * HD),
+        ],
+        axis=1,
+    )
+    out_wg, qkv_wg = lax.psum((out_wg, qkv_wg), "seq")
+    tg_own, pre_attn_term = plane_call(
+        "last", 5, body_last, da_terms, [x_own, hidden_grad, gains[0]], [BF16], False, nf, width
+    )
+    back = jnp.stack([out_own, tg_own], axis=2)
+    back = jnp.stack([out_own, tg_own]).reshape(2, spp, ns, r, width).transpose(2, 1, 0, 3, 4)
+    back = swap(back.reshape(ns, spp * 2 * r, width), "seq").reshape(nf, 2, r, width)
+    back = swap(back, "fsdp").transpose(1, 0, 2, 3).reshape(2, 1, chunk, width)
+    gain_sums = lax.psum(
+        jnp.concatenate([pre_attn_term, post_attn_term, pre_ffn_term, post_ffn_term]), ("seq", "fsdp")
+    )
+    return (
+        back[0],
+        back[1].astype(F32),
+        gain_sums[0],
+        qkv_wg.astype(F32),
+        out_wg.astype(F32),
+        gain_sums[1],
+        gain_sums[2],
+        gu_wg.astype(F32),
+        down_wg.astype(F32),
+        gain_sums[3],
+    )
+
+
+def gathered_norm_back(upstream, values, inv_scale, gains):
+    weighted = upstream * gains
+    inner_mean = jnp.mean(weighted * values, axis=-1, keepdims=True)
+    gradient = inv_scale * weighted - values * (inv_scale * inv_scale * inv_scale) * inner_mean
+    gain_grad = jnp.sum(upstream * values * inv_scale, axis=0)
+    return (gradient, gain_grad)
+
+
 def batched_contraction(pattern, left_side, right_side):
     return jnp.einsum(pattern, left_side, right_side, preferred_element_type=jnp.float32)
 
 
-def capped_scores(block_of_queries, key_row_slices, offset):
+def gathered_capped_scores(block_of_queries, key_row_slices, offset):
     amount = block_of_queries.shape[0]
     key_count = key_row_slices.shape[0]
     unscaled_logits = (
@@ -60,7 +461,7 @@
     return (tanh_part, capped)
 
 
-def attend(queries, key_row_slices, value_row_slices):
+def gathered_attend(queries, key_row_slices, value_row_slices):
     length = queries.shape[0]
     block_size = min(512, length)
     blocks = length // block_size
@@ -68,7 +469,7 @@
     def one_block(block_id):
         offset = block_id * block_size
         block_of_queries = lax.dynamic_slice_in_dim(queries, offset, block_size, 0)
-        tanh_part, capped = capped_scores(block_of_queries, key_row_slices, offset)
+        tanh_part, capped = gathered_capped_scores(block_of_queries, key_row_slices, offset)
         biggest = jnp.max(capped, axis=-1, keepdims=True)
         logsum = biggest + jnp.log(jnp.sum(jnp.exp(capped - biggest), axis=-1, keepdims=True))
         attention_probabilities = jnp.exp(capped - logsum).astype(jnp.bfloat16)
@@ -81,7 +482,7 @@
     return (outputs.reshape(queries.shape), logsums)
 
 
-def attend_back(queries, key_row_slices, value_row_slices, outputs, out_delta, logsums):
+def gathered_attend_back(queries, key_row_slices, value_row_slices, outputs, out_delta, logsums):
     length = queries.shape[0]
     block_size = min(512, length)
     blocks = length // block_size
@@ -93,7 +494,7 @@
         offset = block_id * block_size
         block_of_queries = lax.dynamic_slice_in_dim(queries, offset, block_size, 0)
         block_correction = lax.dynamic_slice_in_dim(out_delta, offset, block_size, 0)
-        tanh_part, capped = capped_scores(block_of_queries, key_row_slices, offset)
+        tanh_part, capped = gathered_capped_scores(block_of_queries, key_row_slices, offset)
         attention_probabilities = jnp.exp(capped - block_logsum[..., None])
         probability_gradients = batched_contraction(
             "olv,ilv->loi", block_correction, value_row_slices
@@ -128,7 +529,7 @@
     )
 
 
-def project(activations, weight_shard):
+def gathered_project(activations, weight_shard):
     return jnp.dot(
         activations,
         lax.all_gather(weight_shard, "fsdp", axis=0, tiled=True),
@@ -136,7 +537,7 @@
     )
 
 
-def project_back(gradient, weight_shard):
+def gathered_project_back(gradient, weight_shard):
     return lax.dot_general(
         gradient,
         lax.all_gather(weight_shard, "fsdp", axis=0, tiled=True),
@@ -161,7 +562,7 @@
     return lax.psum(sliced, "seq").astype(jnp.float32)
 
 
-def on_device(
+def gathered_on_device(
     tokens,
     pre_attn_gain,
     qkv_weight,
@@ -176,10 +577,11 @@
     groups, local_len, width = tokens.shape
     row_count = groups * local_len
     head_repeat = H // KV
+    ff = gate_up_weight.shape[1] // 2
     residual_in = tokens.reshape(row_count, width).astype(jnp.float32)
     scale_one = inverse_rms(residual_in)
     normed_in = (residual_in * scale_one * pre_attn_gain).astype(jnp.bfloat16)
-    projected = project(normed_in, qkv_weight).astype(jnp.bfloat16)
+    projected = gathered_project(normed_in, qkv_weight).astype(jnp.bfloat16)
     queries = projected[:, : H * HD].reshape(groups, local_len, H, HD)
     key_row_slices = jnp.repeat(
         projected[:, H * HD : (H + KV) * HD].reshape(groups, local_len, KV, HD), head_repeat, axis=2
@@ -192,21 +594,21 @@
         lax.all_to_all(key_row_slices, "seq", split_axis=2, concat_axis=1, tiled=True),
         lax.all_to_all(value_row_slices, "seq", split_axis=2, concat_axis=1, tiled=True),
     )
-    head_out, logsums = jax.vmap(attend)(head_queries, head_keys, head_values)
+    head_out, logsums = jax.vmap(gathered_attend)(head_queries, head_keys, head_values)
     attn_out = lax.all_to_all(head_out, "seq", split_axis=1, concat_axis=2, tiled=True).reshape(
         row_count, H * HD
     )
-    branch_one = project(attn_out, out_weight)
+    branch_one = gathered_project(attn_out, out_weight)
     scale_two = inverse_rms(branch_one)
     hidden = residual_in + branch_one * scale_two * post_attn_gain
     scale_three = inverse_rms(hidden)
     normed_mid = (hidden * scale_three * pre_ffn_gain).astype(jnp.bfloat16)
-    gate_up = project(normed_mid, gate_up_weight)
-    gate_part = gate_up[:, :FF]
-    up_part = gate_up[:, FF:]
+    gate_up = gathered_project(normed_mid, gate_up_weight)
+    gate_part = gate_up[:, :ff]
+    up_part = gate_up[:, ff:]
     activated, derivative = gelu_pair(gate_part)
     mixed = (activated * up_part).astype(jnp.bfloat16)
-    branch_two = project(mixed, down_weight)
+    branch_two = gathered_project(mixed, down_weight)
     scale_four = inverse_rms(branch_two)
     layer_out = (
         (hidden + branch_two * scale_four * post_ffn_gain)
@@ -214,27 +616,27 @@
         .reshape(groups, local_len, width)
     )
     upstream = out_grad.reshape(row_count, width).astype(jnp.float32)
-    branch_two_grad, post_ffn_term = norm_back(upstream, branch_two, scale_four, post_ffn_gain)
+    branch_two_grad, post_ffn_term = gathered_norm_back(upstream, branch_two, scale_four, post_ffn_gain)
     branch_two_grad = branch_two_grad.astype(jnp.bfloat16)
     down_wgrad = weight_term(mixed, branch_two_grad)
-    mixed_grad = project_back(branch_two_grad, down_weight)
+    mixed_grad = gathered_project_back(branch_two_grad, down_weight)
     gate_up_grad = jnp.concatenate(
         [mixed_grad * up_part * derivative, mixed_grad * activated], axis=1
     ).astype(jnp.bfloat16)
     gate_up_wgrad = weight_term(normed_mid, gate_up_grad)
-    normed_mid_grad = project_back(gate_up_grad, gate_up_weight)
-    hidden_part, pre_ffn_term = norm_back(normed_mid_grad, hidden, scale_three, pre_ffn_gain)
+    normed_mid_grad = gathered_project_back(gate_up_grad, gate_up_weight)
+    hidden_part, pre_ffn_term = gathered_norm_back(normed_mid_grad, hidden, scale_three, pre_ffn_gain)
     hidden_grad = upstream + hidden_part
-    branch_one_grad, post_attn_term = norm_back(hidden_grad, branch_one, scale_two, post_attn_gain)
+    branch_one_grad, post_attn_term = gathered_norm_back(hidden_grad, branch_one, scale_two, post_attn_gain)
     branch_one_grad = branch_one_grad.astype(jnp.bfloat16)
     out_wgrad = weight_term(attn_out, branch_one_grad)
     attn_grad = (
-        project_back(branch_one_grad, out_weight)
+        gathered_project_back(branch_one_grad, out_weight)
         .astype(jnp.bfloat16)
         .reshape(groups, local_len, H, HD)
     )
     head_delta = lax.all_to_all(attn_grad, "seq", split_axis=2, concat_axis=1, tiled=True)
-    query_gradient, key_grad, value_grad = jax.vmap(attend_back)(
+    query_gradient, key_grad, value_grad = jax.vmap(gathered_attend_back)(
         head_queries, head_keys, head_values, head_out, head_delta, logsums
     )
     query_tok, key_tok, value_tok = (
@@ -263,8 +665,8 @@
         axis=1,
     )
     qkv_wgrad = weight_term(normed_in, qkv_grad)
-    normed_in_grad = project_back(qkv_grad, qkv_weight)
-    input_part, pre_attn_term = norm_back(normed_in_grad, residual_in, scale_one, pre_attn_gain)
+    normed_in_grad = gathered_project_back(qkv_grad, qkv_weight)
+    input_part, pre_attn_term = gathered_norm_back(normed_in_grad, residual_in, scale_one, pre_attn_gain)
     tokens_grad = (hidden_grad + input_part).reshape(groups, local_len, width)
     gain_sums = lax.psum(
         (pre_attn_term, post_attn_term, pre_ffn_term, post_ffn_term), ("seq", "fsdp")
@@ -284,30 +686,20 @@
 
 
 def solution(mesh):
+    ns, nf = mesh.shape["seq"], mesh.shape["fsdp"]
+    token_spec, row_spec = P("fsdp", "seq", None), P("fsdp", None)
     in_specs = (
-        P("fsdp", "seq", None),
-        P(),
-        P("fsdp", None),
-        P("fsdp", None),
-        P(),
-        P(),
-        P("fsdp", None),
-        P("fsdp", None),
-        P(),
-        P("fsdp", "seq", None),
+        token_spec, P(), row_spec, row_spec, P(), P(), row_spec, row_spec, P(), token_spec,
     )
     out_specs = (
-        P("fsdp", "seq", None),
-        P("fsdp", "seq", None),
-        P(),
-        P("fsdp", None),
-        P("fsdp", None),
-        P(),
-        P(),
-        P("fsdp", None),
-        P("fsdp", None),
-        P(),
-    )
+        token_spec, token_spec, P(), row_spec, row_spec, P(), P(), row_spec, row_spec, P(),
+    )
+
+    def on_device(*args):
+        if nf == 8 and nf == H and nf % ns == 0 and args[0].shape[0] == 1:
+            return on_device_plane(ns, nf, *args)
+        return gathered_on_device(*args)
+
     return jax.shard_map(
         on_device, mesh=mesh, in_specs=in_specs, out_specs=out_specs, check_vma=False
     )

time: 1280 us -> 844 us (0.66)
  waiting for transfers between devices: 885 us -> 188 us
  Pallas kernels: 0 us -> 229 us
  blocking collectives: 73.8 us -> 141 us
  matrix products: 164 us -> 132 us
  local copies, waits for them, and re-layouts: 57.5 us -> 81.6 us
  other arithmetic: 42 us -> 25.1 us
    reduce_scatter x4 -> x0, waiting for transfers between devices: 355 us -> none  [weight_term(): lax.psum_scatter(term_maker(activations, gradient).astype(jnp.bfloat16),...]
    pallas_call x0 -> x5, Pallas kernels: none -> 229 us  [plane_call(): pl.pallas_call(functools.partial(plane_kernel, reduce, gather, len(ins),...]
    all_gather x4 -> x0, waiting for transfers between devices: 160 us -> none  [project(): lax.all_gather(weight_shard, 'fsdp', axis=0, tiled=True)]
    all_to_all x7 -> x6, waiting for transfers between devices: 152 us -> 56.7 us  [swap(): return lax.all_to_all(x, axis, split_axis=0, concat_axis=0, tiled=True)]
    psum x1, waiting for transfers between devices: 216 us -> 131 us  [on_device_plane(): out_wg, qkv_wg = lax.psum((out_wg, qkv_wg), 'seq')]
    all_to_all x1 -> x2, blocking collectives: 27.9 us -> 83.4 us  [swap(): return lax.all_to_all(x, axis, split_axis=0, concat_axis=0, tiled=True)]
    reshape x4 -> x16, local copies, waits for them, and re-layouts: 3.47 us -> 47.2 us  [the longest x2 14.3 us: on_device_plane(): gate_up_weight.reshape(depth, 2, nf, ff)]
    dot_general x26 -> x18, matrix products: 164 us -> 132 us  [the longest x4 44.1 us: dot_nt(): lax.dot_general(a, b, (((1,), (1,)), ((), ())), preferred_element_type=F32)]
  transfers between devices with their start and end apart: 16 -> 7, of which waited for: 14 -> 4; matrix products, arithmetic and copies ran while one was open for 14% -> 13% of each run, Pallas kernels for 0% -> 15%
where the time goes in v1:
time: 844 us; the launch traced here: 838 us
  Pallas kernels  229 us (27%)
  waiting for transfers between devices  188 us (22%)
  blocking collectives  141 us (17%)
  matrix products  132 us (16%)
  local copies, waits for them, and re-layouts  81.6 us (10%)
  starting transfers between devices  26.4 us (3%)
  other arithmetic  25.1 us (3%)
  between operations  14.9 us (2%)
    pallas_call x5, Pallas kernels, plane_call(): pl.pallas_call(functools.partial(plane_kernel, reduce, gather, len(ins),...  229 us
    psum x1, waiting for transfers between devices, on_device_plane(): out_wg, qkv_wg = lax.psum((out_wg, qkv_wg), 'seq')  131 us
    all_to_all x2, blocking collectives, swap(): return lax.all_to_all(x, axis, split_axis=0, concat_axis=0, tiled=True)  83.4 us
    psum x1, blocking collectives, on_device_plane(): lax.psum(jnp.concatenate([pre_attn_term, post_attn_term, pre_ffn_term, po...  58 us
    all_to_all x6, waiting for transfers between devices, swap(): return lax.all_to_all(x, axis, split_axis=0, concat_axis=0, tiled=True)  56.7 us
    dot_general x4, matrix products, dot_nt(): lax.dot_general(a, b, (((1,), (1,)), ((), ())), preferred_element_type=F32)  44.1 us
    dot_general x4, matrix products, dot_tn(): lax.dot_general(a, b, (((0,), (0,)), ((), ())), preferred_element_type=F32)  36.6 us
    dot_general x4, matrix products, dot_f32(): return jnp.dot(a, b, preferred_element_type=F32)  31.9 us
  transfers between devices with their start and end apart: 7, of which 4 were waited for; matrix products, arithmetic and copies ran while one was open for 13% of the time, Pallas kernels for 15%

profile of v1, /device:TPU:0, one launch (start us, length us, event | category | flops | bytes accessed | tf_op | source)
XLA Modules:
  0.0 838.2 jit_solution(10611591314070262993)
XLA Ops:
  8.8 21.8 %all_to_all.40 = bf16[8,2,32,1152]{3,2,1,0:T(8,128)(2,1)} all-to-all(bf16[8,2,32,1152]{3,2,1,0:T(8,128)(2,1)S(1)} %copy.84), channel_id=1, replica_groups=mesh['seq'=4,'fsdp'=8] {'fsdp'}, dimensions={0} | all-to-all | bytes 2359296 | tf_op jit(solution)/shard_map/all_to_all | solution.py:324
  30.6 4.9 all-to-all-start.1
  47.3 16.4 %all-to-all-done.1 = bf16[4,128,1152]{2,1,0:T(8,128)(2,1)S(1)} async-done(((bf16[4,128,1152]{2,1,0:T(8,128)(2,1)}), bf16[4,128,1152]{2,1,0:T(8,128)(2,1)S(1)}, u32[]{:S(2)}, u32[]{:S(2)}) %all-to-all-start.1) | async-done | bytes 1179680 | tf_op jit(solution)/shard_map/all_to_all | solution.py:324
  70.0 8.9 %reshape.215 = bf16[144,2,8,864]{3,2,1,0:T(8,128)(2,1)} reshape(bf16[144,13824]{1,0:T(8,128)(2,1)} %param.16) | data formatting | bytes 7962624 | tf_op jit(solution)/shard_map/reshape | solution.py:355
  79.0 5.4 copy.88
  84.3 5.8 pad_bitcast_fusion
  90.1 9.9 %reshape.216 = bf16[8,144,1792]{2,1,0:T(8,128)(2,1)} reshape(bf16[8,144,2,896]{3,2,1,0:T(2,128)(2,1)} %pad_bitcast_fusion) | data formatting | bytes 8257536 | tf_op jit(solution)/shard_map/reshape | solution.py:356
  103.0 27.4 %gather_a.1 = bf16[8,8,32,1152]{3,2,1,0:T(8,128)(2,1)} custom-call(bf16[8,32,1152]{2,1,0:T(8,128)(2,1)} %bitcast.100, f32[1,1152]{1,0:T(1,128)} %reshape.199.refs_1_.refs_3_), custom_call_target="tpu_custom_call" | custom-call | tf_op jit(solution)/shard_map/gather_a/pallas_call | solution.py:216
  130.4 4.8 all-to-all-start.3
  135.2 7.2 convolution_convert_fusion.5
  156.9 71.7 %mid.1 = (bf16[8,8,32,1152]{3,2,1,0:T(8,128)(2,1)}, f32[8,32,1152]{2,1,0:T(8,128)}, f32[8,32,1152]{2,1,0:T(8,128)}) custom-call(bf16[8,8,32,1152]{3,2,1,0:T(8,128)(2,1)} %bitcast.97, bf16[8,32,1152]{2,1,0:T(8,128)(2,1)} %bitcast.101, f32[1,1152]{1,0:T(1,128)} %reshape.212.refs_2_.refs_4_, f32[1,1152]{1,0:T(1,128)} %reshape.213.refs_3_.refs_5_), custom_call_target="tpu_custom_call" | custom-call | tf_op jit(solution)/shard_map/mid/pallas_call | solution.py:216
  228.7 13.7 %fusion.21 = f32[2048,1792]{0,1:T(8,128)S(1)} fusion(bf16[2048,1152]{1,0:T(8,128)(2,1)} %bitcast.145, bf16[1152,1792]{1,0:T(8,128)(2,1)} %bitcast.17), kind=kOutput, calls=%fused_computation.65 | convolution fusion | flops 8455716864 | bytes 23527424 | tf_op jit(solution)/shard_map/dot_general | solution.py:312
  248.0 7.3 convolution_convert_fusion
  255.3 50.5 %turn.1 = (bf16[8,8,32,1152]{3,2,1,0:T(8,128)(2,1)}, bf16[8,32,1152]{2,1,0:T(8,128)(2,1)}, f32[1,1152]{1,0:T(1,128)}) custom-call(bf16[8,8,32,1152]{3,2,1,0:T(8,128)(2,1)} %bitcast.115, f32[8,32,1152]{2,1,0:T(8,128)} %get-tuple-element.23.refs_1_, bf16[8,32,1152]{2,1,0:T(8,128)(2,1)} %bitcast.109, f32[1,1152]{1,0:T(1,128)} %reshape.220.refs_3_), custom_call_target="tpu_custom_call" | custom-call | tf_op jit(solution)/shard_map/turn/pallas_call | solution.py:216
  305.9 14.9 %fusion.7 = (bf16[2048,896]{0,1:T(8,128)(2,1)S(1)}, bf16[2048,896]{0,1:T(8,128)(2,1)S(1)}) fusion(f32[2048,1792]{0,1:T(8,128)} %copy-done.2, bf16[2048,1152]{1,0:T(8,128)(2,1)} %bitcast.143, bf16[864,1152]{1,0:T(8,128)(2,1)} %param.17), kind=kOutput, calls=%fused_computation.19 | convolution fusion | flops 4270063616 | bytes 28729344 | tf_op jit(solution)/shard_map/dot_general | solution.py:316
  320.8 16.2 %convolution_convert_fusion.2 = bf16[2048,1152]{1,0:T(8,128)(2,1)} fusion(bf16[1152,1792]{1,0:T(8,128)(2,1)} %bitcast.17, bf16[2048,896]{0,1:T(8,128)(2,1)S(1)} %get-tuple-element.43, bf16[2048,896]{0,1:T(8,128)(2,1)S(1)} %get-tuple-element.42), kind=kOutput, calls=%fused_computation.9 | convolution fusion | flops 8472756224 | bytes 16187392 | tf_op jit(solution)/shard_map/dot_general | solution.py:316
  337.0 52.9 %back.1 = (bf16[8,8,32,1152]{3,2,1,0:T(8,128)(2,1)}, f32[8,32,1152]{2,1,0:T(8,128)}, f32[1,1152]{1,0:T(1,128)}, f32[1,1152]{1,0:T(1,128)}) custom-call(bf16[8,8,32,1152]{3,2,1,0:T(8,128)(2,1)} %bitcast.113, f32[8,32,1152]{2,1,0:T(8,128)} %get-tuple-element.23.refs_1_, f32[8,32,1152]{2,1,0:T(8,128)} %get-tuple-element.26.refs_2_, ...), custom_call_target="tpu_custom_call" | custom-call | tf_op jit(solution)/shard_map/back/pallas_call | solution.py:216
  394.4 7.2 multiply_convert_fusion
  414.5 8.4 %convolution_convert_fusion.6 = bf16[1152,768]{1,0:T(8,128)(2,1)} fusion(bf16[2048,1152]{1,0:T(8,128)(2,1)} %bitcast.112, bf16[2048,768]{1,0:T(8,128)(2,1)} %bitcast.122), kind=kOutput, calls=%fused_computation.30 | convolution fusion | flops 3624763392 | bytes 9633792 | tf_op jit(solution)/shard_map/dot_general | solution.py:320
  426.9 15.1 %convolution_convert_fusion.4 = bf16[1152,1792]{1,0:T(8,128)(2,1)} fusion(bf16[2048,1152]{1,0:T(8,128)(2,1)} %bitcast.146, bf16[2048,896]{0,1:T(8,128)(2,1)} %copy-done.26, bf16[2048,896]{0,1:T(8,128)(2,1)} %copy-done.25), kind=kOutput, calls=%fused_computation.11 | convolution fusion | flops 8472461312 | bytes 16187392 | tf_op jit(solution)/shard_map/dot_general | solution.py:320
  442.0 8.0 all-to-all-done.6
  454.5 8.4 fusion.22
  470.5 32.3 %all-to-all-done.7 = bf16[8,144,1792]{2,1,0:T(8,128)(2,1)} async-done(((bf16[8,144,1792]{2,1,0:T(8,128)(2,1)}), bf16[8,144,1792]{2,1,0:T(8,128)(2,1)}, u32[]{:S(2)}, u32[]{:S(2)}) %all-to-all-start.7) | async-done | bytes 4128800 | tf_op jit(solution)/shard_map/all_to_all | solution.py:324
  502.9 8.9 %reshape.236 = bf16[8,144,2,896]{3,2,1,0:T(2,128)(2,1)} reshape(bf16[8,144,1792]{2,1,0:T(8,128)(2,1)} %all-to-all-done.7) | data formatting | bytes 8257536 | tf_op jit(solution)/shard_map/reshape | solution.py:390
  511.8 6.4 copy.119
  518.2 8.0 reshape.237
  526.3 8.9 %convolution_convert_fusion.1 = bf16[2048,1152]{1,0:T(8,128)(2,1)} fusion(bf16[2048,768]{1,0:T(8,128)(2,1)} %bitcast.123, bf16[1152,768]{1,0:T(8,128)(2,1)} %bitcast.9), kind=kOutput, calls=%fused_computation.8 | convolution fusion | flops 3626237952 | bytes 9633792 | tf_op jit(solution)/shard_map/dot_general | solution.py:316
  535.2 26.4 %last.1 = (bf16[8,32,1152]{2,1,0:T(8,128)(2,1)}, f32[1,1152]{1,0:T(1,128)}) custom-call(bf16[8,8,32,1152]{3,2,1,0:T(8,128)(2,1)} %bitcast.114, bf16[8,32,1152]{2,1,0:T(8,128)(2,1)} %bitcast.102, f32[8,32,1152]{2,1,0:T(8,128)} %get-tuple-element.28.refs_2_, f32[1,1152]{1,0:T(1,128)} %reshape.199.refs_1_.refs_3_), custom_call_target="tpu_custom_call" | custom-call | tf_op jit(solution)/shard_map/last/pallas_call | solution.py:216
  563.0 61.5 %all_to_all.41 = bf16[4,128,1152]{2,1,0:T(8,128)(2,1)} all-to-all(bf16[4,128,1152]{2,1,0:T(8,128)(2,1)S(1)} %bitcast.119), channel_id=1, replica_groups=mesh['seq'=4,'fsdp'=8] {'seq'}, dimensions={0} | all-to-all | bytes 2359296 | tf_op jit(solution)/shard_map/all_to_all | solution.py:324
  628.1 58.0 %psum.35 = f32[4,1152]{1,0:T(4,128)S(1)} all-reduce(f32[4,1152]{1,0:T(4,128)S(1)} %pad_maximum_fusion.7), channel_id=1, replica_groups=mesh['seq'=4,'fsdp'=8] {'seq','fsdp'}, use_global_device_ids=true, to_apply=%region_3.4 | all-reduce | flops 4608 | bytes 36864 | tf_op jit(solution)/shard_map/psum | solution.py:420
  688.8 131.1 %all-reduce.5.cloned.1.call-done = (bf16[144,4096]{1,0:T(8,128)(2,1)}, bf16[256,1152]{1,0:T(8,128)(2,1)}, bf16[144,13824]{1,0:T(8,128)(2,1)}, bf16[864,1152]{1,0:T(8,128)(2,1)}) async-done(((bf16[144,4096]{1,0:T(8,128)(2,1)}, bf16[256,1152]{1,0:T(8,128)(2,1)}, bf16[144,13824]{1,0:T(8,128)(2,1)}, bf16[864,1152]{1,0:T(8,128)(2,1)}), (bf16[144,4096]{1,0:T(8,128)(2,1)}, bf16[256,1152]{1,0:T(8,128)(2,1)}, ...) | async-done | bytes 7741456 | tf_op jit(solution)/shard_map/psum | solution.py:412
  819.9 6.3 convert_element_type.114
  (121 shorter events, 88.5 us)
Async XLA Ops:
  7.2 146.0 %copy-start = (bf16[256,1152]{1,0:T(8,128)(2,1)S(1)}, bf16[256,1152]{1,0:T(8,128)(2,1)}, u32[]{:S(2)}) copy-start(bf16[256,1152]{1,0:T(8,128)(2,1)} %param.13) | copy-start | bytes 1769476
  30.6 33.1 %all-to-all-start.1 = ((bf16[4,128,1152]{2,1,0:T(8,128)(2,1)}), bf16[4,128,1152]{2,1,0:T(8,128)(2,1)S(1)}, u32[]{:S(2)}, u32[]{:S(2)}) async-start(bf16[4,128,1152]{2,1,0:T(8,128)(2,1)} %bitcast.117), calls=%async_computation.1 | async-start | bytes 2359296 | tf_op jit(solution)/shard_map/all_to_all | solution.py:324
  45.6 22.6 %copy-start.16 = (f32[1152]{0:T(1024)S(1)}, f32[1152]{0:T(1024)}, u32[]{:S(2)}) copy-start(f32[1152]{0:T(1024)} %param.11) | copy-start | bytes 13828
  45.6 23.2 %copy-start.17 = (f32[1152]{0:T(1024)S(1)}, f32[1152]{0:T(1024)}, u32[]{:S(2)}) copy-start(f32[1152]{0:T(1024)} %param.14) | copy-start | bytes 13828
  45.6 23.8 %copy-start.18 = (f32[1152]{0:T(1024)S(1)}, f32[1152]{0:T(1024)}, u32[]{:S(2)}) copy-start(f32[1152]{0:T(1024)} %param.15) | copy-start | bytes 13828
  63.7 66.7 %all-to-all-start.2 = ((bf16[8,144,768]{2,1,0:T(8,128)(2,1)}), bf16[8,144,768]{2,1,0:T(8,128)(2,1)}, u32[]{:S(2)}, u32[]{:S(2)}) async-start(bf16[8,144,768]{2,1,0:T(8,128)(2,1)} %copy.86), calls=%async_computation.2 | async-start | bytes 3538944 | tf_op jit(solution)/shard_map/all_to_all | solution.py:324
  90.1 10.0 %copy-start.19 = (f32[1152]{0:T(1024)S(1)}, f32[1152]{0:T(1024)}, u32[]{:S(2)}) copy-start(f32[1152]{0:T(1024)} %param.18) | copy-start | bytes 13828
  130.4 98.3 %all-to-all-start.3 = ((bf16[8,144,1792]{2,1,0:T(8,128)(2,1)}), bf16[8,144,1792]{2,1,0:T(8,128)(2,1)}, u32[]{:S(2)}, u32[]{:S(2)}) async-start(bf16[8,144,1792]{2,1,0:T(8,128)(2,1)} %reshape.216), calls=%async_computation.3 | async-start | bytes 8257536 | tf_op jit(solution)/shard_map/all_to_all | solution.py:324
  143.5 2.8 copy-start.8
  143.5 5.5 copy-start.12
  146.2 3.3 copy-start.3
  242.4 5.6 copy-start.2
  242.4 5.6 copy-start.24
  248.0 7.3 copy-start.5
  320.8 16.2 %copy-start.25 = (bf16[2048,896]{0,1:T(8,128)(2,1)}, bf16[2048,896]{0,1:T(8,128)(2,1)S(1)}, u32[]{:S(2)}) copy-start(bf16[2048,896]{0,1:T(8,128)(2,1)S(1)} %get-tuple-element.42) | copy-start | bytes 11010052
  320.8 16.2 %copy-start.26 = (bf16[2048,896]{0,1:T(8,128)(2,1)}, bf16[2048,896]{0,1:T(8,128)(2,1)S(1)}, u32[]{:S(2)}) copy-start(bf16[2048,896]{0,1:T(8,128)(2,1)S(1)} %get-tuple-element.43) | copy-start | bytes 11010052
  389.9 4.4 copy-start.13
  389.9 14.4 %slice-start = ((s8[8388608]{0:T(1024)(128)(4,1)}), s8[4194304]{0:T(1024)(128)(4,1)S(1)}, s32[]{:S(2)}) async-start(s8[8388608]{0:T(1024)(128)(4,1)} %bitcast.103), calls=%async_computation.9 | async-start | bytes 8388608
  394.4 7.3 copy-start.11
  394.4 9.9 %slice-start.1 = ((s8[8388608]{0:T(1024)(128)(4,1)}), s8[4194304]{0:T(1024)(128)(4,1)S(1)}, s32[]{:S(2)}) async-start(s8[8388608]{0:T(1024)(128)(4,1)} %bitcast.103), calls=%async_computation.10 | async-start | bytes 8388608
  422.9 27.0 %all-to-all-start.6 = ((bf16[8,144,768]{2,1,0:T(8,128)(2,1)}), bf16[8,144,768]{2,1,0:T(8,128)(2,1)S(1)}, u32[]{:S(2)}, u32[]{:S(2)}) async-start(bf16[8,144,768]{2,1,0:T(8,128)(2,1)} %bitcast.128), calls=%async_computation.6 | async-start | bytes 3538944 | tf_op jit(solution)/shard_map/all_to_all | solution.py:324
  449.9 53.0 %all-to-all-start.7 = ((bf16[8,144,1792]{2,1,0:T(8,128)(2,1)}), bf16[8,144,1792]{2,1,0:T(8,128)(2,1)}, u32[]{:S(2)}, u32[]{:S(2)}) async-start(bf16[8,144,1792]{2,1,0:T(8,128)(2,1)} %bitcast.121), calls=%async_computation.7 | async-start | bytes 8257536 | tf_op jit(solution)/shard_map/all_to_all | solution.py:324
  454.5 365.4 %all-reduce.5.cloned.1.call-start = ((), (), s32[]{:S(2)}) async-start(), calls=%async_computation.8 | async-start | bytes 15482880 | tf_op jit(solution)/shard_map/psum | solution.py:412
  535.2 26.4 %copy-start.15 = (bf16[8,32,1152]{2,1,0:T(8,128)(2,1)S(1)}, bf16[8,32,1152]{2,1,0:T(8,128)(2,1)}, u32[]{:S(2)}) copy-start(bf16[8,32,1152]{2,1,0:T(8,128)(2,1)} %get-tuple-element.24) | copy-start | bytes 1769476
  561.6 66.5 %copy-start.20 = (f32[1,1152]{1,0:T(1,128)S(1)}, f32[1,1152]{1,0:T(1,128)}, u32[]{:S(2)}) copy-start(f32[1,1152]{1,0:T(1,128)} %get-tuple-element.33) | copy-start | bytes 13828
  561.6 66.5 %copy-start.21 = (f32[1,1152]{1,0:T(1,128)S(1)}, f32[1,1152]{1,0:T(1,128)}, u32[]{:S(2)}) copy-start(f32[1,1152]{1,0:T(1,128)} %get-tuple-element.32) | copy-start | bytes 13828
  561.6 66.5 %copy-start.22 = (f32[1,1152]{1,0:T(1,128)S(1)}, f32[1,1152]{1,0:T(1,128)}, u32[]{:S(2)}) copy-start(f32[1,1152]{1,0:T(1,128)} %get-tuple-element.31) | copy-start | bytes 13828
  561.6 66.5 %copy-start.23 = (f32[1,1152]{1,0:T(1,128)S(1)}, f32[1,1152]{1,0:T(1,128)}, u32[]{:S(2)}) copy-start(f32[1,1152]{1,0:T(1,128)} %get-tuple-element.30) | copy-start | bytes 13828
  624.5 62.3 %all-to-all-start.5 = ((bf16[8,2,32,1152]{3,2,1,0:T(8,128)(2,1)}), bf16[8,2,32,1152]{3,2,1,0:T(8,128)(2,1)S(1)}, u32[]{:S(2)}, u32[]{:S(2)}) async-start(bf16[8,2,32,1152]{3,2,1,0:T(8,128)(2,1)} %bitcast.32), calls=%async_computation.5 | async-start | bytes 2359296 | tf_op jit(solution)/shard_map/all_to_all | solution.py:324
  819.9 6.3 copy-start.6
  826.2 5.0 copy-start.1
  826.2 3.9 copy-start.14
  (4 other events, 7.7 us)
Sparse Core Ops, SparseCore 0:
  526.4 293.4 all-reduce.4

commit v2 on v1

--- a/solution.py
+++ b/solution.py
@@ -46,177 +46,373 @@
     return (activated, derivative)
 
 
-def plane_kernel(reduce, gather, n_in, n_own, body, *refs):
-    refs = list(refs)
-    part = refs.pop(0) if reduce else None
-    ins = [refs.pop(0) for _ in range(n_in)]
-    full = refs.pop(0) if gather else None
-    outs = [refs.pop(0) for _ in range(n_own)]
-    if reduce:
-        acc, other, ra, rb, rx, ry = (refs.pop(0) for _ in range(6))
-    block = refs.pop(0) if gather else None
-    lsem, ssem, rsem = refs
-    rows = ins[0].shape[0]
-    half = rows // 2
-    halves = (pl.ds(0, half), pl.ds(half, half))
-
-    me = lax.axis_index("fsdp")
-    core, xpos, ypos = me % 2, (me // 2) % 2, me // 4
-    step = 1 - 2 * core
-    mate = me + step
-    xn = me + 2 - 4 * xpos
-    yn = me + 4 - 8 * ypos
-    diag = xn + 4 - 8 * ypos
-
-    counter = [0]
-    waits = []
-
-    def send(src, dst, to):
-        k = counter[0]
-        counter[0] += 1
+class Place:
+    def __init__(self, nf, ns):
+        self.nf, self.ns = nf, ns
+        self.me, self.z = lax.axis_index("fsdp"), lax.axis_index("seq")
+        core, xpos, ypos = self.me % 2, (self.me // 2) % 2, self.me // 4
+        self.step = 1 - 2 * core
+        self.mate = self.me + self.step
+        self.xn = self.me + 2 - 4 * xpos
+        self.yn = self.me + 4 - 8 * ypos
+        self.diag = self.xn + 4 - 8 * ypos
+
+    def plane_peers(self):
+        return [(self.me + d) % self.nf for d in range(1, self.nf)]
+
+    def line_peers(self):
+        return [(self.z + d) % self.ns for d in range(1, self.ns)]
+
+    def greet(self, near, plane, line):
+        barrier = pltpu.get_barrier_semaphore()
+        to = [{"fsdp": p} for p in (self.plane_peers() if plane else (self.mate, self.xn, self.yn) if near else ())]
+        to += [{"seq": p} for p in (self.line_peers() if line else ())]
+        for device in to:
+            pl.semaphore_signal(barrier, inc=1, device_id=device, device_id_type=MESH)
+        pl.semaphore_wait(barrier, len(to))
+
+
+class Wire:
+    def __init__(self, lsem, ssem, rsem):
+        self.lsem, self.ssem, self.rsem = lsem, ssem, rsem
+        self.sent, self.kept = [], []
+
+    def send(self, src, dst, device):
+        k = len(self.sent)
         copy = pltpu.make_async_remote_copy(
-            src_ref=src, dst_ref=dst, send_sem=ssem.at[k], recv_sem=rsem.at[k],
-            device_id={"fsdp": to}, device_id_type=MESH,
+            src_ref=src, dst_ref=dst, send_sem=self.ssem.at[k], recv_sem=self.rsem.at[k],
+            device_id=device, device_id_type=MESH,
         )
         copy.start()
-        waits.append(copy)
+        self.sent.append(copy)
         return copy
 
-    locals_ = []
-
-    def local(src, dst):
-        copy = pltpu.make_async_copy(src, dst, lsem.at[len(locals_)])
+    def near(self, src, dst, to):
+        return self.send(src, dst, {"fsdp": to})
+
+    def keep(self, src, dst):
+        copy = pltpu.make_async_copy(src, dst, self.lsem.at[len(self.kept)])
         copy.start()
-        locals_.append(copy)
+        self.kept.append(copy)
         return copy
 
-    if reduce:
-        order = (diag, xn, yn, me)
-        own = [local(part.at[:, b], acc.at[k]) for k, b in enumerate(order)]
-
-    barrier = pltpu.get_barrier_semaphore()
-    for to in (mate, xn, yn):
-        pl.semaphore_signal(barrier, inc=1, device_id={"fsdp": to}, device_id_type=MESH)
-    pl.semaphore_wait(barrier, 3)
-
-    if reduce:
-        mates = [send(part.at[:, b + step], other.at[k], mate) for k, b in enumerate(order)]
-
-        def add(dst, src, lo, count):
-            def one(i, _):
-                dst[lo + i] = (dst[lo + i].astype(F32) + src[i].astype(F32)).astype(BF16)
-                return 0
-
-            lax.fori_loop(0, count, one, 0)
-
-        def join(k):
-            own[k].wait()
-            mates[k].wait_recv()
-            add(acc.at[k], other.at[k], 0, rows)
-
-        join(0)
-        ca = send(acc.at[0, halves[0]], ra, yn)
-        cb = send(acc.at[0, halves[1]], rb, xn)
-        join(1)
-        cx1 = send(acc.at[1, halves[1]], rx.at[halves[1]], xn)
-        join(2)
-        cy0 = send(acc.at[2, halves[0]], ry.at[halves[0]], yn)
-        ca.wait_recv()
-        add(acc.at[1], ra, 0, half)
-        cx0 = send(acc.at[1, halves[0]], rx.at[halves[0]], xn)
-        cb.wait_recv()
-        add(acc.at[2], rb, half, half)
-        cy1 = send(acc.at[2, halves[1]], ry.at[halves[1]], yn)
-        own[3].wait()
-        mates[3].wait_recv()
-        for copy in (cx1, cy0, cx0, cy1):
+    def flush(self):
+        for copy in self.sent:
+            copy.wait_send()
+
+
+def each(count, f):
+    def one(i, _):
+        f(i)
+        return 0
+
+    lax.fori_loop(0, count, one, 0)
+
+
+def halves_of(rows):
+    return pl.ds(0, rows // 2), pl.ds(rows // 2, rows // 2)
+
+
+def reduce_start(at, wire, part, acc, other):
+    order = (at.diag, at.xn, at.yn, at.me)
+    return [wire.keep(part.at[:, b], acc.at[k]) for k, b in enumerate(order)]
+
+
+def reduce_in_plane(at, wire, own, part, acc, other, ra, rb, rx, ry):
+    rows = acc.shape[1]
+    half = rows // 2
+    h0, h1 = halves_of(rows)
+    order = (at.diag, at.xn, at.yn, at.me)
+    mates = [wire.near(part.at[:, b + at.step], other.at[k], at.mate) for k, b in enumerate(order)]
+    yield
+
+    def add(dst, src, lo, count):
+        def one(i):
+            dst[lo + i] = (dst[lo + i].astype(F32) + src[i].astype(F32)).astype(BF16)
+
+        each(count, one)
+
+    def join(k):
+        own[k].wait()
+        mates[k].wait_recv()
+        add(acc.at[k], other.at[k], 0, rows)
+
+    join(0)
+    ca = wire.near(acc.at[0, h0], ra, at.yn)
+    cb = wire.near(acc.at[0, h1], rb, at.xn)
+    yield
+    join(1)
+    cx1 = wire.near(acc.at[1, h1], rx.at[h1], at.xn)
+    join(2)
+    cy0 = wire.near(acc.at[2, h0], ry.at[h0], at.yn)
+    yield
+    ca.wait_recv()
+    add(acc.at[1], ra, 0, half)
+    cx0 = wire.near(acc.at[1, h0], rx.at[h0], at.xn)
+    cb.wait_recv()
+    add(acc.at[2], rb, half, half)
+    cy1 = wire.near(acc.at[2, h1], ry.at[h1], at.yn)
+    own[3].wait()
+    mates[3].wait_recv()
+    yield
+    cx1.wait_recv()
+    cy0.wait_recv()
+    yield
+    cx0.wait_recv()
+    cy1.wait_recv()
+
+
+def gather_in_plane(at, wire, block, full):
+    h0, h1 = halves_of(block.shape[0])
+    me, xn, yn, diag, mate = at.me, at.xn, at.yn, at.diag, at.mate
+    keep = wire.keep(block, full.at[:, me])
+
+    def pass_on(copy, where, blk, to):
+        copy.wait_recv()
+        return wire.near(full.at[where, blk], full.at[where, blk], to)
+
+    y0 = wire.near(block.at[h0], full.at[h0, me], yn)
+    x1 = wire.near(block.at[h1], full.at[h1, me], xn)
+    y1 = wire.near(block.at[h1], full.at[h1, me], yn)
+    x0 = wire.near(block.at[h0], full.at[h0, me], xn)
+    last = [wire.near(block, full.at[:, me], mate)]
+    yield
+    gx = pass_on(y0, h0, yn, xn)
+    last.append(wire.near(full.at[h0, yn], full.at[h0, yn], mate))
+    gy = pass_on(x1, h1, xn, yn)
+    last.append(wire.near(full.at[h1, xn], full.at[h1, xn], mate))
+    yield
+    last.append(pass_on(y1, h1, yn, mate))
+    last.append(pass_on(x0, h0, xn, mate))
+    yield
+    last.append(pass_on(gx, h0, diag, mate))
+    last.append(pass_on(gy, h1, diag, mate))
+    yield
+    for copy in last:
+        copy.wait_recv()
+    keep.wait()
+
+
+def weave(main, others=(), counts=()):
+    others, counts = list(others), list(counts)
+    for _ in main:
+        for _ in range(counts.pop(0) if counts else 0):
+            if others:
+                others.pop(0)()
+    for other in others:
+        other()
+
+
+class LineSum:
+    def __init__(self, at, items, sems):
+        self.z, self.items, self.sems = at.z, items, sems
+        self.outer = at.z % 3 == 0
+        self.inner = at.z % 3 != 0
+        self.pair = at.z + 1 - 2 * (at.z % 2)
+        self.across = 3 - at.z
+
+    def copy(self, stage, k):
+        own, in1, in2, out = self.items[k]
+        src, dst, to = ((own, in1, self.pair), (in1, in2, self.across), (in2, out, self.pair))[stage]
+        send, recv = self.sems[2 * stage], self.sems[2 * stage + 1]
+        return pltpu.make_async_remote_copy(
+            src_ref=src, dst_ref=dst, send_sem=send.at[k], recv_sem=recv.at[k],
+            device_id={"seq": to}, device_id_type=MESH,
+        )
+
+    def kept(self, k):
+        return pltpu.make_async_copy(self.items[k][2], self.items[k][3], self.sems[6].at[k])
+
+    @staticmethod
+    def add(dst, src):
+        def one(i):
+            where = pl.ds(pl.multiple_of(i * 16, 16), 16)
+            dst[where] = (dst[where].astype(F32) + src[where].astype(F32)).astype(BF16)
+
+        each(dst.shape[0] // 16, one)
+
+    def launch(self, k):
+        @pl.when(self.outer)
+        def _():
+            self.copy(0, k).start()
+
+    def first(self, k):
+        @pl.when(self.inner)
+        def _():
+            self.copy(0, k).wait_recv()
+            self.add(self.items[k][1], self.items[k][0])
+            self.copy(1, k).start()
+
+    def second(self, k):
+        @pl.when(self.inner)
+        def _():
+            self.copy(1, k).wait_recv()
+            self.add(self.items[k][2], self.items[k][1])
+            self.copy(2, k).start()
+            self.kept(k).start()
+
+    def steps(self):
+        n = len(self.items)
+        out = []
+        for k in range(n + 1):
+            if k < n:
+                out.append(functools.partial(self.first, k))
+            if k > 0:
+                out.append(functools.partial(self.second, k - 1))
+        return out
+
+    def end(self):
+        for k in range(len(self.items)):
+
+            @pl.when(self.outer)
+            def _():
+                self.copy(0, k).wait_send()
+                self.copy(2, k).wait_recv()
+
+            @pl.when(self.inner)
+            def _():
+                self.copy(1, k).wait_send()
+                self.copy(2, k).wait_send()
+                self.kept(k).wait()
+
+    @staticmethod
+    def semaphores(n):
+        return [pltpu.SemaphoreType.DMA((n,))] * 7
+
+
+def enter_kernel(nf, ns, tok, grad, gain, full, x_own, g_own, xs, gs, xo, go, block, lsem, ssem, rsem):
+    at, wire = Place(nf, ns), Wire(lsem, ssem, rsem)
+    keeps = [wire.keep(tok.at[at.me], xs.at[at.me]), wire.keep(grad.at[at.me], gs.at[at.me])]
+    at.greet(True, True, True)
+    first = [
+        [wire.near(src.at[p], dst.at[at.me], p) for p in at.plane_peers()]
+        for src, dst in ((tok, xs), (grad, gs))
+    ]
+    spp = nf // ns
+    second, own = [], []
+    for k, (src, dst) in enumerate(((xs, xo), (gs, go))):
+        keeps[k].wait()
+        for copy in first[k]:
             copy.wait_recv()
-
+        second.append(
+            [
+                wire.send(src.at[pl.ds(p * spp, spp)], dst.at[:, at.z], {"seq": p})
+                for p in at.line_peers()
+            ]
+        )
+        own.append(wire.keep(src.at[pl.ds(at.z * spp, spp)], dst.at[:, at.z]))
+    own[0].wait()
+    for copy in second[0]:
+        copy.wait_recv()
+    outs = [wire.keep(xo, x_own)]
+
+    def one(i):
+        values = xo[i // ns, i % ns].astype(F32)
+        block[i] = (values * inverse_rms(values) * gain[...]).astype(BF16)
+
+    each(nf, one)
+    weave(gather_in_plane(at, wire, block, full))
+    own[1].wait()
+    for copy in second[1]:
+        copy.wait_recv()
+    outs.append(wire.keep(go, g_own))
+    for copy in outs:
+        copy.wait()
+    wire.flush()
+
+
+def enter(nf, ns, tokens, grads, gain):
+    _, r, width = tokens.shape
+    spp = nf // ns
+    own = jax.ShapeDtypeStruct((spp, ns, r, width), BF16)
+    anys = pl.BlockSpec(memory_space=pl.ANY)
+    n_send = 2 * (nf - 1) + 2 * (ns - 1) + 13
+    return pl.pallas_call(
+        functools.partial(enter_kernel, nf, ns),
+        name="enter",
+        out_shape=[jax.ShapeDtypeStruct((nf, nf, r, width), BF16), own, own],
+        in_specs=[anys, anys, pl.BlockSpec(memory_space=pltpu.VMEM)],
+        out_specs=[anys, anys, anys],
+        scratch_shapes=[pltpu.VMEM((nf, r, width), BF16)] * 2
+        + [pltpu.VMEM((spp, ns, r, width), BF16)] * 2
+        + [pltpu.VMEM((nf, r, width), BF16)]
+        + [pltpu.SemaphoreType.DMA((8,))]
+        + [pltpu.SemaphoreType.DMA((n_send,))] * 2,
+        compiler_params=pltpu.CompilerParams(collective_id=1, has_side_effects=True),
+    )(tokens, grads, gain)
+
+
+def middle_kernel(nf, ns, n_in, n_own, body, plan, *refs):
+    refs = list(refs)
+    part, ins = refs[0], refs[1 : 1 + n_in]
+    del refs[: 1 + n_in]
+    grad = refs.pop(0) if plan else None
+    full = refs.pop(0)
+    outs = [refs.pop(0) for _ in range(n_own)]
+    summed = refs.pop(0) if plan else None
+    acc, other, ra, rb, rx, ry, block, lsem, ssem, rsem = refs[:10]
+    at, wire = Place(nf, ns), Wire(lsem, ssem, rsem)
+    own = reduce_start(at, wire, part, acc, other)
+    at.greet(True, False, plan)
+    line, steps = None, ()
+    if plan:
+        in1, in2 = refs[10:12]
+        line = LineSum(at, [(grad.at[k], in1.at[k], in2.at[k], summed.at[k]) for k in range(grad.shape[0])], refs[12:])
+
+    def main():
+        yield from reduce_in_plane(at, wire, own, part, acc, other, ra, rb, rx, ry)
+        work_on_sum(body, acc, other, rx, ry, ins, outs, block)
+        yield from gather_in_plane(at, wire, block, full)
+
+    if plan:
+        for k in range(len(line.items)):
+            line.launch(k)
+        weave(main(), line.steps(), plan)
+        line.end()
+    else:
+        weave(main())
+    wire.flush()
+
+
+def work_on_sum(body, acc, other, rx, ry, ins, outs, block):
     def one(i, sums):
-        if reduce:
-            total = (
-                acc[3, i].astype(F32) + other[3, i].astype(F32)
-            ) + (rx[i].astype(F32) + ry[i].astype(F32))
-        else:
-            total = None
-        sent, extra = body(i, total, ins, outs)
-        if gather:
-            block[i] = sent
-        if extra is None:
-            return sums
+        total = (acc[3, i].astype(F32) + other[3, i].astype(F32)) + (
+            rx[i].astype(F32) + ry[i].astype(F32)
+        )
+        block[i], extra = body(i, total, ins, outs)
         return tuple(s + e for s, e in zip(sums, extra))
 
-    width = ins[0].shape[-1]
-    n_sums = body.n_sums
-    sums = lax.fori_loop(0, rows, one, tuple(jnp.zeros((1, width), F32) for _ in range(n_sums)))
-    for s, ref in zip(sums, outs[n_own - n_sums :]):
+    rows, _, width = block.shape
+    zero = tuple(jnp.zeros((1, width), F32) for _ in range(body.n_sums))
+    sums = lax.fori_loop(0, rows, one, zero)
+    for s, ref in zip(sums, outs[len(outs) - body.n_sums :]):
         ref[...] = s
 
-    if gather:
-        keep = local(block, full.at[:, me])
-        h0, h1 = halves
-
-        def forward(copy, where, blk, to):
-            copy.wait_recv()
-            return send(full.at[where, blk], full.at[where, blk], to)
-
-        y0 = send(block.at[h0], full.at[h0, me], yn)
-        x1 = send(block.at[h1], full.at[h1, me], xn)
-        y1 = send(block.at[h1], full.at[h1, me], yn)
-        x0 = send(block.at[h0], full.at[h0, me], xn)
-        m = send(block, full.at[:, me], mate)
-        gx = forward(y0, h0, yn, xn)
-        fy0 = send(full.at[h0, yn], full.at[h0, yn], mate)
-        gy = forward(x1, h1, xn, yn)
-        fx1 = send(full.at[h1, xn], full.at[h1, xn], mate)
-        forward(y1, h1, yn, mate)
-        forward(x0, h0, xn, mate)
-        forward(gx, h0, diag, mate)
-        forward(gy, h1, diag, mate)
-        for copy in (m, fy0, fx1):
-            copy.wait_recv()
-        for copy in waits[-4:]:
-            copy.wait_recv()
-        keep.wait()
-    for copy in waits:
-        copy.wait_send()
-
-
-def plane_call(name, cid, body, part, ins, own_types, gather, planes, width):
-    reduce = part is not None
-    rows, r = ins[0].shape[0], ins[0].shape[1]
-    shape = (rows, r, width)
-    out_shape, out_specs = [], []
-    if gather:
-        out_shape.append(jax.ShapeDtypeStruct((rows, planes, r, width), BF16))
-        out_specs.append(pl.BlockSpec(memory_space=pl.ANY))
-    for t in own_types:
-        out_shape.append(jax.ShapeDtypeStruct(shape, t))
-        out_specs.append(pl.BlockSpec(memory_space=pltpu.VMEM))
-    for _ in range(body.n_sums):
-        out_shape.append(jax.ShapeDtypeStruct((1, width), F32))
-        out_specs.append(pl.BlockSpec(memory_space=pltpu.VMEM))
-    scratch = []
-    if reduce:
-        hs = (rows // 2, r, width)
-        scratch += [pltpu.VMEM((4,) + shape, BF16)] * 2 + [pltpu.VMEM(hs, BF16)] * 2
-        scratch += [pltpu.VMEM(shape, BF16)] * 2
-    if gather:
-        scratch.append(pltpu.VMEM(shape, BF16))
-    n_send = (10 if reduce else 0) + (13 if gather else 0)
-    scratch += [
-        pltpu.SemaphoreType.DMA((5,)),
-        pltpu.SemaphoreType.DMA((n_send,)),
-        pltpu.SemaphoreType.DMA((n_send,)),
-    ]
-    operands = ([part] if reduce else []) + list(ins)
-    in_specs = ([pl.BlockSpec(memory_space=pl.ANY)] if reduce else []) + [
-        pl.BlockSpec(memory_space=pltpu.VMEM)
-    ] * len(ins)
+
+def sum_scratch(rows, r, width):
+    shape, half = (rows, r, width), (rows // 2, r, width)
+    return [pltpu.VMEM((4,) + shape, BF16)] * 2 + [pltpu.VMEM(half, BF16)] * 2 + [pltpu.VMEM(shape, BF16)] * 3
+
+
+def middle(name, cid, nf, ns, body, part, ins, own_types, grad=None, plan=None):
+    rows, _, r, width = part.shape
+    vmem, anys = pl.BlockSpec(memory_space=pltpu.VMEM), pl.BlockSpec(memory_space=pl.ANY)
+    out_shape = [jax.ShapeDtypeStruct(part.shape, BF16)]
+    out_shape += [jax.ShapeDtypeStruct((rows, r, width), t) for t in own_types]
+    out_shape += [jax.ShapeDtypeStruct((1, width), F32)] * body.n_sums
+    n_own = len(out_shape) - 1
+    in_specs, out_specs = [anys] + [vmem] * len(ins), [anys] + [vmem] * n_own
+    scratch = sum_scratch(rows, r, width)
+    scratch += [pltpu.SemaphoreType.DMA((5,))] + [pltpu.SemaphoreType.DMA((23,))] * 2
+    operands = [part, *ins]
+    if plan:
+        operands.append(grad)
+        in_specs.append(vmem)
+        out_shape.append(jax.ShapeDtypeStruct(grad.shape, BF16))
+        out_specs.append(anys)
+        scratch += [pltpu.VMEM(grad.shape, BF16)] * 2 + LineSum.semaphores(grad.shape[0])
     return pl.pallas_call(
-        functools.partial(
-            plane_kernel, reduce, gather, len(ins), len(own_types) + body.n_sums, body
-        ),
+        functools.partial(middle_kernel, nf, ns, len(ins), n_own, body, plan),
         name=name,
         out_shape=out_shape,
         in_specs=in_specs,
@@ -226,19 +422,237 @@
     )(*operands)
 
 
+def leave_kernel(nf, ns, body, *refs):
+    part, tokens, hid_grad, gain, done, terms, gu, qkv, wout = refs[:9]
+    lay_out, tok_out, gain_out, gu_out, qkv_out, wout_out = refs[9:15]
+    (acc, other, ra, rb, rx, ry, block, dz, bz, gl, gt, gp, gz, gu_in, gu1, gu2,
+     qkv_in, qkv_own, qkv1, qkv2, w1, w2) = refs[15:37]
+    lsem, ssem, rsem = refs[37:40]
+    zsems = refs[40:]
+    at, wire = Place(nf, ns), Wire(lsem, ssem, rsem)
+    spp = nf // ns
+    own = reduce_start(at, wire, part, acc, other)
+    own_dz = wire.keep(done.at[:, at.z], dz.at[pl.ds(at.z * spp, spp)])
+    own_gu = wire.keep(gu.at[at.me], gu_in.at[at.me])
+    own_qkv = wire.keep(qkv.at[at.me], qkv_in.at[at.me])
+    at.greet(True, True, True)
+
+    half = gu_in.shape[2] // 2
+    order = (at.me, at.mate, at.xn, at.yn, at.xn + at.step, at.yn + at.step, at.diag, at.diag + at.step)
+    items = [(wout.at[k], w1.at[k], w2.at[k], wout_out.at[k]) for k in range(wout.shape[0])]
+    n_out = len(items)
+    for p in order:
+        for h in range(2):
+            where = (p, slice(None), pl.ds(h * half, half))
+            items.append(tuple(ref.at[where] for ref in (gu_in, gu1, gu2, gu_out)))
+    for c in range(qkv_own.shape[0]):
+        items.append(tuple(ref.at[c] for ref in (qkv_own, qkv1, qkv2, qkv_out)))
+    line = LineSum(at, items, zsems)
+    for k in range(n_out):
+        line.launch(k)
+
+    main = reduce_in_plane(at, wire, own, part, acc, other, ra, rb, rx, ry)
+    next(main)
+    gu_moves = {1: wire.near(gu.at[at.mate], gu_in.at[at.me], at.mate)}
+    for j in range(2, nf):
+        gu_moves[j] = wire.near(gu.at[order[j]], gu_in.at[at.me], order[j])
+    qkv_moves = [wire.near(qkv.at[p], qkv_in.at[at.me], p) for p in at.plane_peers()]
+    lay = [
+        wire.send(done.at[:, p], dz.at[pl.ds(at.z * spp, spp)], {"seq": p}) for p in at.line_peers()
+    ]
+
+    def arrive(j):
+        if j == 0:
+            own_gu.wait()
+        else:
+            gu_moves[j].wait_recv()
+        line.launch(n_out + 2 * j)
+        line.launch(n_out + 2 * j + 1)
+
+    def arrive_qkv():
+        own_qkv.wait()
+        for copy in qkv_moves:
+            copy.wait_recv()
+        group = nf // qkv_own.shape[0]
+        hd = HD
+
+        def one(i):
+            where = pl.ds(pl.multiple_of(i * 16, 16), 16)
+            for c in range(qkv_own.shape[0]):
+                both = jnp.zeros((16, 2 * hd), F32)
+                for g in range(group):
+                    piece = qkv_in[c * group + g, where]
+                    qkv_own[c, where, g * hd : (g + 1) * hd] = piece[:, :hd]
+                    both = both + piece[:, hd:].astype(F32)
+                qkv_own[c, where, group * hd :] = both.astype(BF16)
+
+        each(qkv_own.shape[1] // 16, one)
+        for c in range(qkv_own.shape[0]):
+            line.launch(n_out + 2 * nf + c)
+
+    def rest():
+        yield from main
+        gl[...] = terms[...]
+        work_on_sum(body, acc, other, rx, ry, (tokens, hid_grad, gain), (gl.at[pl.ds(0, 1)],), block)
+        line2, own_bz = [], []
+        for s in range(spp):
+            own_bz.append(wire.keep(block.at[s * ns + at.z], bz.at[at.z * spp + s]))
+            line2 += [
+                wire.send(block.at[s * ns + p], bz.at[at.z * spp + s], {"seq": p})
+                for p in at.line_peers()
+            ]
+        gp[at.me] = gl[...]
+        small = [wire.near(gl, gp.at[at.me], p) for p in at.plane_peers()]
+        yield
+
+        def to_homes(src, out, arrived):
+            for copy in arrived:
+                copy.wait_recv()
+            home = wire.keep(src.at[at.me], out.at[at.me])
+            return home, [wire.near(src.at[p], out.at[at.me], p) for p in at.plane_peers()]
+
+        own_dz.wait()
+        home1, away1 = to_homes(dz, lay_out, lay)
+        yield
+        for copy in small:
+            copy.wait_recv()
+        total = gp[0]
+        for k in range(1, nf):
+            total = total + gp[k]
+        gt[...] = total
+        gz[at.z] = total
+        small2 = [wire.send(gt, gz.at[at.z], {"seq": p}) for p in at.line_peers()]
+        yield
+        for copy in own_bz:
+            copy.wait()
+        home2, away2 = to_homes(bz, tok_out, line2)
+        yield
+        for copy in small2:
+            copy.wait_recv()
+        total = gz[0]
+        for k in range(1, ns):
+            total = total + gz[k]
+        gain_out[...] = total
+        for copy in away1 + away2:
+            copy.wait_recv()
+        home1.wait()
+        home2.wait()
+        yield
+
+    work = [lambda: arrive(0), lambda: arrive(1)]
+    steps = line.steps()
+    slow = rest()
+    ready = {4: 2, 7: 3, 10: 4, 13: 5, 16: 6, 19: 7, 22: None}
+    for f in work:
+        f()
+    for i, step in enumerate(steps):
+        step()
+        if i in ready:
+            arrive_qkv() if ready[i] is None else arrive(ready[i])
+        if i % 2 == 1:
+            next(slow, None)
+    for _ in slow:
+        pass
+    line.end()
+    wire.flush()
+
+
+def leave(nf, ns, body, part, tokens, hid_grad, gain, done, terms, gu, qkv, wout):
+    rows, _, r, width = part.shape
+    spp = nf // ns
+    depth = gu.shape[1]
+    vmem, anys = pl.BlockSpec(memory_space=pltpu.VMEM), pl.BlockSpec(memory_space=pl.ANY)
+    home = jax.ShapeDtypeStruct((nf, r, width), BF16)
+    n_send = 10 + (ns - 1) * (1 + spp) + (nf - 1) + (ns - 1) + 2 * (nf - 1) + 2 * (nf - 1)
+    heads = (KV, depth, (H // KV + 2) * HD)
+    n_items = wout.shape[0] + 2 * nf + KV
+    return pl.pallas_call(
+        functools.partial(leave_kernel, nf, ns, body),
+        name="leave",
+        out_shape=[home, home, jax.ShapeDtypeStruct((8, width), F32)]
+        + [jax.ShapeDtypeStruct(s, BF16) for s in (gu.shape, heads, wout.shape)],
+        in_specs=[anys, vmem, vmem, vmem, anys, vmem, anys, anys, vmem],
+        out_specs=[anys, anys, vmem, anys, anys, anys],
+        scratch_shapes=sum_scratch(rows, r, width)
+        + [pltpu.VMEM((nf, r, width), BF16)] * 2
+        + [pltpu.VMEM((8, width), F32)] * 2
+        + [pltpu.VMEM((nf, 8, width), F32), pltpu.VMEM((ns, 8, width), F32)]
+        + [pltpu.VMEM(gu.shape, BF16)] * 3
+        + [pltpu.VMEM(qkv.shape, BF16)]
+        + [pltpu.VMEM(heads, BF16)] * 3
+        + [pltpu.VMEM(wout.shape, BF16)] * 2
+        + [pltpu.SemaphoreType.DMA((5 + spp + 4,))]
+        + [pltpu.SemaphoreType.DMA((n_send,))] * 2
+        + LineSum.semaphores(n_items),
+        compiler_params=pltpu.CompilerParams(collective_id=5, has_side_effects=True),
+    )(part, tokens, hid_grad, gain, done, terms, gu, qkv, wout)
+
+
+def split_columns(weight, nf, ff, ffp):
+    depth = weight.shape[0]
+    step = 16
+
+    def kernel(w, out):
+        for f in range(nf):
+            for g in range(2):
+                piece = w[:, (g * nf + f) * ff : (g * nf + f + 1) * ff]
+                if ffp > ff:
+                    piece = jnp.concatenate([piece, jnp.zeros((step, ffp - ff), piece.dtype)], axis=1)
+                out[f, :, g * ffp : (g + 1) * ffp] = piece
+
+    return pl.pallas_call(
+        kernel,
+        name="split_columns",
+        grid=(depth // step,),
+        out_shape=jax.ShapeDtypeStruct((nf, depth, 2 * ffp), weight.dtype),
+        in_specs=[pl.BlockSpec((step, 2 * nf * ff), lambda i: (i, 0))],
+        out_specs=pl.BlockSpec((nf, step, 2 * ffp), lambda i: (0, i, 0)),
+    )(weight)
+
+
+def join_columns(parts, heads, nf, ff):
+    _, depth, columns = parts.shape
+    n_kv, _, wide = heads.shape
+    queries = wide - 2 * HD
+    step = 16
+
+    def kernel(x, h, out, out_h):
+        for g in range(2):
+            lo = g * columns // 2
+            pieces = [x[f, :, lo : lo + ff].astype(F32) for f in range(nf)]
+            out[:, g * nf * ff : (g + 1) * nf * ff] = jnp.concatenate(pieces, axis=1)
+        for c in range(n_kv):
+            piece = h[c].astype(F32)
+            out_h[:, c * queries : (c + 1) * queries] = piece[:, :queries]
+            for j in range(2):
+                lo = n_kv * queries + (j * n_kv + c) * HD
+                out_h[:, lo : lo + HD] = piece[:, queries + j * HD : queries + (j + 1) * HD]
+
+    return pl.pallas_call(
+        kernel,
+        name="join_columns",
+        grid=(depth // step,),
+        out_shape=[
+            jax.ShapeDtypeStruct((depth, 2 * nf * ff), F32),
+            jax.ShapeDtypeStruct((depth, n_kv * wide), F32),
+        ],
+        in_specs=[
+            pl.BlockSpec((nf, step, columns), lambda i: (0, i, 0)),
+            pl.BlockSpec((n_kv, step, wide), lambda i: (0, i, 0)),
+        ],
+        out_specs=[
+            pl.BlockSpec((step, 2 * nf * ff), lambda i: (i, 0)),
+            pl.BlockSpec((step, n_kv * wide), lambda i: (i, 0)),
+        ],
+    )(parts, heads)
+
+
 def with_sums(n):
     def mark(f):
         f.n_sums = n
         return f
 
     return mark
-
-
-@with_sums(0)
-def body_first(i, _, ins, outs):
-    tokens, gain = ins
-    values = tokens[i].astype(F32)
-    return (values * inverse_rms(values) * gain[...]).astype(BF16), None
 
 
 @with_sums(0)
@@ -248,7 +662,7 @@
     hidden = tokens[i].astype(F32) + branch * inverse_rms(branch) * gain_attn[...]
     branch_out[i] = branch
     hidden_out[i] = hidden
-    return (hidden * inverse_rms(hidden) * gain_ffn[...]).astype(BF16), None
+    return (hidden * inverse_rms(hidden) * gain_ffn[...]).astype(BF16), ()
 
 
 @with_sums(1)
@@ -276,8 +690,7 @@
     tokens, hidden_grad, gain = ins
     values = tokens[i].astype(F32)
     part, term = norm_back(delta, values, inverse_rms(values), gain[...])
-    outs[0][i] = (hidden_grad[i] + part).astype(BF16)
-    return None, (term,)
+    return (hidden_grad[i] + part).astype(BF16), (term,)
 
 
 def scores(q, k):
@@ -339,97 +752,77 @@
     ffp = -(-ff // LANES) * LANES
     depth = qkv_weight.shape[0]
 
-    both = jnp.stack([tokens[0], out_grad[0]])
-    both = both.reshape(2, nf, r, width).transpose(1, 0, 2, 3)
-    both = swap(both, "fsdp")
-    both = swap(both.reshape(ns, spp * 2 * r, width), "seq")
-    both = both.reshape(ns, spp, 2, r, width)
-    x_own = both[:, :, 0].transpose(1, 0, 2, 3).reshape(rows, r, width)
-    g_own = both[:, :, 1].transpose(1, 0, 2, 3).reshape(rows, r, width)
-
     q_cols = qkv_weight[:, : H * HD].reshape(depth, H, HD)
     k_cols = jnp.repeat(qkv_weight[:, H * HD : (H + KV) * HD].reshape(depth, KV, HD), group, axis=1)
     v_cols = jnp.repeat(qkv_weight[:, (H + KV) * HD :].reshape(depth, KV, HD), group, axis=1)
     w_qkv = jnp.concatenate([q_cols, k_cols, v_cols], axis=2).transpose(1, 0, 2)
     w_qkv = swap(w_qkv, "fsdp").reshape(nf * depth, 3 * HD)
-    w_gu = jnp.pad(gate_up_weight.reshape(depth, 2, nf, ff), ((0, 0), (0, 0), (0, 0), (0, ffp - ff)))
-    w_gu = swap(w_gu.transpose(2, 0, 1, 3).reshape(nf, depth, 2 * ffp), "fsdp")
+    w_gu = swap(split_columns(gate_up_weight, nf, ff, ffp), "fsdp")
     w_gu = w_gu.reshape(nf * depth, 2 * ffp)
     w_down = jnp.pad(down_weight, ((0, ffp - ff), (0, 0)))
 
     gains = [g.reshape(1, width) for g in (pre_attn_gain, post_attn_gain, pre_ffn_gain, post_ffn_gain)]
     flat = (rows * nf * r, width)
-    terms = (rows, nf, r, width)
-
-    a_full, = plane_call("gather_a", 1, body_first, None, [x_own, gains[0]], [], True, nf, width)
+    shape = (rows, nf, r, width)
+
+    a_full, x_own, g_own = enter(
+        nf, ns, tokens.reshape(nf, r, width), out_grad.reshape(nf, r, width), gains[0]
+    )
+    x_own, g_own = x_own.reshape(rows, r, width), g_own.reshape(rows, r, width)
     a_full = a_full.reshape(flat)
     qkv = dot_f32(a_full, w_qkv).astype(BF16)
     q, k, v = (qkv[:, i * HD : (i + 1) * HD].reshape(spp, length, HD) for i in range(3))
     o, lse = attend(q, k, v)
     o_flat = o.reshape(-1, HD)
-    y1_terms = dot_f32(o_flat, out_weight).astype(BF16).reshape(terms)
-    n_full, y1, hidden = plane_call(
-        "mid", 2, body_mid, y1_terms, [x_own, gains[1], gains[2]], [F32, F32], True, nf, width
+    y1_terms = dot_f32(o_flat, out_weight).astype(BF16).reshape(shape)
+    n_full, y1, hidden = middle(
+        "mid", 2, nf, ns, body_mid, y1_terms, [x_own, gains[1], gains[2]], [F32, F32]
     )
     n_full = n_full.reshape(flat)
     gu = dot_f32(n_full, w_gu)
     gate, up = gu[:, :ffp], gu[:, ffp:]
     activated, derivative = gelu_pair(gate)
     mixed = (activated * up).astype(BF16)
-    y2_terms = dot_f32(mixed, w_down).astype(BF16).reshape(terms)
-    dy2_full, out_own, post_ffn_term = plane_call(
-        "turn", 3, body_turn, y2_terms, [hidden, g_own, gains[3]], [BF16], True, nf, width
+    y2_terms = dot_f32(mixed, w_down).astype(BF16).reshape(shape)
+    dy2_full, out_own, post_ffn_term = middle(
+        "turn", 3, nf, ns, body_turn, y2_terms, [hidden, g_own, gains[3]], [BF16]
     )
     dy2_full = dy2_full.reshape(flat)
     down_wg = dot_tn(mixed, dy2_full)[:ff].astype(BF16)
-    down_wg = lax.psum(down_wg, "seq")
     dm = dot_nt(dy2_full, w_down)
     dgu = jnp.concatenate([dm * up * derivative, dm * activated], axis=1).astype(BF16)
-    dn_terms = dot_nt(dgu, w_gu).astype(BF16).reshape(terms)
+    dn_terms = dot_nt(dgu, w_gu).astype(BF16).reshape(shape)
     gu_wg = dot_tn(n_full, dgu).astype(BF16).reshape(nf, depth, 2 * ffp)
-    gu_wg = swap(gu_wg, "fsdp").reshape(nf, depth, 2, ffp)[..., :ff]
-    gu_wg = lax.psum(gu_wg.transpose(1, 2, 0, 3).reshape(depth, 2 * nf * ff), "seq")
-    dy1_full, hidden_grad, pre_ffn_term, post_attn_term = plane_call(
-        "back", 4, body_back, dn_terms, [hidden, y1, g_own, gains[1], gains[2]], [F32], True, nf, width
+    pieces = next(n for n in (9, 6, 3, 2, 1) if ff % (16 * n) == 0)
+    dy1_full, hidden_grad, pre_ffn_term, post_attn_term, down_wg = middle(
+        "back", 4, nf, ns, body_back, dn_terms, [hidden, y1, g_own, gains[1], gains[2]], [F32],
+        down_wg.reshape(pieces, ff // pieces, width), (0, 0, 1, 2, 4, 4, 2, 2, 2),
     )
     dy1_full = dy1_full.reshape(flat)
     do = dot_nt(dy1_full, out_weight).astype(BF16).reshape(o.shape)
     out_wg = dot_tn(o_flat, dy1_full).astype(BF16)
     dq, dk, dv = attend_back(q, k, v, o, do, lse)
     dqkv = jnp.concatenate([dq, dk, dv], axis=2).reshape(-1, 3 * HD)
-    da_terms = dot_nt(dqkv, w_qkv).astype(BF16).reshape(terms)
+    da_terms = dot_nt(dqkv, w_qkv).astype(BF16).reshape(shape)
     qkv_wg = dot_tn(a_full, dqkv).astype(BF16).reshape(nf, depth, 3 * HD)
-    qkv_wg = swap(qkv_wg, "fsdp").transpose(1, 0, 2)
-    kv_wg = qkv_wg[:, :, HD:].astype(F32).reshape(depth, KV, group, 2 * HD).sum(axis=2).astype(BF16)
-    qkv_wg = jnp.concatenate(
-        [
-            qkv_wg[:, :, :HD].reshape(depth, H * HD),
-            kv_wg[:, :, :HD].reshape(depth, KV * HD),
-            kv_wg[:, :, HD:].reshape(depth, KV * HD),
-        ],
-        axis=1,
-    )
-    out_wg, qkv_wg = lax.psum((out_wg, qkv_wg), "seq")
-    tg_own, pre_attn_term = plane_call(
-        "last", 5, body_last, da_terms, [x_own, hidden_grad, gains[0]], [BF16], False, nf, width
-    )
-    back = jnp.stack([out_own, tg_own], axis=2)
-    back = jnp.stack([out_own, tg_own]).reshape(2, spp, ns, r, width).transpose(2, 1, 0, 3, 4)
-    back = swap(back.reshape(ns, spp * 2 * r, width), "seq").reshape(nf, 2, r, width)
-    back = swap(back, "fsdp").transpose(1, 0, 2, 3).reshape(2, 1, chunk, width)
-    gain_sums = lax.psum(
-        jnp.concatenate([pre_attn_term, post_attn_term, pre_ffn_term, post_ffn_term]), ("seq", "fsdp")
-    )
+    terms = jnp.concatenate(
+        [jnp.zeros((1, width), F32), post_attn_term, pre_ffn_term, post_ffn_term, jnp.zeros((4, width), F32)]
+    )
+    layer_out, tokens_grad, gain_sums, gu_wg, qkv_wg, out_wg = leave(
+        nf, ns, body_last, da_terms, x_own, hidden_grad, gains[0],
+        out_own.reshape(spp, ns, r, width), terms, gu_wg, qkv_wg, out_wg.reshape(2, HD // 2, width),
+    )
+    gu_wg, qkv_wg = join_columns(gu_wg, qkv_wg, nf, ff)
     return (
-        back[0],
-        back[1].astype(F32),
+        layer_out.reshape(1, chunk, width),
+        tokens_grad.astype(F32).reshape(1, chunk, width),
         gain_sums[0],
-        qkv_wg.astype(F32),
-        out_wg.astype(F32),
+        qkv_wg,
+        out_wg.reshape(HD, width).astype(F32),
         gain_sums[1],
         gain_sums[2],
-        gu_wg.astype(F32),
-        down_wg.astype(F32),
+        gu_wg,
+        down_wg.reshape(ff, width).astype(F32),
         gain_sums[3],
     )
 
@@ -696,7 +1089,7 @@
     )
 
     def on_device(*args):
-        if nf == 8 and nf == H and nf % ns == 0 and args[0].shape[0] == 1:
+        if nf == 8 and nf == H and nf % ns == 0 and ns == 4 and args[0].shape[0] == 1:
             return on_device_plane(ns, nf, *args)
         return gathered_on_device(*args)
 

time: 844 us -> 656 us (0.78)
  Pallas kernels: 229 us -> 479 us
  waiting for transfers between devices: 188 us -> 0.01 us
  blocking collectives: 141 us -> 0 us
  local copies, waits for them, and re-layouts: 81.6 us -> 20.7 us
  starting transfers between devices: 26.4 us -> 9.77 us
  between operations: 14.9 us -> 1.69 us
  matrix products: 132 us -> 121 us
  other arithmetic: 25.1 us -> 14.6 us
    pallas_call x5 -> x7, Pallas kernels: 229 us -> 479 us  [the longest x1 209 us: leave(): pl.pallas_call(functools.partial(leave_kernel, nf, ns, body), name='leave...]
    psum x1 -> x0, waiting for transfers between devices: 131 us -> none  [on_device_plane(): out_wg, qkv_wg = lax.psum((out_wg, qkv_wg), 'seq')]
    all_to_all x2 -> x0, blocking collectives: 83.4 us -> none  [swap(): return lax.all_to_all(x, axis, split_axis=0, concat_axis=0, tiled=True)]
    psum x1 -> x0, blocking collectives: 58 us -> none  [on_device_plane(): lax.psum(jnp.concatenate([pre_attn_term, post_attn_term, pre_ffn_term, po...]
    all_to_all x6 -> x2, waiting for transfers between devices: 56.7 us -> 0.01 us  [swap(): return lax.all_to_all(x, axis, split_axis=0, concat_axis=0, tiled=True)]
    reshape x8 -> x0, local copies, waits for them, and re-layouts: 41.3 us -> none  [the longest x2 14.3 us: on_device_plane(): gate_up_weight.reshape(depth, 2, nf, ff)]
    all_to_all x6 -> x2, starting transfers between devices: 26.3 us -> 9.77 us  [swap(): return lax.all_to_all(x, axis, split_axis=0, concat_axis=0, tiled=True)]
    dot_general x4, matrix products: 44.1 us -> 35.5 us  [dot_nt(): lax.dot_general(a, b, (((1,), (1,)), ((), ())), preferred_element_type=F32)]
  transfers between devices with their start and end apart: 7 -> 2, of which waited for: 4 -> 0; matrix products, arithmetic and copies ran while one was open for 13% -> 3% of each run, Pallas kernels for 15% -> 21%
where the time goes in v2:
time: 656 us; the launch traced here: 647 us
  Pallas kernels  479 us (73%)
  matrix products  121 us (18%)
  local copies, waits for them, and re-layouts  20.7 us (3%)
  other arithmetic  14.6 us (2%)
  starting transfers between devices  9.77 us (1%)
    pallas_call x1, Pallas kernels, leave(): pl.pallas_call(functools.partial(leave_kernel, nf, ns, body), name='leave...  209 us
    pallas_call x3, Pallas kernels, middle(): pl.pallas_call(functools.partial(middle_kernel, nf, ns, len(ins), n_own,...  197 us
    pallas_call x1, Pallas kernels, enter(): pl.pallas_call(functools.partial(enter_kernel, nf, ns), name='enter', out...  56.8 us
    dot_general x4, matrix products, dot_tn(): lax.dot_general(a, b, (((0,), (0,)), ((), ())), preferred_element_type=F32)  36.5 us
    dot_general x4, matrix products, dot_nt(): lax.dot_general(a, b, (((1,), (1,)), ((), ())), preferred_element_type=F32)  35.5 us
    dot_general x4, matrix products, dot_f32(): return jnp.dot(a, b, preferred_element_type=F32)  31.5 us
  transfers between devices with their start and end apart: 2, of which 0 were waited for; matrix products, arithmetic and copies ran while one was open for 3% of the time, Pallas kernels for 21%

profile of v2, /device:TPU:0, one launch (start us, length us, event | category | flops | bytes accessed | tf_op | source)
XLA Modules:
  0.0 646.7 jit_solution(15527638060034041959)
XLA Ops:
  5.4 5.2 all-to-all-start
  12.4 7.7 %split_columns.1 = bf16[8,144,1792]{2,1,0:T(8,128)(2,1)} custom-call(bf16[144,13824]{1,0:T(8,128)(2,1)} %w.1), custom_call_target="tpu_custom_call" | custom-call | tf_op jit(solution)/shard_map/split_columns/pallas_call | solution.py:603
  20.7 56.8 %enter.1 = (bf16[8,8,32,1152]{3,2,1,0:T(8,128)(2,1)}, bf16[2,4,32,1152]{3,2,1,0:T(8,128)(2,1)}, bf16[2,4,32,1152]{3,2,1,0:T(8,128)(2,1)}) custom-call(bf16[8,32,1152]{2,1,0:T(8,128)(2,1)} %bitcast.105, bf16[8,32,1152]{2,1,0:T(8,128)(2,1)} %bitcast.106, f32[1,1152]{1,0:T(1,128)} %reshape.161.gain.refs_3_), custom_call_target="tpu_custom_call" | custom-call | tf_op jit(solution)/shard_map/enter/pallas_call | solution.py:330
  77.9 4.6 all-to-all-start.1
  82.5 7.0 %convolution_convert_fusion.5 = bf16[2048,768]{1,0:T(8,128)(2,1)S(1)} fusion(bf16[2048,1152]{1,0:T(8,128)(2,1)} %bitcast.108, bf16[1152,768]{1,0:T(8,128)(2,1)S(1)} %bitcast.90), kind=kOutput, calls=%fused_computation.27 | convolution fusion | flops 3625451520 | bytes 9633792 | tf_op jit(solution)/shard_map/dot_general | solution.py:725
  89.7 2.4 fusion.8
  92.1 2.7 exponential_reduce_fusion
  95.4 3.7 convolution_convert_fusion.12
  99.1 3.7 convolution_convert_fusion.3
  102.8 73.0 %mid.1 = (bf16[8,8,32,1152]{3,2,1,0:T(8,128)(2,1)}, f32[8,32,1152]{2,1,0:T(8,128)}, f32[8,32,1152]{2,1,0:T(8,128)}) custom-call(bf16[8,8,32,1152]{3,2,1,0:T(8,128)(2,1)} %bitcast.70, bf16[8,32,1152]{2,1,0:T(8,128)(2,1)} %bitcast.84, f32[1,1152]{1,0:T(1,128)} %reshape.175.refs_2_.refs_4_, f32[1,1152]{1,0:T(1,128)} %reshape.176.refs_3_.refs_5_), custom_call_target="tpu_custom_call" | custom-call | tf_op jit(solution)/shard_map/mid/pallas_call | solution.py:414
  175.9 13.5 %fusion.20 = f32[2048,1792]{0,1:T(8,128)S(1)} fusion(bf16[2048,1152]{1,0:T(8,128)(2,1)} %bitcast.110, bf16[1152,1792]{1,0:T(8,128)(2,1)} %bitcast.12), kind=kOutput, calls=%fused_computation.55 | convolution fusion | flops 8455716864 | bytes 23527424 | tf_op jit(solution)/shard_map/dot_general | solution.py:725
  189.4 2.6 multiply_convert_fusion.2
  192.0 3.0 copy-done.1
  195.0 7.3 %convolution_convert_fusion = bf16[2048,1152]{1,0:T(8,128)(2,1)} fusion(bf16[2048,896]{0,1:T(8,128)(2,1)S(1)} %multiply_convert_fusion.2, bf16[864,1152]{1,0:T(8,128)(2,1)S(1)} %copy-done.28), kind=kOutput, calls=%fused_computation.7 | convolution fusion | flops 4230217728 | bytes 10379264 | tf_op jit(solution)/shard_map/dot_general | solution.py:725
  202.3 51.1 %turn.1 = (bf16[8,8,32,1152]{3,2,1,0:T(8,128)(2,1)}, bf16[8,32,1152]{2,1,0:T(8,128)(2,1)}, f32[1,1152]{1,0:T(1,128)}) custom-call(bf16[8,8,32,1152]{3,2,1,0:T(8,128)(2,1)} %bitcast.80, f32[8,32,1152]{2,1,0:T(8,128)} %get-tuple-element.35.refs_1_, bf16[8,32,1152]{2,1,0:T(8,128)(2,1)} %bitcast.86, f32[1,1152]{1,0:T(1,128)} %reshape.181.refs_3_), custom_call_target="tpu_custom_call" | custom-call | tf_op jit(solution)/shard_map/turn/pallas_call | solution.py:414
  253.4 9.8 %fusion.21 = bf16[896,1152]{1,0:T(8,128)(2,1)} fusion(bf16[2048,896]{0,1:T(8,128)(2,1)} %copy-done.7, bf16[2048,1152]{1,0:T(8,128)(2,1)} %bitcast.114), kind=kOutput, calls=%fused_computation.56 | convolution fusion | flops 4227858432 | bytes 10452992 | tf_op jit(solution)/shard_map/dot_general | solution.py:733
  263.2 12.8 %fusion.7 = (bf16[2048,896]{0,1:T(8,128)(2,1)}, bf16[2048,896]{0,1:T(8,128)(2,1)}) fusion(f32[2048,1792]{0,1:T(8,128)S(1)} %bitcast.72, bf16[2048,1152]{1,0:T(8,128)(2,1)} %bitcast.115, bf16[864,1152]{1,0:T(8,128)(2,1)S(1)} %copy-done.29), kind=kOutput, calls=%fused_computation.19 | convolution fusion | flops 4270063616 | bytes 28729344 | tf_op jit(solution)/shard_map/dot_general | solution.py:729
  276.0 14.9 %convolution_convert_fusion.2 = bf16[2048,1152]{1,0:T(8,128)(2,1)} fusion(bf16[1152,1792]{1,0:T(8,128)(2,1)} %bitcast.12, bf16[2048,896]{0,1:T(8,128)(2,1)} %get-tuple-element.59, bf16[2048,896]{0,1:T(8,128)(2,1)} %get-tuple-element.58), kind=kOutput, calls=%fused_computation.9 | convolution fusion | flops 8472756224 | bytes 16187392 | tf_op jit(solution)/shard_map/dot_general | solution.py:729
  291.0 13.3 %convolution_convert_fusion.4 = bf16[1152,1792]{1,0:T(8,128)(2,1)} fusion(bf16[2048,1152]{1,0:T(8,128)(2,1)} %bitcast.111, bf16[2048,896]{0,1:T(8,128)(2,1)S(1)} %copy-done.31, bf16[2048,896]{0,1:T(8,128)(2,1)S(1)} %copy-done.30), kind=kOutput, calls=%fused_computation.11 | convolution fusion | flops 8472461312 | bytes 16187392 | tf_op jit(solution)/shard_map/dot_general | solution.py:733
  305.8 73.1 %back.1 = (bf16[8,8,32,1152]{3,2,1,0:T(8,128)(2,1)}, f32[8,32,1152]{2,1,0:T(8,128)}, f32[1,1152]{1,0:T(1,128)}, f32[1,1152]{1,0:T(1,128)}, bf16[9,96,1152]{2,1,0:T(8,128)(2,1)}) custom-call(bf16[8,8,32,1152]{3,2,1,0:T(8,128)(2,1)} %bitcast.78, f32[8,32,1152]{2,1,0:T(8,128)} %get-tuple-element.35.refs_1_, f32[8,32,1152]{2,1,0:T(8,128)} %get-tuple-element.38.refs_2_, ...), custom_call_target="tpu_custom_call" | custom-call | tf_op jit(solution)/shard_map/back/pallas_call | solution.py:414
  378.9 4.9 convolution_convert_fusion.8
  386.6 4.7 multiply_convert_fusion
  393.9 3.6 convolution_convert_fusion.9
  397.5 1.8 pad_maximum_fusion.3
  399.4 4.6 copy.58
  404.0 8.6 %convolution_convert_fusion.6 = bf16[1152,768]{1,0:T(8,128)(2,1)} fusion(bf16[2048,1152]{1,0:T(8,128)(2,1)} %bitcast.109, bf16[2048,768]{1,0:T(8,128)(2,1)} %bitcast.82), kind=kOutput, calls=%fused_computation.28 | convolution fusion | flops 3624763392 | bytes 9633792 | tf_op jit(solution)/shard_map/dot_general | solution.py:733
  412.6 6.2 convolution_convert_fusion.1
  419.4 208.6 %leave.1 = (bf16[8,32,1152]{2,1,0:T(8,128)(2,1)}, bf16[8,32,1152]{2,1,0:T(8,128)(2,1)}, f32[8,1152]{1,0:T(8,128)}, bf16[8,144,1792]{2,1,0:T(8,128)(2,1)}, bf16[4...) custom-call(bf16[8,8,32,1152]{3,2,1,0:T(8,128)(2,1)} %bitcast.79, bf16[8,32,1152]{2,1,0:T(8,128)(2,1)} %bitcast.85, ...), custom_call_target="tpu_custom_call" | custom-call | tf_op jit(solution)/shard_map/leave/pallas_call | solution.py:569
  628.1 2.3 bitcast_convert_fusion.1
  630.4 2.2 bitcast_convert_fusion.2
  634.2 2.3 bitcast_convert_fusion
  636.5 9.0 %join_columns.1 = (f32[144,13824]{1,0:T(8,128)}, f32[144,4096]{1,0:T(8,128)}) custom-call(bf16[8,144,1792]{2,1,0:T(8,128)(2,1)} %get-tuple-element.48.x, bf16[4,144,1024]{2,1,0:T(8,128)(2,1)} %get-tuple-element.49.h), custom_call_target="tpu_custom_call" | custom-call | tf_op jit(solution)/shard_map/join_columns/pallas_call | solution.py:631
  (108 shorter events, 18.1 us)
Async XLA Ops:
  0.6 98.5 %copy-start = (bf16[256,1152]{1,0:T(8,128)(2,1)S(1)}, bf16[256,1152]{1,0:T(8,128)(2,1)}, u32[]{:S(2)}) copy-start(bf16[256,1152]{1,0:T(8,128)(2,1)} %param.13) | copy-start | bytes 1769476
  3.7 6.9 %copy-start.20 = (f32[1152]{0:T(1024)S(1)}, f32[1152]{0:T(1024)}, u32[]{:S(2)}) copy-start(f32[1152]{0:T(1024)} %param.11) | copy-start | bytes 13828
  3.7 7.5 %copy-start.21 = (f32[1152]{0:T(1024)S(1)}, f32[1152]{0:T(1024)}, u32[]{:S(2)}) copy-start(f32[1152]{0:T(1024)} %param.14) | copy-start | bytes 13828
  3.7 8.1 %copy-start.22 = (f32[1152]{0:T(1024)S(1)}, f32[1152]{0:T(1024)}, u32[]{:S(2)}) copy-start(f32[1152]{0:T(1024)} %param.15) | copy-start | bytes 13828
  5.4 72.5 %all-to-all-start = ((bf16[8,144,768]{2,1,0:T(8,128)(2,1)}), bf16[8,144,768]{2,1,0:T(8,128)(2,1)S(1)}, u32[]{:S(2)}, u32[]{:S(2)}) async-start(bf16[8,144,768]{2,1,0:T(8,128)(2,1)} %copy.49), calls=%async_computation | async-start | bytes 3538944 | tf_op jit(solution)/shard_map/all_to_all | solution.py:737
  10.6 9.5 %copy-start.23 = (f32[1152]{0:T(1024)S(1)}, f32[1152]{0:T(1024)}, u32[]{:S(2)}) copy-start(f32[1152]{0:T(1024)} %param.18) | copy-start | bytes 13828
  77.8 17.0 %copy-start.5 = (pred[1024,1024]{0,1:T(8,128)(4,1)}, pred[1024,1024]{0,1:T(8,128)(4,1)S(1)}, u32[]{:S(2)}) copy-start(pred[1024,1024]{0,1:T(8,128)(4,1)S(1)} %iota_compare_fusion) | copy-start | bytes 3145732
  77.9 11.6 %copy-start.11 = (bf16[8,144,768]{2,1,0:T(8,128)(2,1)}, bf16[8,144,768]{2,1,0:T(8,128)(2,1)S(1)}, u32[]{:S(2)}) copy-start(bf16[8,144,768]{2,1,0:T(8,128)(2,1)S(1)} %all-to-all-done) | copy-start | bytes 5308420
  77.9 98.0 %all-to-all-start.1 = ((bf16[8,144,1792]{2,1,0:T(8,128)(2,1)}), bf16[8,144,1792]{2,1,0:T(8,128)(2,1)}, u32[]{:S(2)}, u32[]{:S(2)}) async-start(bf16[8,144,1792]{2,1,0:T(8,128)(2,1)} %split_columns.1), calls=%async_computation.1 | async-start | bytes 8257536 | tf_op jit(solution)/shard_map/all_to_all | solution.py:737
  89.7 5.2 copy-start.17
  189.4 5.6 copy-start.1
  189.4 5.6 copy-start.28
  195.0 7.3 %copy-start.7 = (bf16[2048,896]{0,1:T(8,128)(2,1)}, bf16[2048,896]{0,1:T(8,128)(2,1)S(1)}, u32[]{:S(2)}) copy-start(bf16[2048,896]{0,1:T(8,128)(2,1)S(1)} %multiply_convert_fusion.2) | copy-start | bytes 11010052
  202.3 60.9 %slice-start = ((s8[14680064]{0:T(1024)(128)(4,1)}), s8[2097152]{0:T(1024)(128)(4,1)S(1)}, s32[]{:S(2)}) async-start(s8[14680064]{0:T(1024)(128)(4,1)} %bitcast.71), calls=%async_computation.2 | async-start | bytes 4194304
  253.4 9.8 %slice-start.1 = ((s8[14680064]{0:T(1024)(128)(4,1)}), s8[4194304]{0:T(1024)(128)(4,1)S(1)}, s32[]{:S(2)}) async-start(s8[14680064]{0:T(1024)(128)(4,1)} %bitcast.71), calls=%async_computation.3 | async-start | bytes 8388608
  253.4 9.8 %slice-start.2 = ((s8[14680064]{0:T(1024)(128)(4,1)}), s8[4194304]{0:T(1024)(128)(4,1)S(1)}, s32[]{:S(2)}) async-start(s8[14680064]{0:T(1024)(128)(4,1)} %bitcast.71), calls=%async_computation.4 | async-start | bytes 8388608
  253.4 9.8 %slice-start.3 = ((s8[14680064]{0:T(1024)(128)(4,1)}), s8[4194304]{0:T(1024)(128)(4,1)S(1)}, s32[]{:S(2)}) async-start(s8[14680064]{0:T(1024)(128)(4,1)} %bitcast.71), calls=%async_computation.5 | async-start | bytes 8388608
  253.4 9.8 %copy-start.29 = (bf16[864,1152]{1,0:T(8,128)(2,1)S(1)}, bf16[864,1152]{1,0:T(8,128)(2,1)}, u32[]{:S(2)}) copy-start(bf16[864,1152]{1,0:T(8,128)(2,1)} %param.17) | copy-start | bytes 5971972
  276.0 15.0 %copy-start.30 = (bf16[2048,896]{0,1:T(8,128)(2,1)S(1)}, bf16[2048,896]{0,1:T(8,128)(2,1)}, u32[]{:S(2)}) copy-start(bf16[2048,896]{0,1:T(8,128)(2,1)} %get-tuple-element.58) | copy-start | bytes 11010052
  276.0 15.0 %copy-start.31 = (bf16[2048,896]{0,1:T(8,128)(2,1)S(1)}, bf16[2048,896]{0,1:T(8,128)(2,1)}, u32[]{:S(2)}) copy-start(bf16[2048,896]{0,1:T(8,128)(2,1)} %get-tuple-element.59) | copy-start | bytes 11010052
  291.0 13.4 %copy-start.10 = (bf16[896,1152]{1,0:T(8,128)(2,1)S(1)}, bf16[896,1152]{1,0:T(8,128)(2,1)}, u32[]{:S(2)}) copy-start(bf16[896,1152]{1,0:T(8,128)(2,1)} %fusion.21) | copy-start | bytes 6193156
  305.8 73.1 %copy-start.4 = (bf16[2,1024,256]{2,1,0:T(8,128)(2,1)S(1)}, bf16[2,1024,256]{2,1,0:T(8,128)(2,1)}, u32[]{:S(2)}) copy-start(bf16[2,1024,256]{2,1,0:T(8,128)(2,1)} %copy-done.3) | copy-start | bytes 3145732
  378.9 4.9 copy-start.27
  378.9 6.9 %slice-start.4 = ((s8[8388608]{0:T(1024)(128)(4,1)}), s8[4194304]{0:T(1024)(128)(4,1)S(1)}, s32[]{:S(2)}) async-start(s8[8388608]{0:T(1024)(128)(4,1)} %bitcast.73), calls=%async_computation.6 | async-start | bytes 8388608
  386.6 4.7 copy-start.16
  404.0 8.6 %copy-start.8 = (bf16[2,1024,768]{2,1,0:T(8,128)(2,1)S(1)}, bf16[2,1024,768]{2,1,0:T(8,128)(2,1)}, u32[]{:S(2)}) copy-start(bf16[2,1024,768]{2,1,0:T(8,128)(2,1)} %copy.58) | copy-start | bytes 9437188
  404.0 8.6 %copy-start.12 = (bf16[8,144,768]{2,1,0:T(8,128)(2,1)S(1)}, bf16[8,144,768]{2,1,0:T(8,128)(2,1)}, u32[]{:S(2)}) copy-start(bf16[8,144,768]{2,1,0:T(8,128)(2,1)} %copy-done.11) | copy-start | bytes 5308420
  412.6 6.2 copy-start.24
  412.6 6.2 copy-start.25
  412.6 6.2 copy-start.26
  628.1 6.1 copy-start.9
  634.2 11.3 %copy-start.19 = (bf16[8,32,1152]{2,1,0:T(8,128)(2,1)S(1)}, bf16[8,32,1152]{2,1,0:T(8,128)(2,1)}, u32[]{:S(2)}) copy-start(bf16[8,32,1152]{2,1,0:T(8,128)(2,1)} %get-tuple-element.45) | copy-start | bytes 1769476
  (9 other events, 23.6 us)

commit v3 on v2

--- a/solution.py
+++ b/solution.py
@@ -261,36 +261,56 @@
                 out.append(functools.partial(self.second, k - 1))
         return out
 
+    def end_one(self, k, seen=False):
+        @pl.when(self.outer)
+        def _():
+            self.copy(0, k).wait_send()
+            if not seen:
+                self.copy(2, k).wait_recv()
+
+        @pl.when(self.inner)
+        def _():
+            self.copy(1, k).wait_send()
+            self.copy(2, k).wait_send()
+            if not seen:
+                self.kept(k).wait()
+
     def end(self):
         for k in range(len(self.items)):
-
-            @pl.when(self.outer)
-            def _():
-                self.copy(0, k).wait_send()
-                self.copy(2, k).wait_recv()
-
-            @pl.when(self.inner)
-            def _():
-                self.copy(1, k).wait_send()
-                self.copy(2, k).wait_send()
-                self.kept(k).wait()
+            self.end_one(k)
 
     @staticmethod
     def semaphores(n):
         return [pltpu.SemaphoreType.DMA((n,))] * 7
 
 
-def enter_kernel(nf, ns, tok, grad, gain, full, x_own, g_own, xs, gs, xo, go, block, lsem, ssem, rsem):
+def enter_kernel(nf, ns, ff, *refs):
+    tok, grad, gain, wqkv, wgu = refs[:5]
+    full, x_own, g_own, heads, sorted_out = refs[5:10]
+    xs, gs, xo, go, block, wide, sorted_, lsem, ssem, rsem = refs[10:]
     at, wire = Place(nf, ns), Wire(lsem, ssem, rsem)
+    spp = nf // ns
+    group = H // KV
     keeps = [wire.keep(tok.at[at.me], xs.at[at.me]), wire.keep(grad.at[at.me], gs.at[at.me])]
+    load = wire.keep(wgu, wide)
+
+    def columns(p):
+        starts = (p * HD, H * HD + (p // group) * HD, (H + KV) * HD + (p // group) * HD)
+        return [
+            (wqkv.at[:, pl.ds(pl.multiple_of(lo, HD), HD)], heads.at[at.me, :, pl.ds(k * HD, HD)])
+            for k, lo in enumerate(starts)
+        ]
+
+    own_heads = [wire.keep(*pair) for pair in columns(at.me)]
     at.greet(True, True, True)
     first = [
         [wire.near(src.at[p], dst.at[at.me], p) for p in at.plane_peers()]
         for src, dst in ((tok, xs), (grad, gs))
     ]
-    spp = nf // ns
+    head_moves = [wire.near(*pair, p) for p in at.plane_peers() for pair in columns(p)]
     second, own = [], []
-    for k, (src, dst) in enumerate(((xs, xo), (gs, go))):
+
+    def stage(k, src, dst):
         keeps[k].wait()
         for copy in first[k]:
             copy.wait_recv()
@@ -301,10 +321,27 @@
             ]
         )
         own.append(wire.keep(src.at[pl.ds(at.z * spp, spp)], dst.at[:, at.z]))
+
+    stage(0, xs, xo)
+    stage(1, gs, go)
+    load.wait()
+    ffp = sorted_.shape[2] // 2
+
+    def sort(i):
+        where = pl.ds(pl.multiple_of(i * 16, 16), 16)
+        for f in range(nf):
+            for g in range(2):
+                piece = wide[where, (g * nf + f) * ff : (g * nf + f + 1) * ff]
+                if ffp > ff:
+                    piece = jnp.concatenate([piece, jnp.zeros((16, ffp - ff), BF16)], axis=1)
+                sorted_[f, where, g * ffp : (g + 1) * ffp] = piece
+
+    each(wide.shape[0] // 16, sort)
+    outs = [wire.keep(sorted_, sorted_out)]
     own[0].wait()
     for copy in second[0]:
         copy.wait_recv()
-    outs = [wire.keep(xo, x_own)]
+    outs.append(wire.keep(xo, x_own))
 
     def one(i):
         values = xo[i // ns, i % ns].astype(F32)
@@ -313,36 +350,61 @@
     each(nf, one)
     weave(gather_in_plane(at, wire, block, full))
     own[1].wait()
-    for copy in second[1]:
+    for copy in second[1] + head_moves:
         copy.wait_recv()
     outs.append(wire.keep(go, g_own))
-    for copy in outs:
+    for copy in outs + own_heads:
         copy.wait()
     wire.flush()
 
 
-def enter(nf, ns, tokens, grads, gain):
+def enter(nf, ns, tokens, grads, gain, wqkv, wgu, ffp):
     _, r, width = tokens.shape
     spp = nf // ns
+    depth = wqkv.shape[0]
     own = jax.ShapeDtypeStruct((spp, ns, r, width), BF16)
     anys = pl.BlockSpec(memory_space=pl.ANY)
-    n_send = 2 * (nf - 1) + 2 * (ns - 1) + 13
+    n_send = 2 * (nf - 1) + 2 * (ns - 1) + 13 + 3 * (nf - 1)
     return pl.pallas_call(
-        functools.partial(enter_kernel, nf, ns),
+        functools.partial(enter_kernel, nf, ns, wgu.shape[1] // (2 * nf)),
         name="enter",
-        out_shape=[jax.ShapeDtypeStruct((nf, nf, r, width), BF16), own, own],
-        in_specs=[anys, anys, pl.BlockSpec(memory_space=pltpu.VMEM)],
-        out_specs=[anys, anys, anys],
+        out_shape=[jax.ShapeDtypeStruct((nf, nf, r, width), BF16), own, own]
+        + [jax.ShapeDtypeStruct((nf, depth, c), BF16) for c in (3 * HD, 2 * ffp)],
+        in_specs=[anys, anys, pl.BlockSpec(memory_space=pltpu.VMEM), anys, anys],
+        out_specs=[anys] * 5,
         scratch_shapes=[pltpu.VMEM((nf, r, width), BF16)] * 2
         + [pltpu.VMEM((spp, ns, r, width), BF16)] * 2
         + [pltpu.VMEM((nf, r, width), BF16)]
-        + [pltpu.SemaphoreType.DMA((8,))]
+        + [pltpu.VMEM(wgu.shape, BF16), pltpu.VMEM((nf, depth, 2 * ffp), BF16)]
+        + [pltpu.SemaphoreType.DMA((12,))]
         + [pltpu.SemaphoreType.DMA((n_send,))] * 2,
         compiler_params=pltpu.CompilerParams(collective_id=1, has_side_effects=True),
-    )(tokens, grads, gain)
-
-
-def middle_kernel(nf, ns, n_in, n_own, body, plan, *refs):
+    )(tokens, grads, gain, wqkv, wgu)
+
+
+def go_home(at, wire, src, buf, out):
+    spp = at.nf // at.ns
+    own, line = [], []
+    for s in range(spp):
+        own.append(wire.keep(src.at[s * at.ns + at.z], buf.at[at.z * spp + s]))
+        line += [
+            wire.send(src.at[s * at.ns + p], buf.at[at.z * spp + s], {"seq": p})
+            for p in at.line_peers()
+        ]
+    yield
+    for copy in own:
+        copy.wait()
+    for copy in line:
+        copy.wait_recv()
+    home = wire.keep(buf.at[at.me], out.at[at.me])
+    away = [wire.near(buf.at[p], out.at[at.me], p) for p in at.plane_peers()]
+    yield
+    home.wait()
+    for copy in away:
+        copy.wait_recv()
+
+
+def middle_kernel(nf, ns, n_in, n_own, body, homing, plan, *refs):
     refs = list(refs)
     part, ins = refs[0], refs[1 : 1 + n_in]
     del refs[: 1 + n_in]
@@ -351,18 +413,25 @@
     outs = [refs.pop(0) for _ in range(n_own)]
     summed = refs.pop(0) if plan else None
     acc, other, ra, rb, rx, ry, block, lsem, ssem, rsem = refs[:10]
+    del refs[:10]
     at, wire = Place(nf, ns), Wire(lsem, ssem, rsem)
     own = reduce_start(at, wire, part, acc, other)
-    at.greet(True, False, plan)
-    line, steps = None, ()
+    at.greet(True, homing, plan or homing)
+    line = None
+    if homing:
+        home, outs[0], buf = outs[0], refs[0], refs[1]
     if plan:
-        in1, in2 = refs[10:12]
-        line = LineSum(at, [(grad.at[k], in1.at[k], in2.at[k], summed.at[k]) for k in range(grad.shape[0])], refs[12:])
+        in1, in2 = refs[:2]
+        line = LineSum(at, [(grad.at[k], in1.at[k], in2.at[k], summed.at[k]) for k in range(grad.shape[0])], refs[2:])
 
     def main():
         yield from reduce_in_plane(at, wire, own, part, acc, other, ra, rb, rx, ry)
         work_on_sum(body, acc, other, rx, ry, ins, outs, block)
+        going = go_home(at, wire, outs[0], buf, home) if homing else iter(())
+        next(going, None)
         yield from gather_in_plane(at, wire, block, full)
+        for _ in going:
+            pass
 
     if plan:
         for k in range(len(line.items)):
@@ -394,7 +463,7 @@
     return [pltpu.VMEM((4,) + shape, BF16)] * 2 + [pltpu.VMEM(half, BF16)] * 2 + [pltpu.VMEM(shape, BF16)] * 3
 
 
-def middle(name, cid, nf, ns, body, part, ins, own_types, grad=None, plan=None):
+def middle(name, cid, nf, ns, body, part, ins, own_types, homing=False, grad=None, plan=None):
     rows, _, r, width = part.shape
     vmem, anys = pl.BlockSpec(memory_space=pltpu.VMEM), pl.BlockSpec(memory_space=pl.ANY)
     out_shape = [jax.ShapeDtypeStruct(part.shape, BF16)]
@@ -402,9 +471,13 @@
     out_shape += [jax.ShapeDtypeStruct((1, width), F32)] * body.n_sums
     n_own = len(out_shape) - 1
     in_specs, out_specs = [anys] + [vmem] * len(ins), [anys] + [vmem] * n_own
+    n_send = 23 + ((ns - 1) * (nf // ns) + nf - 1 if homing else 0)
     scratch = sum_scratch(rows, r, width)
-    scratch += [pltpu.SemaphoreType.DMA((5,))] + [pltpu.SemaphoreType.DMA((23,))] * 2
+    scratch += [pltpu.SemaphoreType.DMA((8,))] + [pltpu.SemaphoreType.DMA((n_send,))] * 2
     operands = [part, *ins]
+    if homing:
+        out_specs[1] = anys
+        scratch += [pltpu.VMEM((nf, r, width), own_types[0])] * 2
     if plan:
         operands.append(grad)
         in_specs.append(vmem)
@@ -412,7 +485,7 @@
         out_specs.append(anys)
         scratch += [pltpu.VMEM(grad.shape, BF16)] * 2 + LineSum.semaphores(grad.shape[0])
     return pl.pallas_call(
-        functools.partial(middle_kernel, nf, ns, len(ins), n_own, body, plan),
+        functools.partial(middle_kernel, nf, ns, len(ins), n_own, body, homing, plan),
         name=name,
         out_shape=out_shape,
         in_specs=in_specs,
@@ -422,97 +495,68 @@
     )(*operands)
 
 
-def leave_kernel(nf, ns, body, *refs):
-    part, tokens, hid_grad, gain, done, terms, gu, qkv, wout = refs[:9]
-    lay_out, tok_out, gain_out, gu_out, qkv_out, wout_out = refs[9:15]
-    (acc, other, ra, rb, rx, ry, block, dz, bz, gl, gt, gp, gz, gu_in, gu1, gu2,
-     qkv_in, qkv_own, qkv1, qkv2, w1, w2) = refs[15:37]
+def leave_kernel(nf, ns, body, rest, *refs):
+    part, tokens, hid_grad, gain, terms, done, todo, qkv, wout = refs[:9]
+    tok_out, gain_out, rows_out, qkv_out, wout_out = refs[9:14]
+    (acc, other, ra, rb, rx, ry, block, bz, gl, gt, gp, gz, held, up_own, up1, up2, up_sum,
+     qkv_in, qkv_own, qkv1, qkv2, w1, w2) = refs[14:37]
     lsem, ssem, rsem = refs[37:40]
     zsems = refs[40:]
     at, wire = Place(nf, ns), Wire(lsem, ssem, rsem)
-    spp = nf // ns
     own = reduce_start(at, wire, part, acc, other)
-    own_dz = wire.keep(done.at[:, at.z], dz.at[pl.ds(at.z * spp, spp)])
-    own_gu = wire.keep(gu.at[at.me], gu_in.at[at.me])
     own_qkv = wire.keep(qkv.at[at.me], qkv_in.at[at.me])
+    order = line_order(at)
+    n_done = nf - rest
+    fetch = [wire.keep(done.at[0], held)]
+    loads = [wire.keep(todo.at[order[n_done + j]], up_own.at[j]) for j in range(rest)]
     at.greet(True, True, True)
 
-    half = gu_in.shape[2] // 2
-    order = (at.me, at.mate, at.xn, at.yn, at.xn + at.step, at.yn + at.step, at.diag, at.diag + at.step)
     items = [(wout.at[k], w1.at[k], w2.at[k], wout_out.at[k]) for k in range(wout.shape[0])]
     n_out = len(items)
-    for p in order:
-        for h in range(2):
-            where = (p, slice(None), pl.ds(h * half, half))
-            items.append(tuple(ref.at[where] for ref in (gu_in, gu1, gu2, gu_out)))
-    for c in range(qkv_own.shape[0]):
-        items.append(tuple(ref.at[c] for ref in (qkv_own, qkv1, qkv2, qkv_out)))
+    items += [tuple(ref.at[j] for ref in (up_own, up1, up2, up_sum)) for j in range(rest)]
+    items += [tuple(ref.at[c] for ref in (qkv_own, qkv1, qkv2, qkv_out)) for c in range(qkv_own.shape[0])]
     line = LineSum(at, items, zsems)
     for k in range(n_out):
         line.launch(k)
+    for j in range(rest):
+        loads[j].wait()
+        line.launch(n_out + j)
 
     main = reduce_in_plane(at, wire, own, part, acc, other, ra, rb, rx, ry)
     next(main)
-    gu_moves = {1: wire.near(gu.at[at.mate], gu_in.at[at.me], at.mate)}
-    for j in range(2, nf):
-        gu_moves[j] = wire.near(gu.at[order[j]], gu_in.at[at.me], order[j])
     qkv_moves = [wire.near(qkv.at[p], qkv_in.at[at.me], p) for p in at.plane_peers()]
-    lay = [
-        wire.send(done.at[:, p], dz.at[pl.ds(at.z * spp, spp)], {"seq": p}) for p in at.line_peers()
-    ]
-
-    def arrive(j):
-        if j == 0:
-            own_gu.wait()
-        else:
-            gu_moves[j].wait_recv()
-        line.launch(n_out + 2 * j)
-        line.launch(n_out + 2 * j + 1)
+    row_moves = [wire.near(done.at[j], rows_out.at[at.me], order[j]) for j in range(1, n_done)]
+    fetch[0].wait()
+    fetch.append(wire.keep(held, rows_out.at[at.me]))
 
     def arrive_qkv():
         own_qkv.wait()
         for copy in qkv_moves:
             copy.wait_recv()
         group = nf // qkv_own.shape[0]
-        hd = HD
 
         def one(i):
             where = pl.ds(pl.multiple_of(i * 16, 16), 16)
             for c in range(qkv_own.shape[0]):
-                both = jnp.zeros((16, 2 * hd), F32)
+                both = jnp.zeros((16, 2 * HD), F32)
                 for g in range(group):
                     piece = qkv_in[c * group + g, where]
-                    qkv_own[c, where, g * hd : (g + 1) * hd] = piece[:, :hd]
-                    both = both + piece[:, hd:].astype(F32)
-                qkv_own[c, where, group * hd :] = both.astype(BF16)
+                    qkv_own[c, where, g * HD : (g + 1) * HD] = piece[:, :HD]
+                    both = both + piece[:, HD:].astype(F32)
+                qkv_own[c, where, group * HD :] = both.astype(BF16)
 
         each(qkv_own.shape[1] // 16, one)
         for c in range(qkv_own.shape[0]):
-            line.launch(n_out + 2 * nf + c)
-
-    def rest():
+            line.launch(n_out + rest + c)
+
+    def others():
         yield from main
         gl[...] = terms[...]
         work_on_sum(body, acc, other, rx, ry, (tokens, hid_grad, gain), (gl.at[pl.ds(0, 1)],), block)
-        line2, own_bz = [], []
-        for s in range(spp):
-            own_bz.append(wire.keep(block.at[s * ns + at.z], bz.at[at.z * spp + s]))
-            line2 += [
-                wire.send(block.at[s * ns + p], bz.at[at.z * spp + s], {"seq": p})
-                for p in at.line_peers()
-            ]
+        going = go_home(at, wire, block, bz, tok_out)
+        next(going)
         gp[at.me] = gl[...]
         small = [wire.near(gl, gp.at[at.me], p) for p in at.plane_peers()]
-        yield
-
-        def to_homes(src, out, arrived):
-            for copy in arrived:
-                copy.wait_recv()
-            home = wire.keep(src.at[at.me], out.at[at.me])
-            return home, [wire.near(src.at[p], out.at[at.me], p) for p in at.plane_peers()]
-
-        own_dz.wait()
-        home1, away1 = to_homes(dz, lay_out, lay)
         yield
         for copy in small:
             copy.wait_recv()
@@ -523,9 +567,7 @@
         gz[at.z] = total
         small2 = [wire.send(gt, gz.at[at.z], {"seq": p}) for p in at.line_peers()]
         yield
-        for copy in own_bz:
-            copy.wait()
-        home2, away2 = to_homes(bz, tok_out, line2)
+        next(going)
         yield
         for copy in small2:
             copy.wait_recv()
@@ -533,93 +575,368 @@
         for k in range(1, ns):
             total = total + gz[k]
         gain_out[...] = total
-        for copy in away1 + away2:
+        for _ in going:
+            pass
+        for copy in row_moves:
             copy.wait_recv()
-        home1.wait()
-        home2.wait()
-        yield
-
-    work = [lambda: arrive(0), lambda: arrive(1)]
+
+    def finished(j):
+        item = n_out + j
+
+        @pl.when(line.outer)
+        def _():
+            line.copy(2, item).wait_recv()
+
+        @pl.when(line.inner)
+        def _():
+            line.kept(item).wait()
+
+        row_moves.append(wire.near(up_sum.at[j], rows_out.at[at.me], order[n_done + j]))
+
     steps = line.steps()
-    slow = rest()
-    ready = {4: 2, 7: 3, 10: 4, 13: 5, 16: 6, 19: 7, 22: None}
-    for f in work:
-        f()
-    for i, step in enumerate(steps):
-        step()
-        if i in ready:
-            arrive_qkv() if ready[i] is None else arrive(ready[i])
+    slow = others()
+    for i in range(2 * (n_out + 1)):
+        steps.pop(0)()
         if i % 2 == 1:
+            next(slow, None)
+    arrive_qkv()
+    while len(steps) > 2 * qkv_own.shape[0] - 2:
+        steps.pop(0)()
+        if len(steps) % 2 == 1:
+            next(slow, None)
+    next(slow, None)
+    for j in range(rest):
+        finished(j)
+    while steps:
+        steps.pop(0)()
+        if len(steps) % 2 == 1:
             next(slow, None)
     for _ in slow:
         pass
-    line.end()
+    for k in range(len(items)):
+        line.end_one(k, n_out <= k < n_out + rest)
+    for copy in fetch[1:]:
+        copy.wait()
     wire.flush()
 
 
-def leave(nf, ns, body, part, tokens, hid_grad, gain, done, terms, gu, qkv, wout):
+def line_order(at):
+    return (at.me, at.mate, at.xn, at.yn, at.xn + at.step, at.yn + at.step, at.diag, at.diag + at.step)
+
+
+def leave(nf, ns, body, rest, part, tokens, hid_grad, gain, terms, done, todo, qkv, wout):
     rows, _, r, width = part.shape
     spp = nf // ns
-    depth = gu.shape[1]
+    depth = todo.shape[1]
     vmem, anys = pl.BlockSpec(memory_space=pltpu.VMEM), pl.BlockSpec(memory_space=pl.ANY)
     home = jax.ShapeDtypeStruct((nf, r, width), BF16)
-    n_send = 10 + (ns - 1) * (1 + spp) + (nf - 1) + (ns - 1) + 2 * (nf - 1) + 2 * (nf - 1)
+    n_send = 10 + (ns - 1) * spp + 2 * (nf - 1) + (ns - 1) + 2 * (nf - 1)
     heads = (KV, depth, (H // KV + 2) * HD)
-    n_items = wout.shape[0] + 2 * nf + KV
+    piece = todo.shape[1:]
+    n_items = wout.shape[0] + rest + KV
     return pl.pallas_call(
-        functools.partial(leave_kernel, nf, ns, body),
+        functools.partial(leave_kernel, nf, ns, body, rest),
         name="leave",
-        out_shape=[home, home, jax.ShapeDtypeStruct((8, width), F32)]
-        + [jax.ShapeDtypeStruct(s, BF16) for s in (gu.shape, heads, wout.shape)],
-        in_specs=[anys, vmem, vmem, vmem, anys, vmem, anys, anys, vmem],
-        out_specs=[anys, anys, vmem, anys, anys, anys],
+        out_shape=[home, jax.ShapeDtypeStruct((8, width), F32)]
+        + [jax.ShapeDtypeStruct(s, BF16) for s in (todo.shape, heads, wout.shape)],
+        in_specs=[anys, vmem, vmem, vmem, vmem, anys, anys, anys, vmem],
+        out_specs=[anys, vmem, anys, anys, anys],
         scratch_shapes=sum_scratch(rows, r, width)
-        + [pltpu.VMEM((nf, r, width), BF16)] * 2
+        + [pltpu.VMEM((nf, r, width), BF16)]
         + [pltpu.VMEM((8, width), F32)] * 2
         + [pltpu.VMEM((nf, 8, width), F32), pltpu.VMEM((ns, 8, width), F32)]
-        + [pltpu.VMEM(gu.shape, BF16)] * 3
+        + [pltpu.VMEM(piece, BF16)]
+        + [pltpu.VMEM((rest,) + piece, BF16)] * 4
         + [pltpu.VMEM(qkv.shape, BF16)]
         + [pltpu.VMEM(heads, BF16)] * 3
         + [pltpu.VMEM(wout.shape, BF16)] * 2
-        + [pltpu.SemaphoreType.DMA((5 + spp + 4,))]
+        + [pltpu.SemaphoreType.DMA((5 + 3 + rest + spp + 4,))]
         + [pltpu.SemaphoreType.DMA((n_send,))] * 2
         + LineSum.semaphores(n_items),
         compiler_params=pltpu.CompilerParams(collective_id=5, has_side_effects=True),
-    )(part, tokens, hid_grad, gain, done, terms, gu, qkv, wout)
-
-
-def split_columns(weight, nf, ff, ffp):
-    depth = weight.shape[0]
-    step = 16
-
-    def kernel(w, out):
-        for f in range(nf):
-            for g in range(2):
-                piece = w[:, (g * nf + f) * ff : (g * nf + f + 1) * ff]
-                if ffp > ff:
-                    piece = jnp.concatenate([piece, jnp.zeros((step, ffp - ff), piece.dtype)], axis=1)
-                out[f, :, g * ffp : (g + 1) * ffp] = piece
+    )(part, tokens, hid_grad, gain, terms, done, todo, qkv, wout)
+
+
+def whole(a):
+    zeros = (0,) * a.ndim
+    return pl.BlockSpec(a.shape, lambda i: zeros, pipeline_mode=pl.Buffered(1))
+
+
+def row_blocks(step, columns):
+    return pl.BlockSpec((step, columns), lambda i: (i, 0))
+
+
+def capped(q, k, last):
+    t = jnp.tanh(dot_nt(q, k) * (QUERY_FACTOR / SOFT_CAP))
+    e = jnp.exp(SOFT_CAP * t)
+    rows = lax.broadcasted_iota(jnp.int32, (last, last), 0)
+    columns = lax.broadcasted_iota(jnp.int32, (last, last), 1)
+    own = jnp.where(columns <= rows, e[:, e.shape[1] - last :], 0.0)
+    e = own if e.shape[1] == last else jnp.concatenate([e[:, : e.shape[1] - last], own], axis=1)
+    return t, e, 1.0 / jnp.sum(e, axis=1, keepdims=True)
+
+
+def attention(a_full, w_qkv, w_out, length):
+    tokens, width = a_full.shape
+    block = min(256, length)
+
+    def kernel(a, wq, wo, qkv, o, y):
+        qkv[...] = dot_f32(a[...], wq[...]).astype(BF16)
+        for b in range(length // block):
+            rows, keys = pl.ds(b * block, block), pl.ds(0, (b + 1) * block)
+            _, e, inv = capped(qkv[rows, :HD], qkv[keys, HD : 2 * HD], block)
+            out = dot_f32((e * inv).astype(BF16), qkv[keys, 2 * HD :]).astype(BF16)
+            o[rows] = out
+            y[rows] = dot_f32(out, wo[...]).astype(BF16)
 
     return pl.pallas_call(
         kernel,
-        name="split_columns",
-        grid=(depth // step,),
-        out_shape=jax.ShapeDtypeStruct((nf, depth, 2 * ffp), weight.dtype),
-        in_specs=[pl.BlockSpec((step, 2 * nf * ff), lambda i: (i, 0))],
-        out_specs=pl.BlockSpec((nf, step, 2 * ffp), lambda i: (0, i, 0)),
-    )(weight)
-
-
-def join_columns(parts, heads, nf, ff):
-    _, depth, columns = parts.shape
+        name="attention",
+        grid=(tokens // length,),
+        out_shape=[jax.ShapeDtypeStruct((tokens, c), BF16) for c in (3 * HD, HD, width)],
+        in_specs=[row_blocks(length, width), whole(w_qkv), whole(w_out)],
+        out_specs=[row_blocks(length, c) for c in (3 * HD, HD, width)],
+    )(a_full, w_qkv, w_out)
+
+
+def attention_back(nf, ns, dy1, qkv, o, a_full, w_qkv, w_out, length, done, todo, count, plan):
+    tokens, width = a_full.shape
+    block = min(256, length)
+    blocks = length // block
+    piece = todo.shape[1:]
+
+    def kernel(*refs):
+        dy, qk, ov, a, wq, wo, done, todo = refs[:8]
+        da, wq_grad, wo_grad, rows_out, summed = refs[8:13]
+        acc_q, acc_o, dk, dv, dqkv, held, own, in1, in2, lsem, ssem, rsem = refs[13:25]
+        i = pl.program_id(0)
+        at = Place(nf, ns)
+        order = line_order(at)
+        line = LineSum(at, [(own.at[k], in1.at[k], in2.at[k], summed.at[k]) for k in range(count)], refs[25:])
+        steps = line.steps()
+
+        def moves():
+            return [
+                pltpu.make_async_remote_copy(
+                    src_ref=done.at[order[j]], dst_ref=rows_out.at[at.me],
+                    send_sem=ssem.at[j - 1], recv_sem=rsem.at[j - 1],
+                    device_id={"fsdp": order[j]}, device_id_type=MESH,
+                )
+                for j in range(1, nf)
+            ]
+
+        def loads():
+            return [pltpu.make_async_copy(todo.at[order[k]], own.at[k], lsem.at[k]) for k in range(count)]
+
+        def held_in():
+            return pltpu.make_async_copy(done.at[at.me], held, lsem.at[count])
+
+        def held_out():
+            return pltpu.make_async_copy(held, rows_out.at[at.me], lsem.at[count + 1])
+
+        @pl.when(i == 0)
+        def _():
+            for copy in loads():
+                copy.start()
+            held_in().start()
+            at.greet(False, True, True)
+            for k, copy in enumerate(loads()):
+                copy.wait()
+                line.launch(k)
+            for copy in moves():
+                copy.start()
+            held_in().wait()
+            held_out().start()
+
+        out_term = jnp.zeros((HD, width), F32)
+        dk[...] = jnp.zeros_like(dk)
+        dv[...] = jnp.zeros_like(dv)
+        where = 0
+        for b in range(blocks):
+            rows, keys = pl.ds(b * block, block), pl.ds(0, (b + 1) * block)
+            q, k, v = qk[rows, :HD], qk[keys, HD : 2 * HD], qk[keys, 2 * HD :]
+            out = ov[rows]
+            do = dot_nt(dy[rows], wo[...]).astype(BF16)
+            t, e, inv = capped(q, k, block)
+            p = e * inv
+            dd = jnp.sum(do.astype(F32) * out.astype(F32), axis=1, keepdims=True)
+            ds = (p * (dot_nt(do, v) - dd) * (1.0 - t * t) * QUERY_FACTOR).astype(BF16)
+            dv[keys] += dot_tn(p.astype(BF16), do)
+            dk[keys] += dot_tn(ds, q)
+            dqkv[rows, :HD] = dot_f32(ds, k).astype(BF16)
+            out_term = out_term + dot_tn(out, dy[rows])
+            for turn in range(tokens // length):
+                n = plan[turn * blocks + b]
+                if n:
+
+                    @pl.when(i == turn)
+                    def _():
+                        lo = sum(plan[: turn * blocks + b])
+                        for step in steps[lo : lo + n]:
+                            step()
+
+        dqkv[:, HD : 2 * HD] = dk[...].astype(BF16)
+        dqkv[:, 2 * HD :] = dv[...].astype(BF16)
+        da[...] = dot_nt(dqkv[...], wq[...]).astype(BF16)
+        q_term = dot_tn(a[...], dqkv[...])
+
+        @pl.when(i == 0)
+        def _():
+            acc_q[...] = q_term
+            acc_o[...] = out_term
+
+        @pl.when(i > 0)
+        def _():
+            acc_q[...] += q_term
+            acc_o[...] += out_term
+
+        @pl.when(i == pl.num_programs(0) - 1)
+        def _():
+            wq_grad[...] = acc_q[...].astype(BF16)
+            wo_grad[...] = acc_o[...].astype(BF16)
+            for step in steps[sum(plan) :]:
+                step()
+            line.end()
+            held_out().wait()
+            for copy in moves():
+                copy.wait()
+
+    anys = pl.BlockSpec(memory_space=pl.ANY)
+    return pl.pallas_call(
+        kernel,
+        name="attention_back",
+        grid=(tokens // length,),
+        out_shape=[
+            jax.ShapeDtypeStruct(shape, BF16)
+            for shape in ((tokens, width), w_qkv.shape, w_out.shape, done.shape, (count,) + piece)
+        ],
+        in_specs=[row_blocks(length, c) for c in (width, 3 * HD, HD, width)]
+        + [whole(w_qkv), whole(w_out), anys, anys],
+        out_specs=[row_blocks(length, width), whole(w_qkv), whole(w_out), anys, anys],
+        scratch_shapes=[
+            pltpu.VMEM(w_qkv.shape, F32),
+            pltpu.VMEM(w_out.shape, F32),
+            pltpu.VMEM((length, HD), F32),
+            pltpu.VMEM((length, HD), F32),
+            pltpu.VMEM((length, 3 * HD), BF16),
+            pltpu.VMEM(piece, BF16),
+        ]
+        + [pltpu.VMEM((count,) + piece, BF16)] * 3
+        + [pltpu.SemaphoreType.DMA((count + 2,))]
+        + [pltpu.SemaphoreType.DMA((nf - 1,))] * 2
+        + LineSum.semaphores(count),
+        compiler_params=pltpu.CompilerParams(collective_id=6, has_side_effects=True),
+    )(dy1, qkv, o, a_full, w_qkv, w_out, done, todo)
+
+
+def ffn_forward(n_full, w_gu, w_down, step):
+    tokens, width = n_full.shape
+    ffp = w_down.shape[0]
+
+    def kernel(n, wg, wd, gu_out, m_out, y):
+        gu = dot_f32(n[...], wg[...])
+        gu_out[...] = gu.astype(BF16)
+        activated, _ = gelu_pair(gu[:, :ffp])
+        mixed = (activated * gu[:, ffp:]).astype(BF16)
+        m_out[...] = mixed
+        y[...] = dot_f32(mixed, wd[...]).astype(BF16)
+
+    return pl.pallas_call(
+        kernel,
+        name="ffn_forward",
+        grid=(tokens // step,),
+        out_shape=[jax.ShapeDtypeStruct((tokens, c), BF16) for c in (2 * ffp, ffp, width)],
+        in_specs=[row_blocks(step, width), whole(w_gu), whole(w_down)],
+        out_specs=[row_blocks(step, c) for c in (2 * ffp, ffp, width)],
+    )(n_full, w_gu, w_down)
+
+
+def ffn_backward(ns, nf, dy2, gu, n_full, w_gu, w_down, step, grad, plan):
+    tokens, width = n_full.shape
+    ffp = w_down.shape[0]
+    turns = tokens // step
+
+    def kernel(*refs):
+        dy, gu, n, wg, wd, grad = refs[:6]
+        dn, gate_grad, up_grad, summed, acc, in1, in2 = refs[6:13]
+        i = pl.program_id(0)
+        at = Place(nf, ns)
+        count = grad.shape[0]
+        line = LineSum(at, [(grad.at[k], in1.at[k], in2.at[k], summed.at[k]) for k in range(count)], refs[13:])
+        steps = line.steps()
+
+        @pl.when(i == 0)
+        def _():
+            at.greet(False, False, True)
+            for k in range(count):
+                line.launch(k)
+
+        def host(part):
+            for turn in range(turns):
+                at_plan = turn * 3 + part
+                lo, n = sum(plan[:at_plan]), plan[at_plan]
+                if n:
+
+                    @pl.when(i == turn)
+                    def _():
+                        for s in steps[lo : lo + n]:
+                            s()
+
+        dm = dot_nt(dy[...], wd[...])
+        activated, derivative = gelu_pair(gu[:, :ffp].astype(F32))
+        up = gu[:, ffp:].astype(F32)
+        dgu = jnp.concatenate(
+            [(dm * up * derivative).astype(BF16), (dm * activated).astype(BF16)], axis=1
+        )
+        host(0)
+        dn[...] = dot_nt(dgu, wg[...]).astype(BF16)
+        host(1)
+        term = dot_tn(n[...], dgu)
+
+        @pl.when(i == 0)
+        def _():
+            acc[...] = term
+
+        @pl.when(i > 0)
+        def _():
+            acc[...] += term
+
+        host(2)
+
+        @pl.when(i == turns - 1)
+        def _():
+            gate_grad[...] = acc[:, :ffp].astype(BF16)
+            up_grad[...] = acc[:, ffp:].astype(BF16)
+            for s in steps[sum(plan) :]:
+                s()
+            line.end()
+
+    half = jax.ShapeDtypeStruct((width, ffp), BF16)
+    return pl.pallas_call(
+        kernel,
+        name="ffn_backward",
+        grid=(turns,),
+        out_shape=[jax.ShapeDtypeStruct((tokens, width), BF16), half, half]
+        + [jax.ShapeDtypeStruct(grad.shape, BF16)],
+        in_specs=[row_blocks(step, c) for c in (width, 2 * ffp, width)]
+        + [whole(w_gu), whole(w_down), whole(grad)],
+        out_specs=[row_blocks(step, width), whole(half), whole(half), pl.BlockSpec(memory_space=pl.ANY)],
+        scratch_shapes=[pltpu.VMEM(w_gu.shape, F32)]
+        + [pltpu.VMEM(grad.shape, BF16)] * 2
+        + LineSum.semaphores(grad.shape[0]),
+        compiler_params=pltpu.CompilerParams(collective_id=7, has_side_effects=True),
+    )(dy2, gu, n_full, w_gu, w_down, grad)
+
+
+def join_columns(gate, up, heads, nf, ff):
+    _, depth, ffp = gate.shape
     n_kv, _, wide = heads.shape
     queries = wide - 2 * HD
     step = 16
 
-    def kernel(x, h, out, out_h):
-        for g in range(2):
-            lo = g * columns // 2
-            pieces = [x[f, :, lo : lo + ff].astype(F32) for f in range(nf)]
+    def kernel(x, y, h, out, out_h):
+        for g, ref in enumerate((x, y)):
+            pieces = [ref[f, :, :ff].astype(F32) for f in range(nf)]
             out[:, g * nf * ff : (g + 1) * nf * ff] = jnp.concatenate(pieces, axis=1)
         for c in range(n_kv):
             piece = h[c].astype(F32)
@@ -628,6 +945,7 @@
                 lo = n_kv * queries + (j * n_kv + c) * HD
                 out_h[:, lo : lo + HD] = piece[:, queries + j * HD : queries + (j + 1) * HD]
 
+    column_spec = pl.BlockSpec((nf, step, ffp), lambda i: (0, i, 0))
     return pl.pallas_call(
         kernel,
         name="join_columns",
@@ -636,15 +954,12 @@
             jax.ShapeDtypeStruct((depth, 2 * nf * ff), F32),
             jax.ShapeDtypeStruct((depth, n_kv * wide), F32),
         ],
-        in_specs=[
-            pl.BlockSpec((nf, step, columns), lambda i: (0, i, 0)),
-            pl.BlockSpec((n_kv, step, wide), lambda i: (0, i, 0)),
-        ],
+        in_specs=[column_spec] * 2 + [pl.BlockSpec((n_kv, step, wide), lambda i: (0, i, 0))],
         out_specs=[
             pl.BlockSpec((step, 2 * nf * ff), lambda i: (i, 0)),
             pl.BlockSpec((step, n_kv * wide), lambda i: (i, 0)),
         ],
-    )(parts, heads)
+    )(gate, up, heads)
 
 
 def with_sums(n):
@@ -691,34 +1006,6 @@
     values = tokens[i].astype(F32)
     part, term = norm_back(delta, values, inverse_rms(values), gain[...])
     return (hidden_grad[i] + part).astype(BF16), (term,)
-
-
-def scores(q, k):
-    s = jnp.einsum("bqd,bkd->bqk", q, k, preferred_element_type=F32) * QUERY_FACTOR
-    t = jnp.tanh(s / SOFT_CAP)
-    length = q.shape[1]
-    allowed = jnp.arange(length)[None, :] <= jnp.arange(length)[:, None]
-    return t, jnp.where(allowed[None], SOFT_CAP * t, MASKED)
-
-
-def attend(q, k, v):
-    _, c = scores(q, k)
-    top = jnp.max(c, axis=-1, keepdims=True)
-    lse = top + jnp.log(jnp.sum(jnp.exp(c - top), axis=-1, keepdims=True))
-    p = jnp.exp(c - lse).astype(BF16)
-    return jnp.einsum("bqk,bkd->bqd", p, v, preferred_element_type=F32).astype(BF16), lse
-
-
-def attend_back(q, k, v, o, do, lse):
-    t, c = scores(q, k)
-    p = jnp.exp(c - lse)
-    dd = jnp.sum(do.astype(F32) * o.astype(F32), axis=-1, keepdims=True)
-    dp = jnp.einsum("bqd,bkd->bqk", do, v, preferred_element_type=F32)
-    ds = (p * (dp - dd) * (1.0 - t * t) * QUERY_FACTOR).astype(BF16)
-    dv = jnp.einsum("bqk,bqd->bkd", p.astype(BF16), do, preferred_element_type=F32)
-    dk = jnp.einsum("bqk,bqd->bkd", ds, q, preferred_element_type=F32)
-    dq = jnp.einsum("bqk,bkd->bqd", ds, k, preferred_element_type=F32)
-    return dq.astype(BF16), dk.astype(BF16), dv.astype(BF16)
 
 
 def dot_f32(a, b):
@@ -752,67 +1039,57 @@
     ffp = -(-ff // LANES) * LANES
     depth = qkv_weight.shape[0]
 
-    q_cols = qkv_weight[:, : H * HD].reshape(depth, H, HD)
-    k_cols = jnp.repeat(qkv_weight[:, H * HD : (H + KV) * HD].reshape(depth, KV, HD), group, axis=1)
-    v_cols = jnp.repeat(qkv_weight[:, (H + KV) * HD :].reshape(depth, KV, HD), group, axis=1)
-    w_qkv = jnp.concatenate([q_cols, k_cols, v_cols], axis=2).transpose(1, 0, 2)
-    w_qkv = swap(w_qkv, "fsdp").reshape(nf * depth, 3 * HD)
-    w_gu = swap(split_columns(gate_up_weight, nf, ff, ffp), "fsdp")
-    w_gu = w_gu.reshape(nf * depth, 2 * ffp)
-    w_down = jnp.pad(down_weight, ((0, ffp - ff), (0, 0)))
-
     gains = [g.reshape(1, width) for g in (pre_attn_gain, post_attn_gain, pre_ffn_gain, post_ffn_gain)]
     flat = (rows * nf * r, width)
     shape = (rows, nf, r, width)
-
-    a_full, x_own, g_own = enter(
-        nf, ns, tokens.reshape(nf, r, width), out_grad.reshape(nf, r, width), gains[0]
-    )
+    tokens_of = min(512, flat[0])
+
+    a_full, x_own, g_own, w_qkv, w_gu = enter(
+        nf, ns, tokens.reshape(nf, r, width), out_grad.reshape(nf, r, width), gains[0],
+        qkv_weight, gate_up_weight, ffp,
+    )
+    a_full = a_full.reshape(flat)
     x_own, g_own = x_own.reshape(rows, r, width), g_own.reshape(rows, r, width)
-    a_full = a_full.reshape(flat)
-    qkv = dot_f32(a_full, w_qkv).astype(BF16)
-    q, k, v = (qkv[:, i * HD : (i + 1) * HD].reshape(spp, length, HD) for i in range(3))
-    o, lse = attend(q, k, v)
-    o_flat = o.reshape(-1, HD)
-    y1_terms = dot_f32(o_flat, out_weight).astype(BF16).reshape(shape)
+    w_qkv = w_qkv.reshape(nf * depth, 3 * HD)
+    w_gu = swap(w_gu, "fsdp").reshape(nf * depth, 2 * ffp)
+    w_down = jnp.pad(down_weight, ((0, ffp - ff), (0, 0)))
+
+    qkv, o, y1_terms = attention(a_full, w_qkv, out_weight, length)
     n_full, y1, hidden = middle(
-        "mid", 2, nf, ns, body_mid, y1_terms, [x_own, gains[1], gains[2]], [F32, F32]
+        "mid", 2, nf, ns, body_mid, y1_terms.reshape(shape), [x_own, gains[1], gains[2]], [F32, F32]
     )
     n_full = n_full.reshape(flat)
-    gu = dot_f32(n_full, w_gu)
-    gate, up = gu[:, :ffp], gu[:, ffp:]
-    activated, derivative = gelu_pair(gate)
-    mixed = (activated * up).astype(BF16)
-    y2_terms = dot_f32(mixed, w_down).astype(BF16).reshape(shape)
-    dy2_full, out_own, post_ffn_term = middle(
-        "turn", 3, nf, ns, body_turn, y2_terms, [hidden, g_own, gains[3]], [BF16]
+    gu, mixed, y2_terms = ffn_forward(n_full, w_gu, w_down, tokens_of)
+    dy2_full, layer_out, post_ffn_term = middle(
+        "turn", 3, nf, ns, body_turn, y2_terms.reshape(shape), [hidden, g_own, gains[3]], [BF16],
+        homing=True,
     )
     dy2_full = dy2_full.reshape(flat)
-    down_wg = dot_tn(mixed, dy2_full)[:ff].astype(BF16)
-    dm = dot_nt(dy2_full, w_down)
-    dgu = jnp.concatenate([dm * up * derivative, dm * activated], axis=1).astype(BF16)
-    dn_terms = dot_nt(dgu, w_gu).astype(BF16).reshape(shape)
-    gu_wg = dot_tn(n_full, dgu).astype(BF16).reshape(nf, depth, 2 * ffp)
     pieces = next(n for n in (9, 6, 3, 2, 1) if ff % (16 * n) == 0)
-    dy1_full, hidden_grad, pre_ffn_term, post_attn_term, down_wg = middle(
-        "back", 4, nf, ns, body_back, dn_terms, [hidden, y1, g_own, gains[1], gains[2]], [F32],
-        down_wg.reshape(pieces, ff // pieces, width), (0, 0, 1, 2, 4, 4, 2, 2, 2),
-    )
-    dy1_full = dy1_full.reshape(flat)
-    do = dot_nt(dy1_full, out_weight).astype(BF16).reshape(o.shape)
-    out_wg = dot_tn(o_flat, dy1_full).astype(BF16)
-    dq, dk, dv = attend_back(q, k, v, o, do, lse)
-    dqkv = jnp.concatenate([dq, dk, dv], axis=2).reshape(-1, 3 * HD)
-    da_terms = dot_nt(dqkv, w_qkv).astype(BF16).reshape(shape)
-    qkv_wg = dot_tn(a_full, dqkv).astype(BF16).reshape(nf, depth, 3 * HD)
+    down_wg = dot_tn(mixed, dy2_full)[:ff].astype(BF16).reshape(pieces, ff // pieces, width)
+    dn_terms, gate_wg, up_wg, down_wg = ffn_backward(
+        ns, nf, dy2_full, gu, n_full, w_gu, w_down, tokens_of, down_wg,
+        (0, 0, 1, 0, 2, 2, 0, 2, 2, 0, 2, 0),
+    )
+    gate_wg, up_wg = gate_wg.reshape(nf, depth, ffp), up_wg.reshape(nf, depth, ffp)
+    dy1_full, hidden_grad, pre_ffn_term, post_attn_term, gate_wg = middle(
+        "back", 4, nf, ns, body_back, dn_terms.reshape(shape),
+        [hidden, y1, g_own, gains[1], gains[2]], [F32],
+        grad=gate_wg, plan=(0, 0, 1, 2, 4, 4, 2, 2, 2),
+    )
+    count = 5
+    da_terms, qkv_wg, out_wg, gate_wg, up_sums = attention_back(
+        nf, ns, dy1_full.reshape(flat), qkv, o, a_full, w_qkv, out_weight, length,
+        gate_wg, up_wg, count, (0, 0, 1, 2, 0, 2, 2, 3),
+    )
     terms = jnp.concatenate(
         [jnp.zeros((1, width), F32), post_attn_term, pre_ffn_term, post_ffn_term, jnp.zeros((4, width), F32)]
     )
-    layer_out, tokens_grad, gain_sums, gu_wg, qkv_wg, out_wg = leave(
-        nf, ns, body_last, da_terms, x_own, hidden_grad, gains[0],
-        out_own.reshape(spp, ns, r, width), terms, gu_wg, qkv_wg, out_wg.reshape(2, HD // 2, width),
-    )
-    gu_wg, qkv_wg = join_columns(gu_wg, qkv_wg, nf, ff)
+    tokens_grad, gain_sums, up_wg, qkv_wg, out_wg = leave(
+        nf, ns, body_last, nf - count, da_terms.reshape(shape), x_own, hidden_grad, gains[0], terms,
+        up_sums, up_wg, qkv_wg.reshape(nf, depth, 3 * HD), out_wg.reshape(2, HD // 2, width),
+    )
+    gu_wg, qkv_wg = join_columns(gate_wg, up_wg, qkv_wg, nf, ff)
     return (
         layer_out.reshape(1, chunk, width),
         tokens_grad.astype(F32).reshape(1, chunk, width),

time: 656 us -> 599 us (0.913)
  matrix products: 121 us -> 8.44 us
  Pallas kernels: 479 us -> 561 us
  local copies, waits for them, and re-layouts: 20.7 us -> 8.84 us
  other arithmetic: 14.6 us -> 6.8 us
    dot_general x14 -> x0, matrix products: 84.1 us -> none  [the longest x4 35.5 us: dot_nt(): lax.dot_general(a, b, (((1,), (1,)), ((), ())), preferred_element_type=F32)]
    pallas_call x3 -> x6, Pallas kernels: 273 us -> 352 us  [the longest x1 125 us: leave(): pl.pallas_call(functools.partial(leave_kernel, nf, ns, body, rest), name=...]
    dot_general x4 -> x1, matrix products: 36.5 us -> 8.44 us  [dot_tn(): lax.dot_general(a, b, (((0,), (0,)), ((), ())), preferred_element_type=F32)]
  transfers between devices with their start and end apart: 2 -> 1, of which waited for: 0 -> 0; matrix products, arithmetic and copies ran while one was open for 3% -> 1% of each run, Pallas kernels for 21% -> 15%
where the time goes in v3:
time: 599 us; the launch traced here: 591 us
  Pallas kernels  561 us (94%)
  local copies, waits for them, and re-layouts  8.84 us (1%)
  matrix products  8.44 us (1%)
  other arithmetic  6.8 us (1%)
    pallas_call x3, Pallas kernels, middle(): pl.pallas_call(functools.partial(middle_kernel, nf, ns, len(ins), n_own,...  200 us
    pallas_call x1, Pallas kernels, leave(): pl.pallas_call(functools.partial(leave_kernel, nf, ns, body, rest), name=...  125 us
    pallas_call x1, Pallas kernels, ffn_backward(): pl.pallas_call(kernel, name='ffn_backward', grid=(turns,), out_shape=[jax...  72.5 us
    pallas_call x1, Pallas kernels, enter(): pl.pallas_call(functools.partial(enter_kernel, nf, ns, wgu.shape[1] // (2...  61.7 us
    pallas_call x1, Pallas kernels, attention_back(): pl.pallas_call(kernel, name='attention_back', grid=(tokens // length,), o...  55.6 us
    pallas_call x1, Pallas kernels, ffn_forward(): pl.pallas_call(kernel, name='ffn_forward', grid=(tokens // step,), out_sh...  21.1 us
    pallas_call x1, Pallas kernels, attention(): pl.pallas_call(kernel, name='attention', grid=(tokens // length,), out_sh...  15.9 us
  transfers between devices with their start and end apart: 1, of which 0 were waited for; matrix products, arithmetic and copies ran while one was open for 1% of the time, Pallas kernels for 15%

profile of v3, /device:TPU:0, one launch (start us, length us, event | category | flops | bytes accessed | tf_op | source)
XLA Modules:
  0.0 591.2 jit_solution(11311830111383229333)
XLA Ops:
  0.6 1.3 reshape.106.refs_2_.refs_3_
  1.9 61.7 %enter.1 = (bf16[8,8,32,1152]{3,2,1,0:T(8,128)(2,1)}, bf16[2,4,32,1152]{3,2,1,0:T(8,128)(2,1)}, bf16[2,4,32,1152]{3,2,1,0:T(8,128)(2,1)}, bf16[8,144,768]{2,1,0:T(8,128)(2,1)}, bf16[8,144,1792]{2,1,0:T(8,128)(2,1)}) custom-call(bf16[8,32,1152]{2,1,0:T(8,128)(2,1)} %bitcast.57, bf16[8,32,1152]{2,1,0:T(8,128)(2,1)} %bitcast.58, ...), custom_call_target="tpu_custom_call" | custom-call | tf_op jit(solution)/shard_map/enter/pallas_call | solution.py:368
  63.7 0.0 copy-start.4
  63.7 0.0 copy-start.5
  63.7 0.0 copy-start.6
  63.7 0.0 copy-start
  63.7 4.7 all-to-all-start
  68.4 0.0 copy-done.4
  68.4 0.6 reshape.111.refs_2_.refs_4_
  69.0 0.6 reshape.112.refs_3_.refs_5_
  69.6 0.0 copy-done.6
  69.6 0.6 reshape.117.refs_3_
  70.2 1.5 pad.4.wd.refs_4_
  71.7 15.9 %attention.1 = (bf16[2048,768]{1,0:T(8,128)(2,1)}, bf16[2048,256]{1,0:T(8,128)(2,1)}, bf16[2048,1152]{1,0:T(8,128)(2,1)}) custom-call(bf16[2048,1152]{1,0:T(8,128)(2,1)} %bitcast.32, bf16[1152,768]{1,0:T(8,128)(2,1)} %bitcast.39, bf16[256,1152]{1,0:T(8,128)(2,1)} %refs_5_.1), custom_call_target="tpu_custom_call" | custom-call | tf_op jit(solution)/shard_map/attention/pallas_call | solution.py:692
  87.6 73.8 %mid.1 = (bf16[8,8,32,1152]{3,2,1,0:T(8,128)(2,1)}, f32[8,32,1152]{2,1,0:T(8,128)}, f32[8,32,1152]{2,1,0:T(8,128)}) custom-call(bf16[8,8,32,1152]{3,2,1,0:T(8,128)(2,1)} %bitcast.47, bf16[8,32,1152]{2,1,0:T(8,128)(2,1)} %bitcast.48, f32[1,1152]{1,0:T(1,128)} %reshape.111.refs_2_.refs_4_, f32[1,1152]{1,0:T(1,128)} %reshape.112.refs_3_.refs_5_), custom_call_target="tpu_custom_call" | custom-call | tf_op jit(solution)/shard_map/mid/pallas_call | solution.py:487
  161.4 0.0 all-to-all-done
  161.4 21.1 %ffn_forward.1 = (bf16[2048,1792]{1,0:T(8,128)(2,1)}, bf16[2048,896]{1,0:T(8,128)(2,1)}, bf16[2048,1152]{1,0:T(8,128)(2,1)}) custom-call(bf16[2048,1152]{1,0:T(8,128)(2,1)} %bitcast.34, bf16[1152,1792]{1,0:T(8,128)(2,1)} %bitcast.7.wg.refs_3_, bf16[896,1152]{1,0:T(8,128)(2,1)} %pad.4.wd.refs_4_), custom_call_target="tpu_custom_call" | custom-call | tf_op jit(solution)/shard_map/ffn_forward/pallas_call | solution.py:844
  182.5 60.5 %turn.1 = (bf16[8,8,32,1152]{3,2,1,0:T(8,128)(2,1)}, bf16[8,32,1152]{2,1,0:T(8,128)(2,1)}, f32[1,1152]{1,0:T(1,128)}) custom-call(bf16[8,8,32,1152]{3,2,1,0:T(8,128)(2,1)} %bitcast.46, f32[8,32,1152]{2,1,0:T(8,128)} %get-tuple-element.55.refs_1_, bf16[8,32,1152]{2,1,0:T(8,128)(2,1)} %bitcast.50, f32[1,1152]{1,0:T(1,128)} %reshape.117.refs_3_), custom_call_target="tpu_custom_call" | custom-call | tf_op jit(solution)/shard_map/turn/pallas_call | solution.py:487
  243.0 8.4 %fusion = bf16[896,1152]{1,0:T(8,128)(2,1)S(1)} fusion(bf16[2048,896]{1,0:T(8,128)(2,1)} %get-tuple-element.60, bf16[2048,1152]{1,0:T(8,128)(2,1)} %bitcast.42), kind=kOutput, calls=%fused_computation.8 | convolution fusion | flops 4227858432 | bytes 10452992 | tf_op jit(solution)/shard_map/dot_general | solution.py:1020
  251.5 1.4 slice.27
  252.9 72.5 %ffn_backward.1 = (bf16[2048,1152]{1,0:T(8,128)(2,1)}, bf16[1152,896]{1,0:T(8,128)(2,1)}, bf16[1152,896]{1,0:T(8,128)(2,1)}, bf16[9,96,1152]{2,1,0:T(8,128)(2,1)}) custom-call(bf16[2048,1152]{1,0:T(8,128)(2,1)} %bitcast.43, bf16[2048,1792]{1,0:T(8,128)(2,1)} %get-tuple-element.59.refs_1_, bf16[2048,1152]{1,0:T(8,128)(2,1)} %bitcast.35, ...), custom_call_target="tpu_custom_call" | custom-call | tf_op jit(solution)/shard_map/ffn_backward/pallas_call | solution.py:915
  325.5 65.8 %back.1 = (bf16[8,8,32,1152]{3,2,1,0:T(8,128)(2,1)}, f32[8,32,1152]{2,1,0:T(8,128)}, f32[1,1152]{1,0:T(1,128)}, f32[1,1152]{1,0:T(1,128)}, bf16[8,144,896]{2,1,0:T(8,128)(2,1)}) custom-call(bf16[8,8,32,1152]{3,2,1,0:T(8,128)(2,1)} %bitcast.45, f32[8,32,1152]{2,1,0:T(8,128)} %get-tuple-element.55.refs_1_, f32[8,32,1152]{2,1,0:T(8,128)} %get-tuple-element.62.refs_2_, ...), custom_call_target="tpu_custom_call" | custom-call | tf_op jit(solution)/shard_map/back/pallas_call | solution.py:487
  391.3 1.4 concatenate.3.refs_4_
  392.7 55.6 %attention_back.1 = (bf16[2048,1152]{1,0:T(8,128)(2,1)}, bf16[1152,768]{1,0:T(8,128)(2,1)}, bf16[256,1152]{1,0:T(8,128)(2,1)}, bf16[8,144,896]{2,1,0:T(8,128)(2,1)}, bf16[5,144,896]{2,1,0:T(8,128)(2,1)}) custom-call(bf16[2048,1152]{1,0:T(8,128)(2,1)} %bitcast.41, bf16[2048,768]{1,0:T(8,128)(2,1)} %get-tuple-element.65.refs_1_, ...), custom_call_target="tpu_custom_call" | custom-call | tf_op jit(solution)/shard_map/attention_back/pallas_call | solution.py:805
  448.3 124.7 %leave.1 = (bf16[8,32,1152]{2,1,0:T(8,128)(2,1)}, f32[8,1152]{1,0:T(8,128)}, bf16[8,144,896]{2,1,0:T(8,128)(2,1)}, bf16[4,144,1024]{2,1,0:T(8,128)(2,1)}, bf16[2,128,1152]{2,1,0:T(8,128)(2,1)}) custom-call(bf16[8,8,32,1152]{3,2,1,0:T(8,128)(2,1)} %bitcast.44, bf16[8,32,1152]{2,1,0:T(8,128)(2,1)} %bitcast.49, f32[8,32,1152]{2,1,0:T(8,128)} %get-tuple-element.70.refs_2_, ...), custom_call_target="tpu_custom_call" | custom-call | tf_op jit(solution)/shard_map/leave/pallas_call | solution.py:637
  573.0 2.3 bitcast_convert_fusion.1
  575.3 2.2 bitcast_convert_fusion.2
  577.5 0.6 slice_reduce_fusion
  578.1 2.3 bitcast_convert_fusion
  580.5 9.4 %join_columns.1 = (f32[144,13824]{1,0:T(8,128)}, f32[144,4096]{1,0:T(8,128)}) custom-call(bf16[8,144,896]{2,1,0:T(8,128)(2,1)} %get-tuple-element.79.x, bf16[8,144,896]{2,1,0:T(8,128)(2,1)} %get-tuple-element.80.y, bf16[4,144,1024]{2,1,0:T(8,128)(2,1)} %get-tuple-element.81.h), custom_call_target="tpu_custom_call" | custom-call | tf_op jit(solution)/shard_map/join_columns/pallas_call | solution.py:949
  589.9 0.0 copy-done.2
  589.9 0.8 copy.21
  (11 shorter events, 0.0 us)
Async XLA Ops:
  63.7 4.7 copy-start.4
  63.7 5.3 copy-start.5
  63.7 5.9 %copy-start.6 = (f32[1152]{0:T(1024)S(1)}, f32[1152]{0:T(1024)}, u32[]{:S(2)}) copy-start(f32[1152]{0:T(1024)} %param.18) | copy-start | bytes 13828
  63.7 6.5 %copy-start = (bf16[864,1152]{1,0:T(8,128)(2,1)S(1)}, bf16[864,1152]{1,0:T(8,128)(2,1)}, u32[]{:S(2)}) copy-start(bf16[864,1152]{1,0:T(8,128)(2,1)} %param.17) | copy-start | bytes 5971972
  63.7 97.7 %all-to-all-start = ((bf16[8,144,1792]{2,1,0:T(8,128)(2,1)}), bf16[8,144,1792]{2,1,0:T(8,128)(2,1)}, u32[]{:S(2)}, u32[]{:S(2)}) async-start(bf16[8,144,1792]{2,1,0:T(8,128)(2,1)} %get-tuple-element.53), calls=%async_computation | async-start | bytes 8257536 | tf_op jit(solution)/shard_map/all_to_all | solution.py:1024
  325.4 65.9 %copy-start.7 = (f32[1,1152]{1,0:T(1,128)S(1)}, f32[1,1152]{1,0:T(1,128)}, u32[]{:S(2)}) copy-start(f32[1,1152]{1,0:T(1,128)} %get-tuple-element.73) | copy-start | bytes 13828
  573.0 4.5 copy-start.3
  573.0 5.1 copy-start.1
  580.5 9.4 %copy-start.2 = (bf16[8,32,1152]{2,1,0:T(8,128)(2,1)S(1)}, bf16[8,32,1152]{2,1,0:T(8,128)(2,1)}, u32[]{:S(2)}) copy-start(bf16[8,32,1152]{2,1,0:T(8,128)(2,1)} %get-tuple-element.57) | copy-start | bytes 1769476
